TPU v7x, 16 devices: a whole 2x2x2 slice. The times are simulated.
16 devices in a mesh: dp: 2 (over z), sp: 8 (over y, x, core).
Axes of the slice: x: 2, y: 2, z: 2, core: 2. Of those that a mesh axis runs over, the one named last changes fastest.
Arguments:
- x: bfloat16 [8192, 3072], P(('dp', 'sp')), parts along dimension 0
- grad_out: bfloat16 [8192, 3072], P(('dp', 'sp')), parts along dimension 0
- positions: int32 [8192], P(('dp', 'sp')), parts along dimension 0
- gain: bfloat16 [3072], replicated
- w_q: bfloat16 [3072, 3072], replicated
- w_k: bfloat16 [3072, 1024], replicated
- w_v: bfloat16 [3072, 1024], replicated
- w_o: bfloat16 [3072, 3072], replicated
Outputs:
- output 1: bfloat16 [8192, 3072], P(('dp', 'sp')), parts along dimension 0
- output 2: bfloat16 [8192, 3072], P(('dp', 'sp')), parts along dimension 0
- output 3: float32 [6144, 3072], P('dp'), parts along dimension 0
- output 4: float32 [6144, 1024], P('dp'), parts along dimension 0
- output 5: float32 [6144, 1024], P('dp'), parts along dimension 0
- output 6: float32 [6144, 3072], P('dp'), parts along dimension 0
- output 7: float32 [6144], P('dp'), parts along dimension 0
There are 2 independent parts. A program takes and returns all parts, laid end to end along the dimension named above; an argument that names none is the same for every part.
All inputs are finite; a program needn't handle non-finite values.
Results may differ from a plain program's by a relative error of at most 0.0182909.
Values are sent between devices in bfloat16 or wider.
A program may use at most 1 GiB of HBM per device.

v0:
```python
import functools

import jax
import jax.numpy as jnp
from jax import lax
from jax.experimental import pallas as pl
from jax.experimental.pallas import tpu as pltpu
from jax.sharding import PartitionSpec as P

HEAD_DIM = 128
HALF = HEAD_DIM // 2
ROPE_THETA = 1000000.0
NORM_EPS = 1e-05
NEG_LARGE = -1e30
LOG2E = 1.4426950408889634
BLK = 512
CHUNKS = 4
FWD_MIDDLE, BWD_MIDDLE, BWD_LATE = 5, 4, 5
MROWS = 1024
RING = 3
ROWS = 64
F32 = jnp.float32
BF16 = jnp.bfloat16
ROWS_ROWS = (((0,), (0,)), ((), ()))
COLS_COLS = (((1,), (1,)), ((), ()))
ROWS_COLS = (((0,), (1,)), ((), ()))
VMEM_LIMIT = 60 * 1024 * 1024


def dot(a, b, dims=(((1,), (0,)), ((), ()))):
    return lax.dot_general(a, b, dims, preferred_element_type=F32)


def params(axes=1):
    return pltpu.CompilerParams(dimension_semantics=("arbitrary",) * axes, vmem_limit_bytes=VMEM_LIMIT)


class Neighbours:
    def __init__(self):
        self.me = lax.axis_index('sp')
        core, col, row = lax.rem(self.me, 2), lax.rem(self.me // 2, 2), self.me // 4
        self.sib = self.me + 1 - 2 * core
        self.xn = self.me + 2 - 4 * col
        self.yn = self.me + 4 - 8 * row
        self.diag = self.xn + self.yn - self.me

    def meet(self, peers):
        barrier = pltpu.get_barrier_semaphore()
        for peer in peers:
            pl.semaphore_signal(barrier, inc=1, device_id={'sp': peer}, device_id_type=pl.DeviceIdType.MESH)
        pl.semaphore_wait(barrier, len(peers))

    def others(self):
        flip = lambda dev: dev + 1 - 2 * lax.rem(dev, 2)
        return [self.sib, self.xn, flip(self.xn), self.yn, flip(self.yn), self.diag, flip(self.diag)]


def send(src, dst, sems, index, peer):
    return pltpu.make_async_remote_copy(src_ref=src, dst_ref=dst, send_sem=sems.at[0, index], recv_sem=sems.at[1, index],
                                        device_id={'sp': peer}, device_id_type=pl.DeviceIdType.MESH)


class Gather:
    COPIES = 22

    def __init__(self, near, own, dst, rows, sems):
        self.near, self.own, self.dst, self.rows, self.sems = near, own, dst, rows, sems

    def block(self, dev, chunk, count=1):
        size = self.rows // CHUNKS
        return self.dst.at[pl.ds(pl.multiple_of(dev * self.rows + chunk * size, size), count * size), :]

    def first(self, chunk, kind):
        peer = (self.near.xn, self.near.yn, self.near.sib)[kind]
        return send(self.own(chunk), self.block(self.near.me, chunk), self.sems, kind * CHUNKS + chunk, peer)

    def onward(self, chunk):
        over_y = chunk < CHUNKS // 2
        rows = self.block(self.near.xn if over_y else self.near.yn, chunk)
        return send(rows, rows, self.sems, 12 + chunk, self.near.yn if over_y else self.near.xn)

    def share(self, kind):
        rows = self.block((self.near.xn, self.near.yn)[kind], 0, CHUNKS)
        return send(rows, rows, self.sems, 16 + kind, self.near.sib)

    def share_diag(self, chunk):
        rows = self.block(self.near.diag, chunk)
        return send(rows, rows, self.sems, 18 + chunk, self.near.sib)

    def begin(self):
        self.near.meet([self.near.sib, self.near.xn, self.near.yn])
        for chunk in range(CHUNKS):
            self.start(chunk)

    def start(self, chunk):
        for kind in range(3):
            self.first(chunk, kind).start()

    def middle(self):
        for chunk in (0, 1):
            self.first(chunk, 0).wait_recv()
            self.onward(chunk).start()
        self.first(2, 1).wait_recv()
        self.onward(2).start()

    def late(self):
        self.first(3, 1).wait_recv()
        self.onward(3).start()
        for chunk in (2, 3):
            self.first(chunk, 0).wait_recv()
        self.share(0).start()
        for chunk in (0, 1):
            self.first(chunk, 1).wait_recv()
        self.share(1).start()

    def end(self):
        for chunk in (0, 2, 1, 3):
            self.onward(chunk).wait_recv()
            self.share_diag(chunk).start()
        sent = [self.first(chunk, kind) for chunk in range(CHUNKS) for kind in range(3)]
        for copy in sent:
            copy.wait_send()
        for chunk in range(CHUNKS):
            self.first(chunk, 2).wait_recv()
            self.onward(chunk).wait_send()
        for copy in [self.share(0), self.share(1)] + [self.share_diag(chunk) for chunk in range(CHUNKS)]:
            copy.wait()


SEMS = pltpu.SemaphoreType.DMA((2, Gather.COPIES))


def comm_params(collective_id):
    return pltpu.CompilerParams(dimension_semantics=("arbitrary",), vmem_limit_bytes=VMEM_LIMIT, collective_id=collective_id,
                                has_side_effects=True)


def gather_h_kernel(x_ref, gain_ref, pos_ref, freq_ref, h_all, cos_ref, sin_ref, x_v, h_v, pos_all, in_sems, out_sem, pos_sems, sems):
    near = Neighbours()
    rows = x_ref.shape[0]
    size = rows // CHUNKS
    part = lambda ref, chunk: ref.at[pl.ds(chunk * size, size), :]
    gather = Gather(near, lambda chunk: part(h_v, chunk), h_all, rows, sems)
    loads = [pltpu.make_async_copy(part(x_ref, chunk), part(x_v, chunk), in_sems.at[chunk]) for chunk in range(CHUNKS)]
    for load in loads:
        load.start()
    others = near.others()
    near.meet(others)
    pos_all[near.me] = pos_ref[...]
    positions = [send(pos_ref, pos_all.at[near.me], pos_sems, r, peer) for r, peer in enumerate(others)]
    for copy in positions:
        copy.start()
    for chunk in range(CHUNKS):
        loads[chunk].wait()

        @pl.loop(0, size // 32)
        def _(r):
            at = pl.ds(pl.multiple_of(chunk * size + r * 32, 32), 32)
            x_f = x_v[at, :].astype(F32)
            normed = x_f * lax.rsqrt(jnp.mean(x_f * x_f, axis=-1, keepdims=True) + NORM_EPS)
            h_v[at, :] = (normed * gain_ref[...]).astype(BF16)

        gather.start(chunk)
    own = pltpu.make_async_copy(h_v, gather.block(near.me, 0, CHUNKS), out_sem)
    own.start()
    for copy in positions:
        copy.wait()
    sign = jnp.where(lax.broadcasted_iota(jnp.int32, (1, HEAD_DIM), 1) < HALF, -1.0, 1.0)

    @pl.loop(0, pos_all.shape[0])
    def _(b):
        at = pl.ds(pl.multiple_of(b * rows, rows), rows)
        pos = jnp.broadcast_to(pos_all[b, 0:1, :].astype(F32), (HEAD_DIM, rows)).T
        angles = pos * freq_ref[...]
        cos_ref[at, :] = jnp.cos(angles)
        sin_ref[at, :] = jnp.sin(angles) * sign

    gather.middle()
    gather.late()
    own.wait()
    gather.end()


def gather_h(x, gain_f, positions, sp_size):
    rows, width = x.shape
    any_spec = pl.BlockSpec(memory_space=pl.ANY)
    vmem = pl.BlockSpec(memory_space=pltpu.VMEM)
    inv_freq = ROPE_THETA ** (-jnp.arange(0, HEAD_DIM, 2).astype(F32) / HEAD_DIM)
    freq = jnp.concatenate([inv_freq, inv_freq])[None, :]
    table = jax.ShapeDtypeStruct((rows * sp_size, HEAD_DIM), F32)
    return pl.pallas_call(
        gather_h_kernel,
        in_specs=[any_spec, vmem, vmem, vmem],
        out_specs=[any_spec, vmem, vmem],
        out_shape=[jax.ShapeDtypeStruct((rows * sp_size, width), BF16), table, table],
        scratch_shapes=[pltpu.VMEM((rows, width), BF16), pltpu.VMEM((rows, width), BF16), pltpu.VMEM((sp_size, 8, rows), jnp.int32),
                        pltpu.SemaphoreType.DMA((CHUNKS,)), pltpu.SemaphoreType.DMA, pltpu.SemaphoreType.DMA((2, 7)), SEMS],
        compiler_params=pltpu.CompilerParams(vmem_limit_bytes=VMEM_LIMIT, collective_id=0, has_side_effects=True),
        name="gather_h",
    )(x, gain_f, jnp.broadcast_to(positions[None, :], (8, rows)), freq)


def masked(scores):
    key = lax.broadcasted_iota(jnp.int32, scores.shape, 0)
    query = lax.broadcasted_iota(jnp.int32, scores.shape, 1)
    return jnp.where(key <= query, scores, NEG_LARGE)


def forward_kernel(heads, h_ref, wq_ref, wk_ref, wv_ref, cos_ref, sin_ref, dy_ref, q_ref, k_ref, v_ref, ht_ref, o_ref, lse_ref, dy_all,
                   w_v, w_sems, k_s, vt, acc, stage, stage_sems, sems):
    i = pl.program_id(0)
    near = Neighbours()
    rows = dy_ref.shape[0]
    size = rows // CHUNKS
    gather = Gather(near, lambda chunk: dy_ref.at[pl.ds(chunk * size, size), :], dy_all, rows, sems)
    stage_in = pltpu.make_async_copy(dy_ref, stage, stage_sems.at[0])
    stage_out = pltpu.make_async_copy(stage, gather.block(near.me, 0, CHUNKS), stage_sems.at[1])
    to_log2 = HEAD_DIM ** -0.5 * LOG2E
    q_cols = heads * HEAD_DIM

    @pl.when(i == 0)
    def _():
        loads, col = [], 0
        for n, (ref, count) in enumerate(((wq_ref, q_cols), (wk_ref, HEAD_DIM), (wv_ref, HEAD_DIM))):
            at = pl.ds(pl.multiple_of(near.me * count, HEAD_DIM), count)
            loads.append(pltpu.make_async_copy(ref.at[:, at], w_v.at[:, pl.ds(col, count)], w_sems.at[n]))
            col += count
        for load in loads:
            load.start()
        gather.begin()
        stage_in.start()
        for load in loads:
            load.wait()

    ht_ref[...] = h_ref[...].T
    prod = dot(h_ref[...], w_v[...])
    cos_t, sin_t = cos_ref[...], sin_ref[...]
    for a in range(heads + 1):
        val = prod[:, a * HEAD_DIM:(a + 1) * HEAD_DIM]
        rot = (val * cos_t + pltpu.roll(val, HALF, 1) * sin_t).astype(BF16)
        if a < heads:
            q_ref[:, a * HEAD_DIM:(a + 1) * HEAD_DIM] = rot
        else:
            k_ref[...] = rot
            k_s[i] = rot
    v_i = prod[:, q_cols + HEAD_DIM:].astype(BF16)
    v_ref[...] = v_i
    vt[i] = v_i.T
    acc[...] = jnp.zeros_like(acc)

    def chunk(c, carry, diagonal):
        k_c, vt_c = k_s[c], vt[c]
        scores = [dot(k_c, q_ref[:, a * HEAD_DIM:(a + 1) * HEAD_DIM], COLS_COLS) * to_log2 for a in range(heads)]
        out = []
        for a in range(heads):
            s = masked(scores[a]) if diagonal else scores[a]
            m_old, l_old = carry[a]
            m_new = jnp.maximum(m_old, jnp.max(s, axis=0, keepdims=True))
            alpha = jnp.exp2(m_old - m_new)
            p = jnp.exp2(s - m_new)
            l_new = l_old * alpha + jnp.sum(p, axis=0, keepdims=True)
            acc[a] = acc[a] * alpha + dot(vt_c, p.astype(BF16))
            out.append((m_new, l_new))
        return tuple(out)

    start = tuple((jnp.full((1, BLK), NEG_LARGE, F32), jnp.zeros((1, BLK), F32)) for _ in range(heads))
    carry = lax.fori_loop(0, i, lambda c, carry: chunk(c, carry, False), start)
    carry = chunk(i, carry, True)
    for a in range(heads):
        m_a, l_a = carry[a]
        o_ref[a * HEAD_DIM:(a + 1) * HEAD_DIM, :] = (acc[a] / l_a).astype(BF16)
        lse_ref[a:a + 1, :] = m_a + jnp.log2(l_a)

    @pl.when(i == FWD_MIDDLE)
    def _():
        gather.middle()
        stage_in.wait()
        stage_out.start()

    @pl.when(i == pl.num_programs(0) - 1)
    def _():
        gather.late()
        stage_out.wait()
        gather.end()


def forward(hidden, w_q, w_k, w_v, cos_t, sin_t, grad_out, heads):
    seq_len, width = hidden.shape
    n_blocks = seq_len // BLK
    q_cols = heads * HEAD_DIM
    pairs = heads * seq_len * (seq_len + BLK) // 2
    any_spec = pl.BlockSpec(memory_space=pl.ANY)
    rows = lambda cols: pl.BlockSpec((BLK, cols), lambda i: (i, 0))
    cols = lambda rows: pl.BlockSpec((rows, BLK), lambda i: (0, i))
    out = lambda *shape, dtype=BF16: jax.ShapeDtypeStruct(shape, dtype)
    return pl.pallas_call(
        functools.partial(forward_kernel, heads),
        grid=(n_blocks,),
        in_specs=[rows(width), any_spec, any_spec, any_spec, rows(HEAD_DIM), rows(HEAD_DIM), any_spec],
        out_specs=[rows(q_cols), rows(HEAD_DIM), rows(HEAD_DIM), cols(width), cols(q_cols), cols(8), any_spec],
        out_shape=[out(seq_len, q_cols), out(seq_len, HEAD_DIM), out(seq_len, HEAD_DIM), out(width, seq_len), out(q_cols, seq_len),
                   out(8, seq_len, dtype=F32), out(seq_len, width)],
        scratch_shapes=[pltpu.VMEM((width, q_cols + 2 * HEAD_DIM), BF16), pltpu.SemaphoreType.DMA((3,)), pltpu.VMEM((n_blocks, BLK, HEAD_DIM), BF16),
                        pltpu.VMEM((n_blocks, HEAD_DIM, BLK), BF16), pltpu.VMEM((heads, HEAD_DIM, BLK), F32), pltpu.VMEM(grad_out.shape, BF16),
                        pltpu.SemaphoreType.DMA((2,)), SEMS],
        compiler_params=comm_params(1),
        cost_estimate=pl.CostEstimate(flops=8 * pairs * HEAD_DIM + 4 * seq_len * width * q_cols, bytes_accessed=8 * seq_len * width, transcendentals=pairs),
        name="forward",
    )(hidden, w_q, w_k, w_v, cos_t, sin_t, grad_out)


def unrotate(val, cos_t, sin_t):
    return (val * cos_t - pltpu.roll(val, HALF, 1) * sin_t).astype(BF16)


def backward_kernel(heads, q_ref, k_ref, v_ref, dy_ref, wo_ref, ot_ref, lse_ref, cos_ref, sin_ref, o_ref, dkv_ref, dq_a_ref, dq_b_ref, o_all,
                    wo_v, w_sem, do_s, kt, dk_acc, dv_acc, dqt, stage, stage_sems, sems):
    i = pl.program_id(0)
    n_blocks = k_ref.shape[0] // BLK
    qk_scale = HEAD_DIM ** -0.5
    to_log2 = qk_scale * LOG2E
    near = Neighbours()
    own_rows = o_ref.shape[0]
    size = own_rows // CHUNKS
    gather = Gather(near, lambda chunk: o_ref.at[pl.ds(chunk * size, size), :], o_all, own_rows, sems)
    stage_in = pltpu.make_async_copy(o_ref, stage, stage_sems.at[0])
    stage_out = pltpu.make_async_copy(stage, gather.block(near.me, 0, CHUNKS), stage_sems.at[1])

    @pl.when(i == 0)
    def _():
        q_cols = heads * HEAD_DIM
        load = pltpu.make_async_copy(wo_ref.at[pl.ds(pl.multiple_of(near.me * q_cols, q_cols), q_cols), :], wo_v, w_sem)
        load.start()
        gather.begin()
        stage_in.start()

        @pl.loop(0, n_blocks)
        def _(c):
            kt[c] = k_ref[pl.ds(pl.multiple_of(c * BLK, BLK), BLK), :].T

        load.wait()

    cols = [slice(a * HEAD_DIM, (a + 1) * HEAD_DIM) for a in range(heads)]
    d_o = dot(dy_ref[...], wo_v[...], COLS_COLS).astype(BF16)
    do_s[...] = d_o
    dqt[...] = jnp.zeros_like(dqt)
    delta = [jnp.sum(ot_ref[cols[a], :].astype(F32) * d_o[:, cols[a]].T.astype(F32), axis=0, keepdims=True) for a in range(heads)]

    def chunk(c, diagonal):
        rows = pl.ds(pl.multiple_of(c * BLK, BLK), BLK)
        k_c, v_c, kt_c = k_ref[rows, :], v_ref[rows, :], kt[c]
        dk_c = dv_c = None
        for a in range(heads):
            q_a, do_a = q_ref[:, cols[a]], do_s[:, cols[a]]
            s = dot(k_c, q_a, COLS_COLS) * to_log2
            if diagonal:
                s = masked(s)
            p = jnp.exp2(s - lse_ref[a:a + 1, :])
            d_p = dot(v_c, do_a, COLS_COLS)
            d_s = (p * (d_p - delta[a])).astype(BF16)
            dv_a = dot(p.astype(BF16), do_a)
            dk_a = dot(d_s, q_a)
            dv_c = dv_a if dv_c is None else dv_c + dv_a
            dk_c = dk_a if dk_c is None else dk_c + dk_a
            dqt[a] += dot(kt_c, d_s)
        if diagonal:
            dk_acc[c] = dk_c
            dv_acc[c] = dv_c
        else:
            dk_acc[c] += dk_c
            dv_acc[c] += dv_c

    @pl.loop(0, i)
    def _(c):
        chunk(c, False)

    chunk(i, True)
    rows = pl.ds(pl.multiple_of(i * BLK, BLK), BLK)
    for a in range(heads):
        d_q = unrotate(dqt[a].T * qk_scale, cos_ref[rows, :], sin_ref[rows, :])
        if a < heads - 1:
            dq_a_ref[:, cols[a]] = d_q
        else:
            dq_b_ref[...] = d_q

    @pl.when(i == BWD_MIDDLE)
    def _():
        gather.middle()
        stage_in.wait()
        stage_out.start()

    @pl.when(i == BWD_LATE)
    def _():
        gather.late()

    @pl.when(i == n_blocks - 1)
    def _():
        @pl.loop(0, n_blocks)
        def _(c):
            rows_c = pl.ds(pl.multiple_of(c * BLK, BLK), BLK)
            dkv_ref[rows_c, :HEAD_DIM] = unrotate(dk_acc[c] * qk_scale, cos_ref[rows_c, :], sin_ref[rows_c, :])
            dkv_ref[rows_c, HEAD_DIM:] = dv_acc[c].astype(BF16)

        stage_out.wait()
        gather.end()


def backward(q, k, v, d_out, w_o, ot, lse, cos_t, sin_t, heads, sp_size):
    seq_len, width = d_out.shape
    n_blocks = seq_len // BLK
    whole = lambda i: (0, 0)
    pairs = heads * seq_len * (seq_len + BLK) // 2
    q_cols = heads * HEAD_DIM
    any_spec = pl.BlockSpec(memory_space=pl.ANY)
    rows = lambda cols: pl.BlockSpec((BLK, cols), lambda i: (i, 0))
    cols = lambda rows: pl.BlockSpec((rows, BLK), lambda i: (0, i))
    kv_spec = pl.BlockSpec(k.shape, whole)
    last = (heads - 1) * HEAD_DIM
    out = lambda *shape: jax.ShapeDtypeStruct(shape, BF16)
    return pl.pallas_call(
        functools.partial(backward_kernel, heads),
        grid=(n_blocks,),
        in_specs=[rows(q_cols), kv_spec, kv_spec, rows(width), any_spec, cols(q_cols), cols(8), kv_spec, kv_spec, any_spec],
        out_specs=[pl.BlockSpec((seq_len, 2 * HEAD_DIM), whole), rows(last), rows(HEAD_DIM), any_spec],
        out_shape=[out(seq_len, 2 * HEAD_DIM), out(seq_len, last), out(seq_len, HEAD_DIM), out(q_cols * sp_size, seq_len)],
        scratch_shapes=[pltpu.VMEM((q_cols, width), BF16), pltpu.SemaphoreType.DMA, pltpu.VMEM((BLK, q_cols), BF16),
                        pltpu.VMEM((n_blocks, HEAD_DIM, BLK), BF16), pltpu.VMEM((n_blocks, BLK, HEAD_DIM), F32),
                        pltpu.VMEM((n_blocks, BLK, HEAD_DIM), F32), pltpu.VMEM((heads, HEAD_DIM, BLK), F32), pltpu.VMEM(ot.shape, BF16),
                        pltpu.SemaphoreType.DMA((2,)), SEMS],
        compiler_params=comm_params(2),
        cost_estimate=pl.CostEstimate(flops=20 * pairs * HEAD_DIM + 2 * seq_len * width * q_cols, bytes_accessed=8 * seq_len * q_cols, transcendentals=pairs),
        name="backward",
    )(q, k, v, d_out, w_o, ot, lse, cos_t, sin_t, ot)


def lanes(*parts):
    return jnp.concatenate(parts, axis=1)


def products_kernel(ot_ref, ht_ref, dy_ref, d_kv_ref, d_qa_ref, d_qb_ref, tiles, kv_all, qa_all, qb_all,
                    a_buf, b_buf, tile, a_sems, b_sems, t_sems, x_sems, kv_s, qa_s, qb_s, stage_sems, kv_sems, qa_sems, qb_sems):
    near = Neighbours()
    core = lax.rem(near.me, 2)
    half = a_buf.shape[1]
    seq_len = d_kv_ref.shape[0]
    chunk = seq_len // CHUNKS
    n_cols = d_kv_ref.shape[1]
    n_o, n_all = dy_ref.shape[1] // (2 * n_cols), tiles.shape[1]
    n_kv = (n_all - n_o) // 2

    def gather_of(src, dst, sems):
        return Gather(near, lambda c: src.at[pl.ds(c * chunk, chunk), :], dst, seq_len, sems)

    gathers = [gather_of(d_kv_ref, kv_all, kv_sems), gather_of(d_qa_ref, qa_all, qa_sems), gather_of(d_qb_ref, qb_all, qb_sems)]
    stage_in = [pltpu.make_async_copy(src, dst, stage_sems.at[0, n]) for n, (src, dst) in enumerate(((d_kv_ref, kv_s), (d_qa_ref, qa_s), (d_qb_ref, qb_s)))]
    stage_out = [pltpu.make_async_copy(src, gather.block(near.me, 0, CHUNKS), stage_sems.at[1, n])
                 for n, (src, gather) in enumerate(zip((kv_s, qa_s, qb_s), gathers))]
    own_rows = pl.ds(pl.multiple_of(core * half, half), half)
    a_loads = [pltpu.make_async_copy(ref.at[own_rows, :], a_buf.at[n], a_sems.at[n]) for n, ref in enumerate((ot_ref, ht_ref))]

    def b_load(source, p, slot, g):
        if source is dy_ref:
            src = dy_ref.at[:, pl.ds(pl.multiple_of((2 * p + g) * n_cols, n_cols), n_cols)]
        else:
            src = source.at[pl.ds(pl.multiple_of((2 * p + g) * seq_len, seq_len), seq_len), :]
        return pltpu.make_async_copy(src, b_buf.at[slot, :, pl.ds(g * n_cols, n_cols)], b_sems.at[slot, g])

    def start_b(step):
        slot = lax.rem(step, 2)
        for source, low, high in ((dy_ref, 0, n_o), (kv_all, n_o, n_o + n_kv), (qa_all, n_o + n_kv, n_all)):
            @pl.when(jnp.logical_and(step >= low, step < high))
            def _():
                for g in range(2):
                    b_load(source, step - low, slot, g).start()

    def keep(step):
        return pltpu.make_async_copy(tile.at[lax.rem(step, 2)], tiles.at[core, step], t_sems.at[lax.rem(step, 2)])

    def give(step):
        return send(tile.at[lax.rem(step, 2)], tiles.at[core, step], x_sems, step, near.sib)

    near.meet([near.sib, near.xn, near.yn])
    for c in range(CHUNKS):
        gathers[0].start(c)
    a_loads[0].start()
    start_b(jnp.int32(0))
    for load in stage_in:
        load.start()
    a_loads[1].start()
    a_loads[0].wait()

    @pl.loop(0, n_all)
    def _(step):
        slot = lax.rem(step, 2)
        for g in range(2):
            b_load(dy_ref, 0, slot, g).wait()

        @pl.when(jnp.logical_and(step != n_o - 1, step != n_o + n_kv - 1))
        def _():
            start_b(step + 1)

        @pl.when(step >= 2)
        def _():
            keep(step - 2).wait()
            give(step - 2).wait_send()

        @pl.when(step == n_o)
        def _():
            a_loads[1].wait()

        tile[slot] = dot(a_buf[jnp.where(step < n_o, 0, 1)], b_buf[slot])
        keep(step).start()
        give(step).start()

        @pl.when(step == n_o - 2)
        def _():
            for load, store in zip(stage_in, stage_out):
                load.wait()
                store.start()
            gathers[0].middle()

        @pl.when(step == n_o - 1)
        def _():
            gathers[0].late()
            for c in range(CHUNKS):
                gathers[1].start(c)
            stage_out[0].wait()
            gathers[0].end()
            start_b(step + 1)

        @pl.when(step == n_o + n_kv - 1)
        def _():
            gathers[1].middle()
            gathers[1].late()
            for c in range(CHUNKS):
                gathers[2].start(c)
            stage_out[1].wait()
            gathers[1].end()
            start_b(step + 1)

        @pl.when(step == n_all - 3)
        def _():
            gathers[2].middle()

        @pl.when(step == n_all - 2)
        def _():
            gathers[2].late()

    stage_out[2].wait()
    gathers[2].end()
    for step in (n_all - 2, n_all - 1):
        keep(step).wait()
        give(step).wait_send()

    @pl.loop(0, n_all)
    def _(step):
        give(step).wait_recv()


def products(ot_all, ht, d_out, d_kv, d_qa, d_qb, sp_size):
    width, seq_len = ht.shape
    half = width // 2
    cols = 2 * d_kv.shape[1]
    n_all = d_out.shape[1] // cols + 2 * sp_size * d_kv.shape[1] // cols
    any_spec = pl.BlockSpec(memory_space=pl.ANY)
    gathered = [jax.ShapeDtypeStruct((sp_size * seq_len, d.shape[1]), BF16) for d in (d_kv, d_qa, d_qb)]
    return pl.pallas_call(
        products_kernel,
        in_specs=[any_spec] * 6,
        out_specs=[any_spec] * 4,
        out_shape=[jax.ShapeDtypeStruct((2, n_all, half, cols), F32)] + gathered,
        scratch_shapes=[pltpu.VMEM((2, half, seq_len), BF16), pltpu.VMEM((2, seq_len, cols), BF16), pltpu.VMEM((2, half, cols), F32),
                        pltpu.SemaphoreType.DMA((2,)), pltpu.SemaphoreType.DMA((2, 2)), pltpu.SemaphoreType.DMA((2,)),
                        pltpu.SemaphoreType.DMA((2, n_all)), pltpu.VMEM(d_kv.shape, BF16), pltpu.VMEM(d_qa.shape, BF16), pltpu.VMEM(d_qb.shape, BF16),
                        pltpu.SemaphoreType.DMA((2, 3)), SEMS, SEMS, SEMS],
        compiler_params=pltpu.CompilerParams(vmem_limit_bytes=VMEM_LIMIT, collective_id=3, has_side_effects=True),
        cost_estimate=pl.CostEstimate(flops=2 * half * cols * seq_len * n_all, bytes_accessed=8 * half * cols * n_all, transcendentals=0),
        name="products",
    )(ot_all, ht, d_out, d_kv, d_qa, d_qb)


def finish_kernel(heads, n_o, n_kv, ht_ref, d_ref, tiles, wq_ref, wk_ref, wv_ref, wo_ref, tile, sems, ring, ring_sems):
    n_cols = d_ref.shape[2]
    n_j = pl.num_programs(1)
    step = pl.program_id(0) * n_j + pl.program_id(1)
    slot = lax.rem(step, 2)
    half = ring.shape[2]
    every = [(c, t) for t in range(tiles.shape[1]) for c in range(2)]
    groups = [every[g:g + RING] for g in range(0, len(every), RING)]

    def pieces(c, t):
        rows = pl.ds(c * half, half)
        cols = ring.shape[3]
        if t < n_o:
            return [(0, cols, wo_ref.at[rows, pl.ds(t * cols, cols)])]
        if t < n_o + n_kv:
            return [(n * HEAD_DIM, HEAD_DIM, (wk_ref, wv_ref)[n % 2].at[rows, pl.ds(((t - n_o) * 2 + n // 2) * HEAD_DIM, HEAD_DIM)]) for n in range(4)]
        wide = (heads - 1) * HEAD_DIM
        return [(n * wide, wide, wq_ref.at[rows, pl.ds(((t - n_o - n_kv) * 2 + n) * heads * HEAD_DIM, wide)]) for n in range(2)]

    def ins(g):
        return [pltpu.make_async_copy(tiles.at[c, t], ring.at[g % 2, n], ring_sems.at[0, g % 2, n, 0]) for n, (c, t) in enumerate(groups[g])]

    def outs(g):
        return [pltpu.make_async_copy(ring.at[g % 2, n, :, pl.ds(col, count)], dst, ring_sems.at[1, g % 2, n, m])
                for n, (c, t) in enumerate(groups[g]) for m, (col, count, dst) in enumerate(pieces(c, t))]

    for g in range(len(groups) + 2):
        @pl.when(step == g)
        def _():
            if 0 <= g - 1 < len(groups):
                for copy in ins(g - 1):
                    copy.wait()
                for copy in outs(g - 1):
                    copy.start()
            if 0 <= g - 2 < len(groups):
                for copy in outs(g - 2):
                    copy.wait()
            if g < len(groups):
                for copy in ins(g):
                    copy.start()

    def copies(step, slot):
        rows = pl.ds(pl.multiple_of((step // n_j) * MROWS, MROWS), MROWS)
        out = []
        for g in range(2):
            col = ((lax.rem(step, n_j) * 2 + g + 1) * heads - 1) * HEAD_DIM
            out.append(pltpu.make_async_copy(tile.at[slot, :, pl.ds(g * n_cols, n_cols)],
                                             wq_ref.at[rows, pl.ds(pl.multiple_of(col, HEAD_DIM), n_cols)], sems.at[slot, g]))
        return out

    @pl.when(step >= 2)
    def _():
        for copy in copies(step - 2, slot):
            copy.wait()

    tile[slot] = dot(ht_ref[...], lanes(d_ref[0], d_ref[1]))
    for copy in copies(step, slot):
        copy.start()

    @pl.when(step == pl.num_programs(0) * n_j - 1)
    def _():
        for copy in copies(step - 1, 1 - slot) + copies(step, slot):
            copy.wait()


def finish(ht, d_q, tiles, heads, n_o, n_kv):
    width, seq_len = ht.shape
    groups, _, n_cols = d_q.shape
    steps = (width // MROWS) * (groups // 2)
    assert -(-2 * tiles.shape[1] // RING) + 2 <= steps
    any_spec = pl.BlockSpec(memory_space=pl.ANY)
    out = lambda cols: jax.ShapeDtypeStruct((width, cols), F32)
    return pl.pallas_call(
        functools.partial(finish_kernel, heads, n_o, n_kv),
        grid=(width // MROWS, groups // 2),
        in_specs=[pl.BlockSpec((MROWS, seq_len), lambda m, j: (m, 0)), pl.BlockSpec((2, seq_len, n_cols), lambda m, j: (j, 0, 0)), any_spec],
        out_specs=[any_spec] * 4,
        out_shape=[out(groups * heads * HEAD_DIM), out(groups * HEAD_DIM), out(groups * HEAD_DIM),
                   jax.ShapeDtypeStruct((groups * heads * HEAD_DIM, width), F32)],
        scratch_shapes=[pltpu.VMEM((2, MROWS, 2 * n_cols), F32), pltpu.SemaphoreType.DMA((2, 2)), pltpu.VMEM((2, RING) + tiles.shape[2:], F32),
                        pltpu.SemaphoreType.DMA((2, 2, RING, 4))],
        compiler_params=params(2),
        cost_estimate=pl.CostEstimate(flops=2 * width * seq_len * groups * n_cols, bytes_accessed=2 * width * seq_len, transcendentals=0),
        name="finish",
    )(ht, d_q, tiles)


def d_hidden_kernel(me_ref, dkv_ref, dq_ref, wk_ref, wv_ref, wq0_ref, wq1_ref, acc_ref):
    prod = dot(lanes(dkv_ref[0], dq_ref[0]), lanes(wk_ref[...], wv_ref[...], wq0_ref[...], wq1_ref[...]), COLS_COLS)

    @pl.when(pl.program_id(0) == 0)
    def _():
        acc_ref[...] = prod

    @pl.when(pl.program_id(0) > 0)
    def _():
        acc_ref[...] += prod


def d_hidden(me, d_kv, d_q, w_k, w_v, w_q, tok_count, heads):
    width = w_q.shape[0]
    groups = d_kv.shape[0]
    own_spec = pl.BlockSpec((1, tok_count, 2 * HEAD_DIM), lambda j, me_ref: (j, me_ref[0], 0))
    w_spec = lambda scale, off: pl.BlockSpec((width, HEAD_DIM), lambda j, me_ref: (0, j * scale + off))
    return pl.pallas_call(
        d_hidden_kernel,
        grid_spec=pltpu.PrefetchScalarGridSpec(
            num_scalar_prefetch=1, grid=(groups,),
            in_specs=[own_spec, own_spec, w_spec(1, 0), w_spec(1, 0), w_spec(heads, 0), w_spec(heads, 1)],
            out_specs=pl.BlockSpec((tok_count, width), lambda j, me_ref: (0, 0))),
        out_shape=jax.ShapeDtypeStruct((tok_count, width), F32),
        compiler_params=params(),
        cost_estimate=pl.CostEstimate(flops=8 * tok_count * width * groups * HEAD_DIM, bytes_accessed=8 * width * groups * HEAD_DIM, transcendentals=0),
        name="d_hidden",
    )(me, d_kv, d_q, w_k, w_v, w_q, w_q)


def grad_x_kernel(me_ref, dq_ref, wq0_ref, wq1_ref, part_ref, x_ref, dy_ref, gain_ref, gx_ref, gg_ref, acc):
    j = pl.program_id(0)
    prod = dot(lanes(dq_ref[0], dq_ref[1]), lanes(wq0_ref[...], wq1_ref[...]), COLS_COLS)

    @pl.when(j == 0)
    def _():
        acc[...] = part_ref[...] + prod

    @pl.when(j > 0)
    def _():
        acc[...] += prod

    @pl.when(j == pl.num_programs(0) - 1)
    def _():
        gain = gain_ref[...]
        gg_ref[...] = jnp.zeros_like(gg_ref)

        @pl.loop(0, x_ref.shape[0] // ROWS)
        def _(r):
            rows = pl.ds(pl.multiple_of(r * ROWS, ROWS), ROWS)
            x_f = x_ref[rows, :].astype(F32)
            inv_rms = lax.rsqrt(jnp.mean(x_f * x_f, axis=-1, keepdims=True) + NORM_EPS)
            normed = x_f * inv_rms
            d_hid = acc[rows, :]
            both = d_hid * normed
            gg_ref[...] += jnp.sum(both.reshape(ROWS // 8, 8, both.shape[1]), axis=0)
            mean = jnp.mean(both * gain, axis=-1, keepdims=True)
            d_x = inv_rms * (d_hid * gain - normed * mean)
            gx_ref[rows, :] = (dy_ref[rows, :].astype(F32) + d_x).astype(BF16)


def grad_x_final(me, d_q, w_q, part, x, grad_out, gain_f, heads):
    tok_count, width = x.shape
    groups = d_q.shape[0]
    whole = lambda j, me_ref: (0, 0)
    w_spec = lambda g: pl.BlockSpec((width, HEAD_DIM), lambda j, me_ref: (0, (2 * j + g + 1) * heads - 1))
    full = pl.BlockSpec((tok_count, width), whole)
    return pl.pallas_call(
        grad_x_kernel,
        grid_spec=pltpu.PrefetchScalarGridSpec(
            num_scalar_prefetch=1, grid=(groups // 2,),
            in_specs=[pl.BlockSpec((2, tok_count, HEAD_DIM), lambda j, me_ref: (j, me_ref[0], 0)), w_spec(0), w_spec(1), full, full, full,
                      pl.BlockSpec((1, width), whole)],
            out_specs=[full, pl.BlockSpec((8, width), whole)],
            scratch_shapes=[pltpu.VMEM((tok_count, width), F32)]),
        out_shape=[jax.ShapeDtypeStruct((tok_count, width), BF16), jax.ShapeDtypeStruct((8, width), F32)],
        compiler_params=params(),
        cost_estimate=pl.CostEstimate(flops=2 * tok_count * width * groups * HEAD_DIM, bytes_accessed=8 * width * tok_count, transcendentals=0),
        name="grad_x",
    )(me, d_q, w_q, w_q, part, x, grad_out, gain_f)


def solution(mesh):
    sp_size = mesh.shape['sp']
    seq_spec = P(('dp', 'sp'), None)
    pos_spec = P(('dp', 'sp'))
    replicated = P(None, None)
    part_rows = P('dp', None)

    def local_step(x, grad_out, positions, gain, w_q, w_k, w_v, w_o):
        tok_count = x.shape[0]
        n_heads = w_q.shape[1] // HEAD_DIM
        heads = n_heads // sp_size
        me = lax.axis_index('sp')
        gain_f = gain.astype(F32).reshape(1, -1)
        hidden, cos_t, sin_t = gather_h(x, gain_f, positions, sp_size)
        q, k, v, ht, ot, lse, d_out = forward(hidden, w_q, w_k, w_v, cos_t, sin_t, grad_out, heads)
        *grads, ot_all = backward(q, k, v, d_out, w_o, ot, lse, cos_t, sin_t, heads, sp_size)
        tiles, *gathered = products(ot_all, ht, d_out, *grads, sp_size)
        dkv_all, dqa_all, dqb_all = [val.reshape(sp_size, -1, val.shape[1]) for val in gathered]
        n_kv = sp_size // 2
        grad_wq, grad_wk, grad_wv, grad_wo = finish(ht, dqb_all, tiles, heads, tiles.shape[1] - 2 * n_kv, n_kv)
        o_own = lax.dynamic_slice_in_dim(ot_all, me * tok_count, tok_count, axis=1)
        result = (x.astype(F32) + dot(o_own, w_o, ROWS_ROWS)).astype(BF16)
        me_arr = me.reshape(1).astype(jnp.int32)
        part = d_hidden(me_arr, dkv_all, dqa_all, w_k, w_v, w_q, tok_count, heads)
        grad_x, gg = grad_x_final(me_arr, dqb_all, w_q, part, x, grad_out, gain_f, heads)
        grad_gain = jnp.sum(lax.all_gather(gg, 'sp', axis=0, tiled=True), axis=0)
        return result, grad_x, grad_wq, grad_wk, grad_wv, grad_wo, grad_gain

    return jax.shard_map(local_step, mesh=mesh,
                         in_specs=(seq_spec, seq_spec, pos_spec, P(None), replicated, replicated, replicated, replicated),
                         out_specs=(seq_spec, seq_spec, part_rows, part_rows, part_rows, part_rows, P('dp')),
                         check_vma=False)
```

profile of v0, /device:TPU:0, one launch (start us, length us, event | category | flops | bytes accessed | tf_op | source)
XLA Modules:
  0.0 684.1 jit_solution(6288556822040344124)
XLA Ops:
  0.6 1.3 reshape.38
  1.9 1.3 broadcast_in_dim.4.pos_ref
  3.2 0.6 maximum_bitcast_fusion.freq_ref
  3.8 114.5 %gather_h.1 = (bf16[4096,3072]{1,0:T(8,128)(2,1)}, f32[4096,128]{1,0:T(8,128)}, f32[4096,128]{1,0:T(8,128)}) custom-call(bf16[512,3072]{1,0:T(8,128)(2,1)} %x_ref.3, f32[1,3072]{1,0:T(1,128)} %bitcast.12, s32[8,512]{1,0:T(8,128)} %broadcast_in_dim.4.pos_ref, f32[1,128]{1,0:T(1,128)} %maximum_bitcast_fusion.freq_ref), custom_call_target="tpu_custom_call" | custom-call | tf_op jit(solution)/shard_map/gather_h/pallas_call | solution.py:191
  118.3 112.0 %forward.1 = (bf16[4096,384]{1,0:T(8,128)(2,1)}, bf16[4096,128]{1,0:T(8,128)(2,1)}, bf16[4096,128]{1,0:T(8,128)(2,1)}, bf16[3072,4096]{1,0:T(8,128)(2,1)}, bf16[...) custom-call(bf16[4096,3072]{1,0:T(8,128)(2,1)} %get-tuple-element.31.h_ref, ...), custom_call_target="tpu_custom_call" | custom-call | flops 48318382080 | bytes 100663296 | tf_op jit(solution)/shard_map/forward/pallas_call | solution.py:296
  230.3 0.0 copy-start
  230.3 121.5 %backward.1 = (bf16[4096,256]{1,0:T(8,128)(2,1)}, bf16[4096,256]{1,0:T(8,128)(2,1)}, bf16[4096,128]{1,0:T(8,128)(2,1)}, bf16[3072,4096]{1,0:T(8,128)(2,1)}) custom-call(bf16[4096,384]{1,0:T(8,128)(2,1)} %get-tuple-element.34.q_ref, bf16[4096,128]{1,0:T(8,128)(2,1)} %get-tuple-element.35.k_ref, bf16[4096,128]{1,0:T(8,128)(2,1)} %get-tuple-element.36.v_ref, ...), custom_call_target="tpu_custom_call" | custom-call | flops 82141249536 | bytes 12582912 | tf_op jit(solution)/shard_map/backward/pallas_call | solution.py:420
  351.9 0.0 copy-done
  351.9 16.2 %add_convert_fusion = bf16[512,3072]{1,0:T(8,128)(2,1)} fusion(bf16[512,3072]{1,0:T(8,128)(2,1)S(1)} %copy-done, bf16[3072,3072]{1,0:T(8,128)(2,1)} %wo_ref.1, bf16[3072,4096]{1,0:T(8,128)(2,1)} %get-tuple-element.40.ot_ref, s32[]{:T(128)S(6)} %select_n.3), kind=kOutput, calls=%fused_computation | convolution fusion | flops 9668395008 | bytes 28311556 | tf_op jit(solution)/shard_map/dot_general | solution.py:31
  368.0 179.3 %products.1 = (f32[2,14,1536,512]{3,2,1,0:T(8,128)}, bf16[32768,256]{1,0:T(8,128)(2,1)}, bf16[32768,256]{1,0:T(8,128)(2,1)}, bf16[32768,128]{1,0:T(8,128)(2,1)}) custom-call(bf16[3072,4096]{1,0:T(8,128)(2,1)} %get-tuple-element.40.ot_ref, bf16[3072,4096]{1,0:T(8,128)(2,1)} %get-tuple-element.41.ht_ref, bf16[4096,3072]{1,0:T(8,128)(2,1)} %get-tuple-element.37.dy_ref, ...), custom_call_target="tpu_custom_call" | custom-call | flops 90194313216 | bytes 88080384 | tf_op jit(solution)/shard_map/products/pallas_call | solution.py:567
  547.3 24.5 %d_hidden.1.part_ref = f32[512,3072]{1,0:T(8,128)} custom-call(s32[1]{0:T(128)} %bitcast.2.me_ref, bf16[8,4096,256]{2,1,0:T(8,128)(2,1)} %bitcast.10, bf16[8,4096,256]{2,1,0:T(8,128)(2,1)} %bitcast.11, bf16[3072,1024]{1,0:T(8,128)(2,1)} %wk_ref.3, bf16[3072,1024]{1,0:T(8,128)(2,1)} %wv_ref.3, bf16[3072,3072]{1,0:T(8,128)(2,1)} %wq1_ref.3, ...), custom_call_target="tpu_custom_call" | custom-call | flops 12884901888 | bytes 25165824 | tf_op jit(solution)/shard_map/d_hidden/pallas_call | solution.py:686
  571.8 18.8 %grad_x.1 = (bf16[512,3072]{1,0:T(8,128)(2,1)}, f32[8,3072]{1,0:T(8,128)}) custom-call(s32[1]{0:T(128)} %bitcast.2.me_ref, bf16[8,4096,128]{2,1,0:T(8,128)(2,1)} %bitcast.8, bf16[3072,3072]{1,0:T(8,128)(2,1)} %wq1_ref.3, bf16[3072,3072]{1,0:T(8,128)(2,1)} %wq1_ref.3, f32[512,3072]{1,0:T(8,128)} %d_hidden.1.part_ref, bf16[512,3072]{1,0:T(8,128)(2,1)} %x_ref.3, ...), custom_call_target="tpu_custom_call" | custom-call | flops 3221225472 | bytes 12582912 | tf_op jit(solution)/shard_map/grad_x/pallas_call | solution.py:736
  590.6 0.0 copy-start.1
  590.6 82.6 %finish.1 = (f32[3072,3072]{1,0:T(8,128)}, f32[3072,1024]{1,0:T(8,128)}, f32[3072,1024]{1,0:T(8,128)}, f32[3072,3072]{1,0:T(8,128)}) custom-call(bf16[3072,4096]{1,0:T(8,128)(2,1)} %get-tuple-element.41.ht_ref, bf16[8,4096,128]{2,1,0:T(8,128)(2,1)} %bitcast.9, f32[2,14,1536,512]{3,2,1,0:T(8,128)} %get-tuple-element.49.tiles), custom_call_target="tpu_custom_call" | custom-call | flops 25769803776 | bytes 25165824 | tf_op jit(solution)/shard_map/finish/pallas_call | solution.py:654
  673.2 0.0 copy-done.1
  673.2 10.3 %all_gather.3 = f32[64,3072]{1,0:T(8,128)S(1)} all-gather(f32[8,3072]{1,0:T(8,128)S(1)} %copy-done.1), channel_id=1, replica_groups=mesh['dp'=2,'sp'=8] {'sp'}, dimensions={0}, use_global_device_ids=true | all-gather | bytes 884736 | tf_op jit(solution)/shard_map/all_gather | solution.py:776
  683.4 0.7 reduce_sum.9
  (1 shorter events, 0.0 us)
Async XLA Ops:
  230.3 121.5 %copy-start = (bf16[512,3072]{1,0:T(8,128)(2,1)S(1)}, bf16[512,3072]{1,0:T(8,128)(2,1)}, u32[]{:S(2)}) copy-start(bf16[512,3072]{1,0:T(8,128)(2,1)} %x_ref.3) | copy-start | bytes 9437188
  590.6 82.6 %copy-start.1 = (f32[8,3072]{1,0:T(8,128)S(1)}, f32[8,3072]{1,0:T(8,128)}, u32[]{:S(2)}) copy-start(f32[8,3072]{1,0:T(8,128)} %get-tuple-element.54) | copy-start | bytes 294916
where the time goes:
time: 684 us
  Pallas kernels  653 us (95%)
  matrix products  16.2 us (2%)
  blocking collectives  10.3 us (2%)
    pallas_call x1, Pallas kernels, products(): pl.pallas_call(products_kernel, in_specs=[any_spec] * 6, out_specs=[any_s...  179 us
    pallas_call x1, Pallas kernels, backward(): pl.pallas_call(functools.partial(backward_kernel, heads), grid=(n_blocks,...  121 us
    pallas_call x1, Pallas kernels, gather_h(): pl.pallas_call(gather_h_kernel, in_specs=[any_spec, vmem, vmem, vmem], ou...  115 us
    pallas_call x1, Pallas kernels, forward(): pl.pallas_call(functools.partial(forward_kernel, heads), grid=(n_blocks,)...  112 us
    pallas_call x1, Pallas kernels, finish(): pl.pallas_call(functools.partial(finish_kernel, heads, n_o, n_kv), grid=(...  82.6 us
    pallas_call x1, Pallas kernels, d_hidden(): pl.pallas_call(d_hidden_kernel, grid_spec=pltpu.PrefetchScalarGridSpec(nu...  24.5 us
    pallas_call x1, Pallas kernels, grad_x_final(): pl.pallas_call(grad_x_kernel, grid_spec=pltpu.PrefetchScalarGridSpec(num_...  18.8 us
    dot_general x1, matrix products, dot(): return lax.dot_general(a, b, dims, preferred_element_type=F32)  16.2 us

commit v1 on v0

--- a/solution.py
+++ b/solution.py
@@ -18,13 +18,13 @@
 FWD_MIDDLE, BWD_MIDDLE, BWD_LATE = 5, 4, 5
 MROWS = 1024
 RING = 3
-ROWS = 64
+ROW_STEPS = 8
 F32 = jnp.float32
 BF16 = jnp.bfloat16
 ROWS_ROWS = (((0,), (0,)), ((), ()))
 COLS_COLS = (((1,), (1,)), ((), ()))
 ROWS_COLS = (((0,), (1,)), ((), ()))
-VMEM_LIMIT = 60 * 1024 * 1024
+VMEM_LIMIT = 63 * 1024 * 1024
 
 
 def dot(a, b, dims=(((1,), (0,)), ((), ()))):
@@ -437,26 +437,45 @@
     return jnp.concatenate(parts, axis=1)
 
 
-def products_kernel(ot_ref, ht_ref, dy_ref, d_kv_ref, d_qa_ref, d_qb_ref, tiles, kv_all, qa_all, qb_all,
-                    a_buf, b_buf, tile, a_sems, b_sems, t_sems, x_sems, kv_s, qa_s, qb_s, stage_sems, kv_sems, qa_sems, qb_sems):
+def products_kernel(heads, ot_ref, ht_ref, dy_ref, d_kv_ref, d_qa_ref, d_qb_ref, x_ref, wo_ref, wk_ref, wv_ref, wq_ref,
+                    tiles, kv_all, qa_all, qb_all, res_ref, hid_ref,
+                    a_buf, b_buf, tile, a_sem, b_sems, t_sems, x_sems, stage, stage_sems, ot_v, o_v, x_v, io_sems, own, own_sems, w_v, w_sems, acc,
+                    kv_sems, qa_sems, qb_sems):
     near = Neighbours()
     core = lax.rem(near.me, 2)
-    half = a_buf.shape[1]
+    half = a_buf.shape[0]
     seq_len = d_kv_ref.shape[0]
+    rows, width = x_ref.shape
     chunk = seq_len // CHUNKS
     n_cols = d_kv_ref.shape[1]
-    n_o, n_all = dy_ref.shape[1] // (2 * n_cols), tiles.shape[1]
+    n_o, n_all = width // (2 * n_cols), tiles.shape[1]
     n_kv = (n_all - n_o) // 2
 
     def gather_of(src, dst, sems):
         return Gather(near, lambda c: src.at[pl.ds(c * chunk, chunk), :], dst, seq_len, sems)
 
+    local = (d_kv_ref, d_qa_ref, d_qb_ref)
     gathers = [gather_of(d_kv_ref, kv_all, kv_sems), gather_of(d_qa_ref, qa_all, qa_sems), gather_of(d_qb_ref, qb_all, qb_sems)]
-    stage_in = [pltpu.make_async_copy(src, dst, stage_sems.at[0, n]) for n, (src, dst) in enumerate(((d_kv_ref, kv_s), (d_qa_ref, qa_s), (d_qb_ref, qb_s)))]
-    stage_out = [pltpu.make_async_copy(src, gather.block(near.me, 0, CHUNKS), stage_sems.at[1, n])
-                 for n, (src, gather) in enumerate(zip((kv_s, qa_s, qb_s), gathers))]
+
+    def stage_in(n):
+        return pltpu.make_async_copy(local[n], stage.at[:, pl.ds(0, local[n].shape[1])], stage_sems.at[0])
+
+    def stage_out(n):
+        return pltpu.make_async_copy(stage.at[:, pl.ds(0, local[n].shape[1])], gathers[n].block(near.me, 0, CHUNKS), stage_sems.at[1])
+
+    def copy_own(n):
+        stage_in(n).wait()
+        stage_out(n).start()
+
     own_rows = pl.ds(pl.multiple_of(core * half, half), half)
-    a_loads = [pltpu.make_async_copy(ref.at[own_rows, :], a_buf.at[n], a_sems.at[n]) for n, ref in enumerate((ot_ref, ht_ref))]
+    tokens = pl.ds(pl.multiple_of(near.me * rows, rows), rows)
+    ot_load = pltpu.make_async_copy(ot_ref.at[:, tokens], ot_v, io_sems.at[0])
+    x_load = pltpu.make_async_copy(x_ref, x_v, io_sems.at[1])
+    res_store = pltpu.make_async_copy(x_v, res_ref, io_sems.at[2])
+    hid_store = pltpu.make_async_copy(acc, hid_ref, io_sems.at[3])
+
+    def a_load(ref):
+        return pltpu.make_async_copy(ref.at[own_rows, :], a_buf, a_sem)
 
     def b_load(source, p, slot, g):
         if source is dy_ref:
@@ -479,15 +498,100 @@
     def give(step):
         return send(tile.at[lax.rem(step, 2)], tiles.at[core, step], x_sems, step, near.sib)
 
+    def result_part():
+        cols = b_buf.shape[2]
+
+        def w_load(n):
+            slot = lax.rem(n, 2)
+            return pltpu.make_async_copy(wo_ref.at[:, pl.ds(pl.multiple_of(n * cols, cols), cols)], b_buf.at[slot, pl.ds(0, wo_ref.shape[0]), :],
+                                         b_sems.at[slot, 0])
+
+        w_load(jnp.int32(0)).start()
+        ot_load.wait()
+
+        @pl.loop(0, ot_v.shape[0] // BLK)
+        def _(r):
+            at = pl.ds(pl.multiple_of(r * BLK, BLK), BLK)
+            o_v[:, at] = ot_v[at, :].T
+
+        x_load.wait()
+
+        @pl.loop(0, n_o)
+        def _(n):
+            w_load(n).wait()
+
+            @pl.when(n + 1 < n_o)
+            def _():
+                w_load(n + 1).start()
+
+            at = pl.ds(pl.multiple_of(n * cols, cols), cols)
+            x_v[:, at] = (x_v[:, at].astype(F32) + dot(o_v[...], b_buf[lax.rem(n, 2), :wo_ref.shape[0], :])).astype(BF16)
+
+        res_store.start()
+
+    def hidden_parts(kind):
+        per = 2 if kind == 2 else 1
+        count = own.shape[0] // per
+
+        def own_load(j, g):
+            source = (kv_all, qa_all, qb_all)[kind]
+            device, col = (2 * j + g, 0) if kind == 2 else (j, g * HEAD_DIM)
+            at = pl.ds(pl.multiple_of(device * seq_len + near.me * rows, rows), rows)
+            return pltpu.make_async_copy(source.at[at, pl.ds(col, HEAD_DIM)], own.at[j, :, pl.ds(g * HEAD_DIM, HEAD_DIM)], own_sems.at[j, g])
+
+        def w_load(j, g):
+            source = (wk_ref, wv_ref)[g] if kind == 0 else wq_ref
+            col = j if kind == 0 else heads * j + g if kind == 1 else heads * (2 * j + g + 1) - 1
+            slot = lax.rem(j, 2)
+            return pltpu.make_async_copy(source.at[:, pl.ds(pl.multiple_of(col * HEAD_DIM, HEAD_DIM), HEAD_DIM)],
+                                         w_v.at[slot, :, pl.ds(g * HEAD_DIM, HEAD_DIM)], w_sems.at[slot, g])
+
+        return count, own_load, w_load
+
+    def hidden_start(kind):
+        count, own_load, w_load = hidden_parts(kind)
+        for g in range(2):
+            w_load(jnp.int32(0), g).start()
+
+            @pl.loop(0, count)
+            def _(j):
+                own_load(j, g).start()
+
+    def hidden_add(kind):
+        count, own_load, w_load = hidden_parts(kind)
+
+        @pl.loop(0, count)
+        def _(j):
+            for g in range(2):
+                w_load(j, g).wait()
+                own_load(j, g).wait()
+
+            @pl.when(j + 1 < count)
+            def _():
+                for g in range(2):
+                    w_load(j + 1, g).start()
+
+            prod = dot(own[j], w_v[lax.rem(j, 2)], COLS_COLS)
+            if kind == 0:
+                @pl.when(j == 0)
+                def _():
+                    acc[...] = prod
+
+                @pl.when(j > 0)
+                def _():
+                    acc[...] += prod
+            else:
+                acc[...] += prod
+
     near.meet([near.sib, near.xn, near.yn])
     for c in range(CHUNKS):
         gathers[0].start(c)
-    a_loads[0].start()
+    a_load(ot_ref).start()
     start_b(jnp.int32(0))
-    for load in stage_in:
-        load.start()
-    a_loads[1].start()
-    a_loads[0].wait()
+    stage_in(0).start()
+    ot_load.start()
+    x_load.start()
+    a_load(ot_ref).wait()
 
     @pl.loop(0, n_all)
     def _(step):
@@ -506,80 +610,98 @@
 
         @pl.when(step == n_o)
         def _():
-            a_loads[1].wait()
-
-        tile[slot] = dot(a_buf[jnp.where(step < n_o, 0, 1)], b_buf[slot])
+            a_load(ht_ref).wait()
+
+        tile[slot] = dot(a_buf[...], b_buf[slot])
         keep(step).start()
         give(step).start()
 
         @pl.when(step == n_o - 2)
         def _():
-            for load, store in zip(stage_in, stage_out):
-                load.wait()
-                store.start()
+            copy_own(0)
             gathers[0].middle()
 
         @pl.when(step == n_o - 1)
         def _():
+            a_load(ht_ref).start()
             gathers[0].late()
             for c in range(CHUNKS):
                 gathers[1].start(c)
-            stage_out[0].wait()
+            stage_out(0).wait()
+            stage_in(1).start()
+            result_part()
             gathers[0].end()
             start_b(step + 1)
+            hidden_start(0)
 
         @pl.when(step == n_o + n_kv - 1)
         def _():
             gathers[1].middle()
+            copy_own(1)
+            hidden_add(0)
             gathers[1].late()
             for c in range(CHUNKS):
                 gathers[2].start(c)
-            stage_out[1].wait()
+            stage_out(1).wait()
+            stage_in(2).start()
             gathers[1].end()
             start_b(step + 1)
+            hidden_start(1)
 
         @pl.when(step == n_all - 3)
         def _():
+            copy_own(2)
             gathers[2].middle()
 
         @pl.when(step == n_all - 2)
         def _():
             gathers[2].late()
 
-    stage_out[2].wait()
+    hidden_add(1)
+    stage_out(2).wait()
     gathers[2].end()
+    hidden_start(2)
     for step in (n_all - 2, n_all - 1):
         keep(step).wait()
         give(step).wait_send()
+    hidden_add(2)
+    hid_store.start()
 
     @pl.loop(0, n_all)
     def _(step):
         give(step).wait_recv()
 
-
-def products(ot_all, ht, d_out, d_kv, d_qa, d_qb, sp_size):
+    res_store.wait()
+    hid_store.wait()
+
+
+def products(ot_all, ht, d_out, d_kv, d_qa, d_qb, x, w_o, w_k, w_v, w_q, sp_size, heads):
     width, seq_len = ht.shape
     half = width // 2
     cols = 2 * d_kv.shape[1]
-    n_all = d_out.shape[1] // cols + 2 * sp_size * d_kv.shape[1] // cols
+    n_all = width // cols + 2 * sp_size * d_kv.shape[1] // cols
     any_spec = pl.BlockSpec(memory_space=pl.ANY)
+    dma = pltpu.SemaphoreType.DMA
     gathered = [jax.ShapeDtypeStruct((sp_size * seq_len, d.shape[1]), BF16) for d in (d_kv, d_qa, d_qb)]
     return pl.pallas_call(
-        products_kernel,
-        in_specs=[any_spec] * 6,
-        out_specs=[any_spec] * 4,
-        out_shape=[jax.ShapeDtypeStruct((2, n_all, half, cols), F32)] + gathered,
-        scratch_shapes=[pltpu.VMEM((2, half, seq_len), BF16), pltpu.VMEM((2, seq_len, cols), BF16), pltpu.VMEM((2, half, cols), F32),
-                        pltpu.SemaphoreType.DMA((2,)), pltpu.SemaphoreType.DMA((2, 2)), pltpu.SemaphoreType.DMA((2,)),
-                        pltpu.SemaphoreType.DMA((2, n_all)), pltpu.VMEM(d_kv.shape, BF16), pltpu.VMEM(d_qa.shape, BF16), pltpu.VMEM(d_qb.shape, BF16),
-                        pltpu.SemaphoreType.DMA((2, 3)), SEMS, SEMS, SEMS],
+        functools.partial(products_kernel, heads),
+        in_specs=[any_spec] * 11,
+        out_specs=[any_spec] * 6,
+        out_shape=[jax.ShapeDtypeStruct((2, n_all, half, cols), F32)] + gathered
+        + [jax.ShapeDtypeStruct(x.shape, BF16), jax.ShapeDtypeStruct(x.shape, F32)],
+        scratch_shapes=[pltpu.VMEM((half, seq_len), BF16), pltpu.VMEM((2, seq_len, cols), BF16), pltpu.VMEM((2, half, cols), F32),
+                        dma, dma((2, 2)), dma((2,)), dma((2, n_all)), pltpu.VMEM(d_kv.shape, BF16), dma((2,)),
+                        pltpu.VMEM((ot_all.shape[0], x.shape[0]), BF16), pltpu.VMEM((x.shape[0], ot_all.shape[0]), BF16), pltpu.VMEM(x.shape, BF16),
+                        dma((4,)), pltpu.VMEM((sp_size, x.shape[0], 2 * HEAD_DIM), BF16), dma((sp_size, 2)),
+                        pltpu.VMEM((2, width, 2 * HEAD_DIM), BF16), dma((2, 2)), pltpu.VMEM(x.shape, F32), SEMS, SEMS, SEMS],
         compiler_params=pltpu.CompilerParams(vmem_limit_bytes=VMEM_LIMIT, collective_id=3, has_side_effects=True),
         cost_estimate=pl.CostEstimate(flops=2 * half * cols * seq_len * n_all, bytes_accessed=8 * half * cols * n_all, transcendentals=0),
         name="products",
-    )(ot_all, ht, d_out, d_kv, d_qa, d_qb)
-
-
-def finish_kernel(heads, n_o, n_kv, ht_ref, d_ref, tiles, wq_ref, wk_ref, wv_ref, wo_ref, tile, sems, ring, ring_sems):
+    )(ot_all, ht, d_out, d_kv, d_qa, d_qb, x, w_o, w_k, w_v, w_q)
+
+
+def finish_kernel(heads, n_o, n_kv, ht_ref, d_ref, hid_ref, x_ref, dy_ref, gain_ref, part_ref, tiles,
+                  wq_ref, wk_ref, wv_ref, wo_ref, gx_ref, gg_ref, res_ref, tile, sems, ring, ring_sems):
     n_cols = d_ref.shape[2]
     n_j = pl.num_programs(1)
     step = pl.program_id(0) * n_j + pl.program_id(1)
@@ -634,118 +756,61 @@
         for copy in copies(step - 2, slot):
             copy.wait()
 
-    tile[slot] = dot(ht_ref[...], lanes(d_ref[0], d_ref[1]))
+    pair = 2 * pl.program_id(1)
+    tile[slot] = dot(ht_ref[...], lanes(d_ref[pair], d_ref[pair + 1]))
     for copy in copies(step, slot):
         copy.start()
 
+    @pl.when(step == 0)
+    def _():
+        gg_ref[...] = jnp.zeros_like(gg_ref)
+
+    @pl.when(step < ROW_STEPS)
+    def _():
+        x_f = x_ref[...].astype(F32)
+        inv_rms = lax.rsqrt(jnp.mean(x_f * x_f, axis=-1, keepdims=True) + NORM_EPS)
+        normed = x_f * inv_rms
+        d_hid = hid_ref[...]
+        both = d_hid * normed
+        gain = gain_ref[...]
+        gg_ref[...] += jnp.sum(both.reshape(both.shape[0] // 8, 8, both.shape[1]), axis=0)
+        mean = jnp.mean(both * gain, axis=-1, keepdims=True)
+        d_x = inv_rms * (d_hid * gain - normed * mean)
+        gx_ref[...] = (dy_ref[...].astype(F32) + d_x).astype(BF16)
+        res_ref[...] = part_ref[...]
+
     @pl.when(step == pl.num_programs(0) * n_j - 1)
     def _():
         for copy in copies(step - 1, 1 - slot) + copies(step, slot):
             copy.wait()
 
 
-def finish(ht, d_q, tiles, heads, n_o, n_kv):
+def finish(ht, d_q, tiles, d_hid, x, grad_out, gain_f, result, heads, n_o, n_kv):
     width, seq_len = ht.shape
     groups, _, n_cols = d_q.shape
-    steps = (width // MROWS) * (groups // 2)
+    n_j = groups // 2
+    steps = (width // MROWS) * n_j
     assert -(-2 * tiles.shape[1] // RING) + 2 <= steps
     any_spec = pl.BlockSpec(memory_space=pl.ANY)
+    rows = pl.BlockSpec((x.shape[0] // ROW_STEPS, width), lambda m, j: (jnp.minimum(m * n_j + j, ROW_STEPS - 1), 0))
+    whole = lambda *shape: pl.BlockSpec(shape, lambda m, j: (0,) * len(shape))
     out = lambda cols: jax.ShapeDtypeStruct((width, cols), F32)
     return pl.pallas_call(
         functools.partial(finish_kernel, heads, n_o, n_kv),
-        grid=(width // MROWS, groups // 2),
-        in_specs=[pl.BlockSpec((MROWS, seq_len), lambda m, j: (m, 0)), pl.BlockSpec((2, seq_len, n_cols), lambda m, j: (j, 0, 0)), any_spec],
-        out_specs=[any_spec] * 4,
+        grid=(width // MROWS, n_j),
+        in_specs=[pl.BlockSpec((MROWS, seq_len), lambda m, j: (m, 0)),
+                  pl.BlockSpec(d_q.shape, lambda m, j: (0, 0, 0), pipeline_mode=pl.Buffered(1)),
+                  rows, rows, rows, whole(1, width), rows, any_spec],
+        out_specs=[any_spec] * 4 + [rows, whole(8, width), rows],
         out_shape=[out(groups * heads * HEAD_DIM), out(groups * HEAD_DIM), out(groups * HEAD_DIM),
-                   jax.ShapeDtypeStruct((groups * heads * HEAD_DIM, width), F32)],
+                   jax.ShapeDtypeStruct((groups * heads * HEAD_DIM, width), F32), jax.ShapeDtypeStruct(x.shape, BF16),
+                   jax.ShapeDtypeStruct((8, width), F32), jax.ShapeDtypeStruct(x.shape, BF16)],
         scratch_shapes=[pltpu.VMEM((2, MROWS, 2 * n_cols), F32), pltpu.SemaphoreType.DMA((2, 2)), pltpu.VMEM((2, RING) + tiles.shape[2:], F32),
                         pltpu.SemaphoreType.DMA((2, 2, RING, 4))],
         compiler_params=params(2),
         cost_estimate=pl.CostEstimate(flops=2 * width * seq_len * groups * n_cols, bytes_accessed=2 * width * seq_len, transcendentals=0),
         name="finish",
-    )(ht, d_q, tiles)
-
-
-def d_hidden_kernel(me_ref, dkv_ref, dq_ref, wk_ref, wv_ref, wq0_ref, wq1_ref, acc_ref):
-    prod = dot(lanes(dkv_ref[0], dq_ref[0]), lanes(wk_ref[...], wv_ref[...], wq0_ref[...], wq1_ref[...]), COLS_COLS)
-
-    @pl.when(pl.program_id(0) == 0)
-    def _():
-        acc_ref[...] = prod
-
-    @pl.when(pl.program_id(0) > 0)
-    def _():
-        acc_ref[...] += prod
-
-
-def d_hidden(me, d_kv, d_q, w_k, w_v, w_q, tok_count, heads):
-    width = w_q.shape[0]
-    groups = d_kv.shape[0]
-    own_spec = pl.BlockSpec((1, tok_count, 2 * HEAD_DIM), lambda j, me_ref: (j, me_ref[0], 0))
-    w_spec = lambda scale, off: pl.BlockSpec((width, HEAD_DIM), lambda j, me_ref: (0, j * scale + off))
-    return pl.pallas_call(
-        d_hidden_kernel,
-        grid_spec=pltpu.PrefetchScalarGridSpec(
-            num_scalar_prefetch=1, grid=(groups,),
-            in_specs=[own_spec, own_spec, w_spec(1, 0), w_spec(1, 0), w_spec(heads, 0), w_spec(heads, 1)],
-            out_specs=pl.BlockSpec((tok_count, width), lambda j, me_ref: (0, 0))),
-        out_shape=jax.ShapeDtypeStruct((tok_count, width), F32),
-        compiler_params=params(),
-        cost_estimate=pl.CostEstimate(flops=8 * tok_count * width * groups * HEAD_DIM, bytes_accessed=8 * width * groups * HEAD_DIM, transcendentals=0),
-        name="d_hidden",
-    )(me, d_kv, d_q, w_k, w_v, w_q, w_q)
-
-
-def grad_x_kernel(me_ref, dq_ref, wq0_ref, wq1_ref, part_ref, x_ref, dy_ref, gain_ref, gx_ref, gg_ref, acc):
-    j = pl.program_id(0)
-    prod = dot(lanes(dq_ref[0], dq_ref[1]), lanes(wq0_ref[...], wq1_ref[...]), COLS_COLS)
-
-    @pl.when(j == 0)
-    def _():
-        acc[...] = part_ref[...] + prod
-
-    @pl.when(j > 0)
-    def _():
-        acc[...] += prod
-
-    @pl.when(j == pl.num_programs(0) - 1)
-    def _():
-        gain = gain_ref[...]
-        gg_ref[...] = jnp.zeros_like(gg_ref)
-
-        @pl.loop(0, x_ref.shape[0] // ROWS)
-        def _(r):
-            rows = pl.ds(pl.multiple_of(r * ROWS, ROWS), ROWS)
-            x_f = x_ref[rows, :].astype(F32)
-            inv_rms = lax.rsqrt(jnp.mean(x_f * x_f, axis=-1, keepdims=True) + NORM_EPS)
-            normed = x_f * inv_rms
-            d_hid = acc[rows, :]
-            both = d_hid * normed
-            gg_ref[...] += jnp.sum(both.reshape(ROWS // 8, 8, both.shape[1]), axis=0)
-            mean = jnp.mean(both * gain, axis=-1, keepdims=True)
-            d_x = inv_rms * (d_hid * gain - normed * mean)
-            gx_ref[rows, :] = (dy_ref[rows, :].astype(F32) + d_x).astype(BF16)
-
-
-def grad_x_final(me, d_q, w_q, part, x, grad_out, gain_f, heads):
-    tok_count, width = x.shape
-    groups = d_q.shape[0]
-    whole = lambda j, me_ref: (0, 0)
-    w_spec = lambda g: pl.BlockSpec((width, HEAD_DIM), lambda j, me_ref: (0, (2 * j + g + 1) * heads - 1))
-    full = pl.BlockSpec((tok_count, width), whole)
-    return pl.pallas_call(
-        grad_x_kernel,
-        grid_spec=pltpu.PrefetchScalarGridSpec(
-            num_scalar_prefetch=1, grid=(groups // 2,),
-            in_specs=[pl.BlockSpec((2, tok_count, HEAD_DIM), lambda j, me_ref: (j, me_ref[0], 0)), w_spec(0), w_spec(1), full, full, full,
-                      pl.BlockSpec((1, width), whole)],
-            out_specs=[full, pl.BlockSpec((8, width), whole)],
-            scratch_shapes=[pltpu.VMEM((tok_count, width), F32)]),
-        out_shape=[jax.ShapeDtypeStruct((tok_count, width), BF16), jax.ShapeDtypeStruct((8, width), F32)],
-        compiler_params=params(),
-        cost_estimate=pl.CostEstimate(flops=2 * tok_count * width * groups * HEAD_DIM, bytes_accessed=8 * width * tok_count, transcendentals=0),
-        name="grad_x",
-    )(me, d_q, w_q, w_q, part, x, grad_out, gain_f)
+    )(ht, d_q, d_hid, x, grad_out, gain_f, result, tiles)
 
 
 def solution(mesh):
@@ -756,23 +821,16 @@
     part_rows = P('dp', None)
 
     def local_step(x, grad_out, positions, gain, w_q, w_k, w_v, w_o):
-        tok_count = x.shape[0]
         n_heads = w_q.shape[1] // HEAD_DIM
         heads = n_heads // sp_size
-        me = lax.axis_index('sp')
         gain_f = gain.astype(F32).reshape(1, -1)
         hidden, cos_t, sin_t = gather_h(x, gain_f, positions, sp_size)
         q, k, v, ht, ot, lse, d_out = forward(hidden, w_q, w_k, w_v, cos_t, sin_t, grad_out, heads)
         *grads, ot_all = backward(q, k, v, d_out, w_o, ot, lse, cos_t, sin_t, heads, sp_size)
-        tiles, *gathered = products(ot_all, ht, d_out, *grads, sp_size)
-        dkv_all, dqa_all, dqb_all = [val.reshape(sp_size, -1, val.shape[1]) for val in gathered]
+        tiles, _, _, dqb_all, part, d_hid = products(ot_all, ht, d_out, *grads, x, w_o, w_k, w_v, w_q, sp_size, heads)
         n_kv = sp_size // 2
-        grad_wq, grad_wk, grad_wv, grad_wo = finish(ht, dqb_all, tiles, heads, tiles.shape[1] - 2 * n_kv, n_kv)
-        o_own = lax.dynamic_slice_in_dim(ot_all, me * tok_count, tok_count, axis=1)
-        result = (x.astype(F32) + dot(o_own, w_o, ROWS_ROWS)).astype(BF16)
-        me_arr = me.reshape(1).astype(jnp.int32)
-        part = d_hidden(me_arr, dkv_all, dqa_all, w_k, w_v, w_q, tok_count, heads)
-        grad_x, gg = grad_x_final(me_arr, dqb_all, w_q, part, x, grad_out, gain_f, heads)
+        grad_wq, grad_wk, grad_wv, grad_wo, grad_x, gg, result = finish(
+            ht, dqb_all.reshape(sp_size, -1, HEAD_DIM), tiles, d_hid, x, grad_out, gain_f, part, heads, tiles.shape[1] - 2 * n_kv, n_kv)
         grad_gain = jnp.sum(lax.all_gather(gg, 'sp', axis=0, tiled=True), axis=0)
         return result, grad_x, grad_wq, grad_wk, grad_wv, grad_wo, grad_gain
 

time: 684 us -> 646 us (0.944)
  Pallas kernels: 653 us -> 630 us
  matrix products: 16.2 us -> 0 us
    pallas_call x3 -> x1, Pallas kernels: 223 us -> 195 us  [products(): pl.pallas_call(functools.partial(products_kernel, heads), in_specs=[any_s...]
    dot_general x1 -> x0, matrix products: 16.2 us -> none  [dot(): return lax.dot_general(a, b, dims, preferred_element_type=F32)]
where the time goes in v1:
time: 646 us; the launch traced here: 645 us
  Pallas kernels  630 us (98%)
  blocking collectives  10.2 us (2%)
    pallas_call x1, Pallas kernels, products(): pl.pallas_call(functools.partial(products_kernel, heads), in_specs=[any_s...  195 us
    pallas_call x1, Pallas kernels, backward(): pl.pallas_call(functools.partial(backward_kernel, heads), grid=(n_blocks,...  121 us
    pallas_call x1, Pallas kernels, gather_h(): pl.pallas_call(gather_h_kernel, in_specs=[any_spec, vmem, vmem, vmem], ou...  115 us
    pallas_call x1, Pallas kernels, forward(): pl.pallas_call(functools.partial(forward_kernel, heads), grid=(n_blocks,)...  112 us
    pallas_call x1, Pallas kernels, finish(): pl.pallas_call(functools.partial(finish_kernel, heads, n_o, n_kv), grid=(...  87.1 us

profile of v1, /device:TPU:0, one launch (start us, length us, event | category | flops | bytes accessed | tf_op | source)
XLA Modules:
  0.0 645.1 jit_solution(16957592950187954312)
XLA Ops:
  0.6 0.6 maximum_bitcast_fusion.freq_ref
  1.2 1.3 reshape.26
  2.5 1.3 broadcast_in_dim.4.pos_ref
  3.8 114.5 %gather_h.1 = (bf16[4096,3072]{1,0:T(8,128)(2,1)}, f32[4096,128]{1,0:T(8,128)}, f32[4096,128]{1,0:T(8,128)}) custom-call(bf16[512,3072]{1,0:T(8,128)(2,1)} %x_ref.5, f32[1,3072]{1,0:T(1,128)} %bitcast.5, s32[8,512]{1,0:T(8,128)} %broadcast_in_dim.4.pos_ref, f32[1,128]{1,0:T(1,128)} %maximum_bitcast_fusion.freq_ref), custom_call_target="tpu_custom_call" | custom-call | tf_op jit(solution)/shard_map/gather_h/pallas_call | solution.py:191
  118.3 111.9 %forward.1 = (bf16[4096,384]{1,0:T(8,128)(2,1)}, bf16[4096,128]{1,0:T(8,128)(2,1)}, bf16[4096,128]{1,0:T(8,128)(2,1)}, bf16[3072,4096]{1,0:T(8,128)(2,1)}, bf16[...) custom-call(bf16[4096,3072]{1,0:T(8,128)(2,1)} %get-tuple-element.32.h_ref, ...), custom_call_target="tpu_custom_call" | custom-call | flops 48318382080 | bytes 100663296 | tf_op jit(solution)/shard_map/forward/pallas_call | solution.py:296
  230.3 121.3 %backward.1 = (bf16[4096,256]{1,0:T(8,128)(2,1)}, bf16[4096,256]{1,0:T(8,128)(2,1)}, bf16[4096,128]{1,0:T(8,128)(2,1)}, bf16[3072,4096]{1,0:T(8,128)(2,1)}) custom-call(bf16[4096,384]{1,0:T(8,128)(2,1)} %get-tuple-element.36.q_ref, bf16[4096,128]{1,0:T(8,128)(2,1)} %get-tuple-element.37.k_ref, bf16[4096,128]{1,0:T(8,128)(2,1)} %get-tuple-element.38.v_ref, ...), custom_call_target="tpu_custom_call" | custom-call | flops 82141249536 | bytes 12582912 | tf_op jit(solution)/shard_map/backward/pallas_call | solution.py:420
  351.6 195.5 %products.1 = (f32[2,14,1536,512]{3,2,1,0:T(8,128)}, bf16[32768,256]{1,0:T(8,128)(2,1)}, bf16[32768,256]{1,0:T(8,128)(2,1)}, bf16[32768,128]{1,0:T(8,128)(2,1)},...) custom-call(bf16[3072,4096]{1,0:T(8,128)(2,1)} %get-tuple-element.42.ot_ref, ...), custom_call_target="tpu_custom_call" | custom-call | flops 90194313216 | bytes 88080384 | tf_op jit(solution)/shard_map/products/pallas_call | solution.py:686
  547.1 87.1 %finish.1 = (f32[3072,3072]{1,0:T(8,128)}, f32[3072,1024]{1,0:T(8,128)}, f32[3072,1024]{1,0:T(8,128)}, f32[3072,3072]{1,0:T(8,128)}, bf16[512,3072]{1,0:T(8,128)...) custom-call(bf16[3072,4096]{1,0:T(8,128)(2,1)} %get-tuple-element.35.ht_ref, bf16[8,4096,128]{2,1,0:T(8,128)(2,1)} %bitcast.4, ...), custom_call_target="tpu_custom_call" | custom-call | flops 25769803776 | bytes 25165824 | tf_op jit(solution)/shard_map/finish/pallas_call | solution.py:798
  634.2 10.2 %all_gather.3 = f32[64,3072]{1,0:T(8,128)S(1)} all-gather(f32[8,3072]{1,0:T(8,128)} %get-tuple-element.56), channel_id=1, replica_groups=mesh['dp'=2,'sp'=8] {'sp'}, dimensions={0}, use_global_device_ids=true | all-gather | bytes 884736 | tf_op jit(solution)/shard_map/all_gather | solution.py:834
  644.4 0.7 reduce_sum.9
  (1 shorter events, 0.0 us)

commit v2 on v1

--- a/solution.py
+++ b/solution.py
@@ -16,8 +16,8 @@
 BLK = 512
 CHUNKS = 4
 FWD_MIDDLE, BWD_MIDDLE, BWD_LATE = 5, 4, 5
-MROWS = 1024
-RING = 3
+MROWS = 768
+RING = 2
 ROW_STEPS = 8
 F32 = jnp.float32
 BF16 = jnp.bfloat16
@@ -49,6 +49,10 @@
         for peer in peers:
             pl.semaphore_signal(barrier, inc=1, device_id={'sp': peer}, device_id_type=pl.DeviceIdType.MESH)
         pl.semaphore_wait(barrier, len(peers))
+
+    def across(self, r):
+        core, col, row = lax.rem(self.me, 2), lax.rem(self.me // 2, 2), self.me // 4
+        return (self.me + lax.rem(r, 2) * (1 - 2 * core) + lax.rem(r // 2, 2) * (2 - 4 * col) + (r // 4) * (4 - 8 * row))
 
     def others(self):
         flip = lambda dev: dev + 1 - 2 * lax.rem(dev, 2)
@@ -113,18 +117,28 @@
             self.first(chunk, 1).wait_recv()
         self.share(1).start()
 
-    def end(self):
+    def end_near(self):
+        for chunk in range(CHUNKS):
+            self.first(chunk, 2).wait_recv()
+        for kind in range(2):
+            self.share(kind).wait_recv()
+
+    def end_far(self):
         for chunk in (0, 2, 1, 3):
             self.onward(chunk).wait_recv()
             self.share_diag(chunk).start()
-        sent = [self.first(chunk, kind) for chunk in range(CHUNKS) for kind in range(3)]
-        for copy in sent:
-            copy.wait_send()
         for chunk in range(CHUNKS):
-            self.first(chunk, 2).wait_recv()
+            for kind in range(3):
+                self.first(chunk, kind).wait_send()
             self.onward(chunk).wait_send()
-        for copy in [self.share(0), self.share(1)] + [self.share_diag(chunk) for chunk in range(CHUNKS)]:
-            copy.wait()
+        for kind in range(2):
+            self.share(kind).wait_send()
+        for chunk in range(CHUNKS):
+            self.share_diag(chunk).wait()
+
+    def end(self):
+        self.end_near()
+        self.end_far()
 
 
 SEMS = pltpu.SemaphoreType.DMA((2, Gather.COPIES))
@@ -449,13 +463,14 @@
     chunk = seq_len // CHUNKS
     n_cols = d_kv_ref.shape[1]
     n_o, n_all = width // (2 * n_cols), tiles.shape[1]
-    n_kv = (n_all - n_o) // 2
+    n_qa = (n_all - n_o) * 2 // 3
+    n_oa = n_o + n_qa
 
     def gather_of(src, dst, sems):
         return Gather(near, lambda c: src.at[pl.ds(c * chunk, chunk), :], dst, seq_len, sems)
 
-    local = (d_kv_ref, d_qa_ref, d_qb_ref)
-    gathers = [gather_of(d_kv_ref, kv_all, kv_sems), gather_of(d_qa_ref, qa_all, qa_sems), gather_of(d_qb_ref, qb_all, qb_sems)]
+    local = (d_qa_ref, d_qb_ref, d_kv_ref)
+    gathers = [gather_of(d_qa_ref, qa_all, qa_sems), gather_of(d_qb_ref, qb_all, qb_sems), gather_of(d_kv_ref, kv_all, kv_sems)]
 
     def stage_in(n):
         return pltpu.make_async_copy(local[n], stage.at[:, pl.ds(0, local[n].shape[1])], stage_sems.at[0])
@@ -477,20 +492,23 @@
     def a_load(ref):
         return pltpu.make_async_copy(ref.at[own_rows, :], a_buf, a_sem)
 
-    def b_load(source, p, slot, g):
+    def b_loads(source, p, slot, g):
         if source is dy_ref:
-            src = dy_ref.at[:, pl.ds(pl.multiple_of((2 * p + g) * n_cols, n_cols), n_cols)]
+            srcs = [dy_ref.at[:, pl.ds(pl.multiple_of((2 * p + g) * n_cols, n_cols), n_cols)]]
         else:
-            src = source.at[pl.ds(pl.multiple_of((2 * p + g) * seq_len, seq_len), seq_len), :]
-        return pltpu.make_async_copy(src, b_buf.at[slot, :, pl.ds(g * n_cols, n_cols)], b_sems.at[slot, g])
+            per = n_cols // source.shape[1]
+            srcs = [source.at[pl.ds(pl.multiple_of(((2 * p + g) * per + n) * seq_len, seq_len), seq_len), :] for n in range(per)]
+        return [pltpu.make_async_copy(src, b_buf.at[slot, :, pl.ds(g * n_cols + n * src.shape[1], src.shape[1])], b_sems.at[slot, g])
+                for n, src in enumerate(srcs)]
 
     def start_b(step):
         slot = lax.rem(step, 2)
-        for source, low, high in ((dy_ref, 0, n_o), (kv_all, n_o, n_o + n_kv), (qa_all, n_o + n_kv, n_all)):
+        for source, low, high in ((dy_ref, 0, n_o), (qa_all, n_o, n_oa), (qb_all, n_oa, n_all)):
             @pl.when(jnp.logical_and(step >= low, step < high))
             def _():
                 for g in range(2):
-                    b_load(source, step - low, slot, g).start()
+                    for load in b_loads(source, step - low, slot, g):
+                        load.start()
 
     def keep(step):
         return pltpu.make_async_copy(tile.at[lax.rem(step, 2)], tiles.at[core, step], t_sems.at[lax.rem(step, 2)])
@@ -530,54 +548,54 @@
         res_store.start()
 
     def hidden_parts(kind):
-        per = 2 if kind == 2 else 1
-        count = own.shape[0] // per
-
-        def own_load(j, g):
-            source = (kv_all, qa_all, qb_all)[kind]
-            device, col = (2 * j + g, 0) if kind == 2 else (j, g * HEAD_DIM)
+        count = own.shape[0] // (2 if kind == 1 else 1)
+
+        def own_load(r, g):
+            source = (qa_all, qb_all, kv_all)[kind]
+            device, col = (2 * r + g, 0) if kind == 1 else (near.across(r), g * HEAD_DIM)
             at = pl.ds(pl.multiple_of(device * seq_len + near.me * rows, rows), rows)
-            return pltpu.make_async_copy(source.at[at, pl.ds(col, HEAD_DIM)], own.at[j, :, pl.ds(g * HEAD_DIM, HEAD_DIM)], own_sems.at[j, g])
-
-        def w_load(j, g):
-            source = (wk_ref, wv_ref)[g] if kind == 0 else wq_ref
-            col = j if kind == 0 else heads * j + g if kind == 1 else heads * (2 * j + g + 1) - 1
-            slot = lax.rem(j, 2)
+            return pltpu.make_async_copy(source.at[at, pl.ds(col, HEAD_DIM)], own.at[r, :, pl.ds(g * HEAD_DIM, HEAD_DIM)], own_sems.at[r, g])
+
+        def w_load(r, g):
+            source = (wk_ref, wv_ref)[g] if kind == 2 else wq_ref
+            col = near.across(r) if kind == 2 else heads * near.across(r) + g if kind == 0 else heads * (2 * r + g + 1) - 1
+            slot = lax.rem(r, 2)
             return pltpu.make_async_copy(source.at[:, pl.ds(pl.multiple_of(col * HEAD_DIM, HEAD_DIM), HEAD_DIM)],
                                          w_v.at[slot, :, pl.ds(g * HEAD_DIM, HEAD_DIM)], w_sems.at[slot, g])
 
         return count, own_load, w_load
 
-    def hidden_start(kind):
+    def hidden_start(kind, low=0, high=None):
         count, own_load, w_load = hidden_parts(kind)
         for g in range(2):
-            w_load(jnp.int32(0), g).start()
-
-            @pl.loop(0, count)
-            def _(j):
-                own_load(j, g).start()
-
-    def hidden_add(kind):
+            if low == 0:
+                w_load(jnp.int32(0), g).start()
+
+            @pl.loop(low, high or count)
+            def _(r):
+                own_load(r, g).start()
+
+    def hidden_add(kind, low=0, high=None):
         count, own_load, w_load = hidden_parts(kind)
 
-        @pl.loop(0, count)
-        def _(j):
+        @pl.loop(low, high or count)
+        def _(r):
             for g in range(2):
-                w_load(j, g).wait()
-                own_load(j, g).wait()
-
-            @pl.when(j + 1 < count)
+                w_load(r, g).wait()
+                own_load(r, g).wait()
+
+            @pl.when(r + 1 < count)
             def _():
                 for g in range(2):
-                    w_load(j + 1, g).start()
-
-            prod = dot(own[j], w_v[lax.rem(j, 2)], COLS_COLS)
+                    w_load(r + 1, g).start()
+
+            prod = dot(own[r], w_v[lax.rem(r, 2)], COLS_COLS)
             if kind == 0:
-                @pl.when(j == 0)
+                @pl.when(r == 0)
                 def _():
                     acc[...] = prod
 
-                @pl.when(j > 0)
+                @pl.when(r > 0)
                 def _():
                     acc[...] += prod
             else:
@@ -597,9 +615,9 @@
     def _(step):
         slot = lax.rem(step, 2)
         for g in range(2):
-            b_load(dy_ref, 0, slot, g).wait()
-
-        @pl.when(jnp.logical_and(step != n_o - 1, step != n_o + n_kv - 1))
+            b_loads(dy_ref, 0, slot, g)[0].wait()
+
+        @pl.when(jnp.logical_and(step != n_o - 1, step != n_oa - 1))
         def _():
             start_b(step + 1)
 
@@ -634,37 +652,41 @@
             start_b(step + 1)
             hidden_start(0)
 
-        @pl.when(step == n_o + n_kv - 1)
+        @pl.when(step == n_oa - 3)
         def _():
+            copy_own(1)
             gathers[1].middle()
-            copy_own(1)
-            hidden_add(0)
+
+        @pl.when(step == n_oa - 2)
+        def _():
             gathers[1].late()
             for c in range(CHUNKS):
                 gathers[2].start(c)
             stage_out(1).wait()
             stage_in(2).start()
+
+        @pl.when(step == n_oa - 1)
+        def _():
             gathers[1].end()
             start_b(step + 1)
+            hidden_add(0)
             hidden_start(1)
 
-        @pl.when(step == n_all - 3)
-        def _():
-            copy_own(2)
-            gathers[2].middle()
-
-        @pl.when(step == n_all - 2)
-        def _():
-            gathers[2].late()
-
     hidden_add(1)
+    copy_own(2)
+    gathers[2].middle()
+    gathers[2].late()
     stage_out(2).wait()
-    gathers[2].end()
-    hidden_start(2)
+    gathers[2].end_near()
+    near_count = own.shape[0] * 3 // 4
+    hidden_start(2, 0, near_count)
     for step in (n_all - 2, n_all - 1):
         keep(step).wait()
         give(step).wait_send()
-    hidden_add(2)
+    hidden_add(2, 0, near_count)
+    gathers[2].end_far()
+    hidden_start(2, near_count)
+    hidden_add(2, near_count)
     hid_store.start()
 
     @pl.loop(0, n_all)
@@ -679,7 +701,7 @@
     width, seq_len = ht.shape
     half = width // 2
     cols = 2 * d_kv.shape[1]
-    n_all = width // cols + 2 * sp_size * d_kv.shape[1] // cols
+    n_all = width // cols + sp_size * (d_qa.shape[1] + d_qb.shape[1]) // cols
     any_spec = pl.BlockSpec(memory_space=pl.ANY)
     dma = pltpu.SemaphoreType.DMA
     gathered = [jax.ShapeDtypeStruct((sp_size * seq_len, d.shape[1]), BF16) for d in (d_kv, d_qa, d_qb)]
@@ -700,12 +722,9 @@
     )(ot_all, ht, d_out, d_kv, d_qa, d_qb, x, w_o, w_k, w_v, w_q)
 
 
-def finish_kernel(heads, n_o, n_kv, ht_ref, d_ref, hid_ref, x_ref, dy_ref, gain_ref, part_ref, tiles,
-                  wq_ref, wk_ref, wv_ref, wo_ref, gx_ref, gg_ref, res_ref, tile, sems, ring, ring_sems):
-    n_cols = d_ref.shape[2]
-    n_j = pl.num_programs(1)
-    step = pl.program_id(0) * n_j + pl.program_id(1)
-    slot = lax.rem(step, 2)
+def finish_kernel(heads, n_o, n_qa, ht_ref, d_ref, hid_ref, x_ref, dy_ref, gain_ref, part_ref, tiles,
+                  wk_ref, wv_ref, wq_ref, wo_ref, gx_ref, gg_ref, res_ref, ring, ring_sems):
+    step = pl.program_id(0) * pl.num_programs(1) + pl.program_id(1)
     half = ring.shape[2]
     every = [(c, t) for t in range(tiles.shape[1]) for c in range(2)]
     groups = [every[g:g + RING] for g in range(0, len(every), RING)]
@@ -715,10 +734,9 @@
         cols = ring.shape[3]
         if t < n_o:
             return [(0, cols, wo_ref.at[rows, pl.ds(t * cols, cols)])]
-        if t < n_o + n_kv:
-            return [(n * HEAD_DIM, HEAD_DIM, (wk_ref, wv_ref)[n % 2].at[rows, pl.ds(((t - n_o) * 2 + n // 2) * HEAD_DIM, HEAD_DIM)]) for n in range(4)]
-        wide = (heads - 1) * HEAD_DIM
-        return [(n * wide, wide, wq_ref.at[rows, pl.ds(((t - n_o - n_kv) * 2 + n) * heads * HEAD_DIM, wide)]) for n in range(2)]
+        wide, first, t = ((heads - 1) * HEAD_DIM, 0, t - n_o) if t < n_o + n_qa else (HEAD_DIM, heads - 1, t - n_o - n_qa)
+        per = cols // wide
+        return [(n * wide, wide, wq_ref.at[rows, pl.ds(((t * per + n) * heads + first) * HEAD_DIM, wide)]) for n in range(per)]
 
     def ins(g):
         return [pltpu.make_async_copy(tiles.at[c, t], ring.at[g % 2, n], ring_sems.at[0, g % 2, n, 0]) for n, (c, t) in enumerate(groups[g])]
@@ -742,24 +760,10 @@
                 for copy in ins(g):
                     copy.start()
 
-    def copies(step, slot):
-        rows = pl.ds(pl.multiple_of((step // n_j) * MROWS, MROWS), MROWS)
-        out = []
-        for g in range(2):
-            col = ((lax.rem(step, n_j) * 2 + g + 1) * heads - 1) * HEAD_DIM
-            out.append(pltpu.make_async_copy(tile.at[slot, :, pl.ds(g * n_cols, n_cols)],
-                                             wq_ref.at[rows, pl.ds(pl.multiple_of(col, HEAD_DIM), n_cols)], sems.at[slot, g]))
-        return out
-
-    @pl.when(step >= 2)
-    def _():
-        for copy in copies(step - 2, slot):
-            copy.wait()
-
+    ht = ht_ref[...]
     pair = 2 * pl.program_id(1)
-    tile[slot] = dot(ht_ref[...], lanes(d_ref[pair], d_ref[pair + 1]))
-    for copy in copies(step, slot):
-        copy.start()
+    wk_ref[...] = dot(ht, lanes(d_ref[pair, :, :HEAD_DIM], d_ref[pair + 1, :, :HEAD_DIM]))
+    wv_ref[...] = dot(ht, lanes(d_ref[pair, :, HEAD_DIM:], d_ref[pair + 1, :, HEAD_DIM:]))
 
     @pl.when(step == 0)
     def _():
@@ -779,38 +783,33 @@
         gx_ref[...] = (dy_ref[...].astype(F32) + d_x).astype(BF16)
         res_ref[...] = part_ref[...]
 
-    @pl.when(step == pl.num_programs(0) * n_j - 1)
-    def _():
-        for copy in copies(step - 1, 1 - slot) + copies(step, slot):
-            copy.wait()
-
-
-def finish(ht, d_q, tiles, d_hid, x, grad_out, gain_f, result, heads, n_o, n_kv):
+
+def finish(ht, d_kv, tiles, d_hid, x, grad_out, gain_f, result, heads, n_o, n_qa):
     width, seq_len = ht.shape
-    groups, _, n_cols = d_q.shape
+    groups = d_kv.shape[0]
     n_j = groups // 2
     steps = (width // MROWS) * n_j
     assert -(-2 * tiles.shape[1] // RING) + 2 <= steps
     any_spec = pl.BlockSpec(memory_space=pl.ANY)
     rows = pl.BlockSpec((x.shape[0] // ROW_STEPS, width), lambda m, j: (jnp.minimum(m * n_j + j, ROW_STEPS - 1), 0))
     whole = lambda *shape: pl.BlockSpec(shape, lambda m, j: (0,) * len(shape))
+    kv_out = pl.BlockSpec((MROWS, 2 * HEAD_DIM), lambda m, j: (m, j))
     out = lambda cols: jax.ShapeDtypeStruct((width, cols), F32)
     return pl.pallas_call(
-        functools.partial(finish_kernel, heads, n_o, n_kv),
+        functools.partial(finish_kernel, heads, n_o, n_qa),
         grid=(width // MROWS, n_j),
         in_specs=[pl.BlockSpec((MROWS, seq_len), lambda m, j: (m, 0)),
-                  pl.BlockSpec(d_q.shape, lambda m, j: (0, 0, 0), pipeline_mode=pl.Buffered(1)),
+                  pl.BlockSpec(d_kv.shape, lambda m, j: (0, 0, 0), pipeline_mode=pl.Buffered(1)),
                   rows, rows, rows, whole(1, width), rows, any_spec],
-        out_specs=[any_spec] * 4 + [rows, whole(8, width), rows],
-        out_shape=[out(groups * heads * HEAD_DIM), out(groups * HEAD_DIM), out(groups * HEAD_DIM),
+        out_specs=[kv_out, kv_out, any_spec, any_spec, rows, whole(8, width), rows],
+        out_shape=[out(groups * HEAD_DIM), out(groups * HEAD_DIM), out(groups * heads * HEAD_DIM),
                    jax.ShapeDtypeStruct((groups * heads * HEAD_DIM, width), F32), jax.ShapeDtypeStruct(x.shape, BF16),
                    jax.ShapeDtypeStruct((8, width), F32), jax.ShapeDtypeStruct(x.shape, BF16)],
-        scratch_shapes=[pltpu.VMEM((2, MROWS, 2 * n_cols), F32), pltpu.SemaphoreType.DMA((2, 2)), pltpu.VMEM((2, RING) + tiles.shape[2:], F32),
-                        pltpu.SemaphoreType.DMA((2, 2, RING, 4))],
+        scratch_shapes=[pltpu.VMEM((2, RING) + tiles.shape[2:], F32), pltpu.SemaphoreType.DMA((2, 2, RING, 4))],
         compiler_params=params(2),
-        cost_estimate=pl.CostEstimate(flops=2 * width * seq_len * groups * n_cols, bytes_accessed=2 * width * seq_len, transcendentals=0),
+        cost_estimate=pl.CostEstimate(flops=4 * width * seq_len * groups * HEAD_DIM, bytes_accessed=2 * width * seq_len, transcendentals=0),
         name="finish",
-    )(ht, d_q, d_hid, x, grad_out, gain_f, result, tiles)
+    )(ht, d_kv, d_hid, x, grad_out, gain_f, result, tiles)
 
 
 def solution(mesh):
@@ -827,10 +826,10 @@
         hidden, cos_t, sin_t = gather_h(x, gain_f, positions, sp_size)
         q, k, v, ht, ot, lse, d_out = forward(hidden, w_q, w_k, w_v, cos_t, sin_t, grad_out, heads)
         *grads, ot_all = backward(q, k, v, d_out, w_o, ot, lse, cos_t, sin_t, heads, sp_size)
-        tiles, _, _, dqb_all, part, d_hid = products(ot_all, ht, d_out, *grads, x, w_o, w_k, w_v, w_q, sp_size, heads)
-        n_kv = sp_size // 2
-        grad_wq, grad_wk, grad_wv, grad_wo, grad_x, gg, result = finish(
-            ht, dqb_all.reshape(sp_size, -1, HEAD_DIM), tiles, d_hid, x, grad_out, gain_f, part, heads, tiles.shape[1] - 2 * n_kv, n_kv)
+        tiles, kv_all, _, _, part, d_hid = products(ot_all, ht, d_out, *grads, x, w_o, w_k, w_v, w_q, sp_size, heads)
+        n_o = x.shape[1] // tiles.shape[3]
+        grad_wk, grad_wv, grad_wq, grad_wo, grad_x, gg, result = finish(
+            ht, kv_all.reshape(sp_size, -1, 2 * HEAD_DIM), tiles, d_hid, x, grad_out, gain_f, part, heads, n_o, (tiles.shape[1] - n_o) * 2 // 3)
         grad_gain = jnp.sum(lax.all_gather(gg, 'sp', axis=0, tiled=True), axis=0)
         return result, grad_x, grad_wq, grad_wk, grad_wv, grad_wo, grad_gain
 

time: 646 us -> 641 us (level)
    pallas_call x1, Pallas kernels: 195 us -> 182 us  [products(): pl.pallas_call(functools.partial(products_kernel, heads), in_specs=[any_s...]
    pallas_call x1, Pallas kernels: 87.1 us -> 95.9 us  [finish(): pl.pallas_call(functools.partial(finish_kernel, heads, n_o, n_qa), grid=(...]
where the time goes in v2:
time: 641 us
  Pallas kernels  626 us (98%)
  blocking collectives  10.1 us (2%)
    pallas_call x1, Pallas kernels, products(): pl.pallas_call(functools.partial(products_kernel, heads), in_specs=[any_s...  182 us
    pallas_call x1, Pallas kernels, backward(): pl.pallas_call(functools.partial(backward_kernel, heads), grid=(n_blocks,...  121 us
    pallas_call x1, Pallas kernels, gather_h(): pl.pallas_call(gather_h_kernel, in_specs=[any_spec, vmem, vmem, vmem], ou...  115 us
    pallas_call x1, Pallas kernels, forward(): pl.pallas_call(functools.partial(forward_kernel, heads), grid=(n_blocks,)...  112 us
    pallas_call x1, Pallas kernels, finish(): pl.pallas_call(functools.partial(finish_kernel, heads, n_o, n_qa), grid=(...  95.9 us

profile of v2, /device:TPU:0, one launch (start us, length us, event | category | flops | bytes accessed | tf_op | source)
XLA Modules:
  0.0 640.6 jit_solution(2011568385212698912)
XLA Ops:
  0.6 0.6 maximum_bitcast_fusion.freq_ref
  1.2 1.3 reshape.26
  2.5 1.3 broadcast_in_dim.4.pos_ref
  3.8 114.5 %gather_h.1 = (bf16[4096,3072]{1,0:T(8,128)(2,1)}, f32[4096,128]{1,0:T(8,128)}, f32[4096,128]{1,0:T(8,128)}) custom-call(bf16[512,3072]{1,0:T(8,128)(2,1)} %x_ref.5, f32[1,3072]{1,0:T(1,128)} %bitcast.4, s32[8,512]{1,0:T(8,128)} %broadcast_in_dim.4.pos_ref, f32[1,128]{1,0:T(1,128)} %maximum_bitcast_fusion.freq_ref), custom_call_target="tpu_custom_call" | custom-call | tf_op jit(solution)/shard_map/gather_h/pallas_call | solution.py:205
  118.3 111.9 %forward.1 = (bf16[4096,384]{1,0:T(8,128)(2,1)}, bf16[4096,128]{1,0:T(8,128)(2,1)}, bf16[4096,128]{1,0:T(8,128)(2,1)}, bf16[3072,4096]{1,0:T(8,128)(2,1)}, bf16[...) custom-call(bf16[4096,3072]{1,0:T(8,128)(2,1)} %get-tuple-element.32.h_ref, ...), custom_call_target="tpu_custom_call" | custom-call | flops 48318382080 | bytes 100663296 | tf_op jit(solution)/shard_map/forward/pallas_call | solution.py:310
  230.3 121.3 %backward.1 = (bf16[4096,256]{1,0:T(8,128)(2,1)}, bf16[4096,256]{1,0:T(8,128)(2,1)}, bf16[4096,128]{1,0:T(8,128)(2,1)}, bf16[3072,4096]{1,0:T(8,128)(2,1)}) custom-call(bf16[4096,384]{1,0:T(8,128)(2,1)} %get-tuple-element.36.q_ref, bf16[4096,128]{1,0:T(8,128)(2,1)} %get-tuple-element.37.k_ref, bf16[4096,128]{1,0:T(8,128)(2,1)} %get-tuple-element.38.v_ref, ...), custom_call_target="tpu_custom_call" | custom-call | flops 82141249536 | bytes 12582912 | tf_op jit(solution)/shard_map/backward/pallas_call | solution.py:434
  351.6 182.4 %products.1 = (f32[2,12,1536,512]{3,2,1,0:T(8,128)}, bf16[32768,256]{1,0:T(8,128)(2,1)}, bf16[32768,256]{1,0:T(8,128)(2,1)}, bf16[32768,128]{1,0:T(8,128)(2,1)},...) custom-call(bf16[3072,4096]{1,0:T(8,128)(2,1)} %get-tuple-element.42.ot_ref, ...), custom_call_target="tpu_custom_call" | custom-call | flops 77309411328 | bytes 75497472 | tf_op jit(solution)/shard_map/products/pallas_call | solution.py:708
  534.0 95.9 %finish.1 = (f32[3072,1024]{1,0:T(8,128)}, f32[3072,1024]{1,0:T(8,128)}, f32[3072,3072]{1,0:T(8,128)}, f32[3072,3072]{1,0:T(8,128)}, bf16[512,3072]{1,0:T(8,128)...) custom-call(bf16[3072,4096]{1,0:T(8,128)(2,1)} %get-tuple-element.35.ht_ref, bf16[8,4096,256]{2,1,0:T(8,128)(2,1)} %bitcast.6, ...), custom_call_target="tpu_custom_call" | custom-call | flops 51539607552 | bytes 25165824 | tf_op jit(solution)/shard_map/finish/pallas_call | solution.py:798
  629.9 10.1 %all_gather.3 = f32[64,3072]{1,0:T(8,128)S(1)} all-gather(f32[8,3072]{1,0:T(8,128)} %get-tuple-element.56), channel_id=1, replica_groups=mesh['dp'=2,'sp'=8] {'sp'}, dimensions={0}, use_global_device_ids=true | all-gather | bytes 884736 | tf_op jit(solution)/shard_map/all_gather | solution.py:833
  640.0 0.7 reduce_sum.9
  (1 shorter events, 0.0 us)

commit v3 on v2

--- a/solution.py
+++ b/solution.py
@@ -2,6 +2,7 @@
 
 import jax
 import jax.numpy as jnp
+import numpy as np
 from jax import lax
 from jax.experimental import pallas as pl
 from jax.experimental.pallas import tpu as pltpu
@@ -15,9 +16,10 @@
 LOG2E = 1.4426950408889634
 BLK = 512
 CHUNKS = 4
-FWD_MIDDLE, BWD_MIDDLE, BWD_LATE = 5, 4, 5
-MROWS = 768
+FWD_MIDDLE, FWD_LATE, BWD_MIDDLE, BWD_LATE = 5, 6, 5, 6
+MROWS = 384
 RING = 2
+DEPTH = 5
 ROW_STEPS = 8
 F32 = jnp.float32
 BF16 = jnp.bfloat16
@@ -144,26 +146,41 @@
 SEMS = pltpu.SemaphoreType.DMA((2, Gather.COPIES))
 
 
-def comm_params(collective_id):
-    return pltpu.CompilerParams(dimension_semantics=("arbitrary",), vmem_limit_bytes=VMEM_LIMIT, collective_id=collective_id,
-                                has_side_effects=True)
-
-
-def gather_h_kernel(x_ref, gain_ref, pos_ref, freq_ref, h_all, cos_ref, sin_ref, x_v, h_v, pos_all, in_sems, out_sem, pos_sems, sems):
+def masked(scores):
+    key = lax.broadcasted_iota(jnp.int32, scores.shape, 0)
+    query = lax.broadcasted_iota(jnp.int32, scores.shape, 1)
+    return jnp.where(key <= query, scores, NEG_LARGE)
+
+
+def unrotate(val, cos_t, sin_t):
+    return (val * cos_t - pltpu.roll(val, HALF, 1) * sin_t).astype(BF16)
+
+
+def attention_kernel(heads, x_ref, gain_ref, pos_ref, freq_ref, dy_ref, wq_ref, wk_ref, wv_ref, wo_ref,
+                     h_all, dy_all, o_all, ht_ref, dkv_ref, dq_a_ref, dq_b_ref,
+                     x_v, h_v, x_sems, own_sems, pos_all, pos_sems, cos_s, sin_s, w_v, wo_v, w_sems, blk, blk_sems, ht_v, ht_sems,
+                     q_s, k_s, v_s, vt, kt, ot_s, lse_s, acc, do_s, dk_acc, dv_acc, dq_v, dq_sems, dkv_v, h_sems, dy_sems, o_sems):
     near = Neighbours()
-    rows = x_ref.shape[0]
+    rows, width = x_ref.shape
+    n_blocks = k_s.shape[0]
+    q_cols = heads * HEAD_DIM
     size = rows // CHUNKS
-    part = lambda ref, chunk: ref.at[pl.ds(chunk * size, size), :]
-    gather = Gather(near, lambda chunk: part(h_v, chunk), h_all, rows, sems)
-    loads = [pltpu.make_async_copy(part(x_ref, chunk), part(x_v, chunk), in_sems.at[chunk]) for chunk in range(CHUNKS)]
+    qk_scale = HEAD_DIM ** -0.5
+    to_log2 = qk_scale * LOG2E
+    cols = [slice(a * HEAD_DIM, (a + 1) * HEAD_DIM) for a in range(heads)]
+    part = lambda ref, chunk, count=size: ref.at[pl.ds(chunk * count, count), :]
+    gather_h = Gather(near, lambda chunk: part(h_v, chunk), h_all, rows, h_sems)
+    gather_dy = Gather(near, lambda chunk: part(dy_ref, chunk), dy_all, rows, dy_sems)
+    gather_o = Gather(near, lambda chunk: part(ot_s, chunk, q_cols // CHUNKS), o_all, q_cols, o_sems)
+
+    loads = [pltpu.make_async_copy(part(x_ref, chunk), part(x_v, chunk), x_sems.at[chunk]) for chunk in range(CHUNKS)]
     for load in loads:
         load.start()
     others = near.others()
     near.meet(others)
-    pos_all[near.me] = pos_ref[...]
-    positions = [send(pos_ref, pos_all.at[near.me], pos_sems, r, peer) for r, peer in enumerate(others)]
-    for copy in positions:
-        copy.start()
+    pos_all[near.me] = jnp.broadcast_to(pos_ref[...], pos_all.shape[1:])
+    positions = [send(pos_ref, pos_all.at[near.me, pl.ds(0, 1), :], pos_sems, r, peer) for r, peer in enumerate(others)]
+    gain = gain_ref[...].astype(F32)
     for chunk in range(CHUNKS):
         loads[chunk].wait()
 
@@ -172,99 +189,50 @@
             at = pl.ds(pl.multiple_of(chunk * size + r * 32, 32), 32)
             x_f = x_v[at, :].astype(F32)
             normed = x_f * lax.rsqrt(jnp.mean(x_f * x_f, axis=-1, keepdims=True) + NORM_EPS)
-            h_v[at, :] = (normed * gain_ref[...]).astype(BF16)
-
-        gather.start(chunk)
-    own = pltpu.make_async_copy(h_v, gather.block(near.me, 0, CHUNKS), out_sem)
-    own.start()
+            h_v[at, :] = (normed * gain).astype(BF16)
+
+        gather_h.start(chunk)
+    for copy in positions:
+        copy.start()
+    own_h = pltpu.make_async_copy(h_v, gather_h.block(near.me, 0, CHUNKS), own_sems.at[0])
+    own_h.start()
+    w_loads, col = [], 0
+    for n, (ref, count) in enumerate(((wq_ref, q_cols), (wk_ref, HEAD_DIM), (wv_ref, HEAD_DIM))):
+        at = pl.ds(pl.multiple_of(near.me * count, HEAD_DIM), count)
+        w_loads.append(pltpu.make_async_copy(ref.at[:, at], w_v.at[:, pl.ds(col, count)], w_sems.at[n]))
+        col += count
+    w_loads.append(pltpu.make_async_copy(wo_ref.at[pl.ds(pl.multiple_of(near.me * q_cols, q_cols), q_cols), :], wo_v, w_sems.at[3]))
+    stage_in = pltpu.make_async_copy(dy_ref, x_v, own_sems.at[1])
+    stage_out = pltpu.make_async_copy(x_v, gather_dy.block(near.me, 0, CHUNKS), own_sems.at[2])
+    for load in w_loads + [stage_in]:
+        load.start()
     for copy in positions:
         copy.wait()
     sign = jnp.where(lax.broadcasted_iota(jnp.int32, (1, HEAD_DIM), 1) < HALF, -1.0, 1.0)
 
-    @pl.loop(0, pos_all.shape[0])
+    @pl.loop(0, n_blocks)
     def _(b):
-        at = pl.ds(pl.multiple_of(b * rows, rows), rows)
         pos = jnp.broadcast_to(pos_all[b, 0:1, :].astype(F32), (HEAD_DIM, rows)).T
         angles = pos * freq_ref[...]
-        cos_ref[at, :] = jnp.cos(angles)
-        sin_ref[at, :] = jnp.sin(angles) * sign
-
-    gather.middle()
-    gather.late()
-    own.wait()
-    gather.end()
-
-
-def gather_h(x, gain_f, positions, sp_size):
-    rows, width = x.shape
-    any_spec = pl.BlockSpec(memory_space=pl.ANY)
-    vmem = pl.BlockSpec(memory_space=pltpu.VMEM)
-    inv_freq = ROPE_THETA ** (-jnp.arange(0, HEAD_DIM, 2).astype(F32) / HEAD_DIM)
-    freq = jnp.concatenate([inv_freq, inv_freq])[None, :]
-    table = jax.ShapeDtypeStruct((rows * sp_size, HEAD_DIM), F32)
-    return pl.pallas_call(
-        gather_h_kernel,
-        in_specs=[any_spec, vmem, vmem, vmem],
-        out_specs=[any_spec, vmem, vmem],
-        out_shape=[jax.ShapeDtypeStruct((rows * sp_size, width), BF16), table, table],
-        scratch_shapes=[pltpu.VMEM((rows, width), BF16), pltpu.VMEM((rows, width), BF16), pltpu.VMEM((sp_size, 8, rows), jnp.int32),
-                        pltpu.SemaphoreType.DMA((CHUNKS,)), pltpu.SemaphoreType.DMA, pltpu.SemaphoreType.DMA((2, 7)), SEMS],
-        compiler_params=pltpu.CompilerParams(vmem_limit_bytes=VMEM_LIMIT, collective_id=0, has_side_effects=True),
-        name="gather_h",
-    )(x, gain_f, jnp.broadcast_to(positions[None, :], (8, rows)), freq)
-
-
-def masked(scores):
-    key = lax.broadcasted_iota(jnp.int32, scores.shape, 0)
-    query = lax.broadcasted_iota(jnp.int32, scores.shape, 1)
-    return jnp.where(key <= query, scores, NEG_LARGE)
-
-
-def forward_kernel(heads, h_ref, wq_ref, wk_ref, wv_ref, cos_ref, sin_ref, dy_ref, q_ref, k_ref, v_ref, ht_ref, o_ref, lse_ref, dy_all,
-                   w_v, w_sems, k_s, vt, acc, stage, stage_sems, sems):
-    i = pl.program_id(0)
-    near = Neighbours()
-    rows = dy_ref.shape[0]
-    size = rows // CHUNKS
-    gather = Gather(near, lambda chunk: dy_ref.at[pl.ds(chunk * size, size), :], dy_all, rows, sems)
-    stage_in = pltpu.make_async_copy(dy_ref, stage, stage_sems.at[0])
-    stage_out = pltpu.make_async_copy(stage, gather.block(near.me, 0, CHUNKS), stage_sems.at[1])
-    to_log2 = HEAD_DIM ** -0.5 * LOG2E
-    q_cols = heads * HEAD_DIM
-
-    @pl.when(i == 0)
-    def _():
-        loads, col = [], 0
-        for n, (ref, count) in enumerate(((wq_ref, q_cols), (wk_ref, HEAD_DIM), (wv_ref, HEAD_DIM))):
-            at = pl.ds(pl.multiple_of(near.me * count, HEAD_DIM), count)
-            loads.append(pltpu.make_async_copy(ref.at[:, at], w_v.at[:, pl.ds(col, count)], w_sems.at[n]))
-            col += count
-        for load in loads:
-            load.start()
-        gather.begin()
-        stage_in.start()
-        for load in loads:
-            load.wait()
-
-    ht_ref[...] = h_ref[...].T
-    prod = dot(h_ref[...], w_v[...])
-    cos_t, sin_t = cos_ref[...], sin_ref[...]
-    for a in range(heads + 1):
-        val = prod[:, a * HEAD_DIM:(a + 1) * HEAD_DIM]
-        rot = (val * cos_t + pltpu.roll(val, HALF, 1) * sin_t).astype(BF16)
-        if a < heads:
-            q_ref[:, a * HEAD_DIM:(a + 1) * HEAD_DIM] = rot
-        else:
-            k_ref[...] = rot
-            k_s[i] = rot
-    v_i = prod[:, q_cols + HEAD_DIM:].astype(BF16)
-    v_ref[...] = v_i
-    vt[i] = v_i.T
-    acc[...] = jnp.zeros_like(acc)
-
-    def chunk(c, carry, diagonal):
+        cos_s[b] = jnp.cos(angles)
+        sin_s[b] = jnp.sin(angles) * sign
+
+    gather_h.middle()
+    gather_h.late()
+    for chunk in range(CHUNKS):
+        gather_dy.start(chunk)
+    for load in w_loads + [stage_in]:
+        load.wait()
+    stage_out.start()
+    own_h.wait()
+    gather_h.end()
+
+    def block_load(ref, block, slot):
+        return pltpu.make_async_copy(ref.at[pl.ds(pl.multiple_of(block * rows, rows), rows), :], blk.at[slot], blk_sems.at[slot])
+
+    def fwd_chunk(i, c, carry, diagonal):
         k_c, vt_c = k_s[c], vt[c]
-        scores = [dot(k_c, q_ref[:, a * HEAD_DIM:(a + 1) * HEAD_DIM], COLS_COLS) * to_log2 for a in range(heads)]
+        scores = [dot(k_c, q_s[i, :, cols[a]], COLS_COLS) * to_log2 for a in range(heads)]
         out = []
         for a in range(heads):
             s = masked(scores[a]) if diagonal else scores[a]
@@ -277,106 +245,99 @@
             out.append((m_new, l_new))
         return tuple(out)
 
-    start = tuple((jnp.full((1, BLK), NEG_LARGE, F32), jnp.zeros((1, BLK), F32)) for _ in range(heads))
-    carry = lax.fori_loop(0, i, lambda c, carry: chunk(c, carry, False), start)
-    carry = chunk(i, carry, True)
-    for a in range(heads):
-        m_a, l_a = carry[a]
-        o_ref[a * HEAD_DIM:(a + 1) * HEAD_DIM, :] = (acc[a] / l_a).astype(BF16)
-        lse_ref[a:a + 1, :] = m_a + jnp.log2(l_a)
-
-    @pl.when(i == FWD_MIDDLE)
-    def _():
-        gather.middle()
-        stage_in.wait()
-        stage_out.start()
-
-    @pl.when(i == pl.num_programs(0) - 1)
-    def _():
-        gather.late()
-        stage_out.wait()
-        gather.end()
-
-
-def forward(hidden, w_q, w_k, w_v, cos_t, sin_t, grad_out, heads):
-    seq_len, width = hidden.shape
-    n_blocks = seq_len // BLK
-    q_cols = heads * HEAD_DIM
-    pairs = heads * seq_len * (seq_len + BLK) // 2
-    any_spec = pl.BlockSpec(memory_space=pl.ANY)
-    rows = lambda cols: pl.BlockSpec((BLK, cols), lambda i: (i, 0))
-    cols = lambda rows: pl.BlockSpec((rows, BLK), lambda i: (0, i))
-    out = lambda *shape, dtype=BF16: jax.ShapeDtypeStruct(shape, dtype)
-    return pl.pallas_call(
-        functools.partial(forward_kernel, heads),
-        grid=(n_blocks,),
-        in_specs=[rows(width), any_spec, any_spec, any_spec, rows(HEAD_DIM), rows(HEAD_DIM), any_spec],
-        out_specs=[rows(q_cols), rows(HEAD_DIM), rows(HEAD_DIM), cols(width), cols(q_cols), cols(8), any_spec],
-        out_shape=[out(seq_len, q_cols), out(seq_len, HEAD_DIM), out(seq_len, HEAD_DIM), out(width, seq_len), out(q_cols, seq_len),
-                   out(8, seq_len, dtype=F32), out(seq_len, width)],
-        scratch_shapes=[pltpu.VMEM((width, q_cols + 2 * HEAD_DIM), BF16), pltpu.SemaphoreType.DMA((3,)), pltpu.VMEM((n_blocks, BLK, HEAD_DIM), BF16),
-                        pltpu.VMEM((n_blocks, HEAD_DIM, BLK), BF16), pltpu.VMEM((heads, HEAD_DIM, BLK), F32), pltpu.VMEM(grad_out.shape, BF16),
-                        pltpu.SemaphoreType.DMA((2,)), SEMS],
-        compiler_params=comm_params(1),
-        cost_estimate=pl.CostEstimate(flops=8 * pairs * HEAD_DIM + 4 * seq_len * width * q_cols, bytes_accessed=8 * seq_len * width, transcendentals=pairs),
-        name="forward",
-    )(hidden, w_q, w_k, w_v, cos_t, sin_t, grad_out)
-
-
-def unrotate(val, cos_t, sin_t):
-    return (val * cos_t - pltpu.roll(val, HALF, 1) * sin_t).astype(BF16)
-
-
-def backward_kernel(heads, q_ref, k_ref, v_ref, dy_ref, wo_ref, ot_ref, lse_ref, cos_ref, sin_ref, o_ref, dkv_ref, dq_a_ref, dq_b_ref, o_all,
-                    wo_v, w_sem, do_s, kt, dk_acc, dv_acc, dqt, stage, stage_sems, sems):
-    i = pl.program_id(0)
-    n_blocks = k_ref.shape[0] // BLK
-    qk_scale = HEAD_DIM ** -0.5
-    to_log2 = qk_scale * LOG2E
-    near = Neighbours()
-    own_rows = o_ref.shape[0]
-    size = own_rows // CHUNKS
-    gather = Gather(near, lambda chunk: o_ref.at[pl.ds(chunk * size, size), :], o_all, own_rows, sems)
-    stage_in = pltpu.make_async_copy(o_ref, stage, stage_sems.at[0])
-    stage_out = pltpu.make_async_copy(stage, gather.block(near.me, 0, CHUNKS), stage_sems.at[1])
-
-    @pl.when(i == 0)
-    def _():
-        q_cols = heads * HEAD_DIM
-        load = pltpu.make_async_copy(wo_ref.at[pl.ds(pl.multiple_of(near.me * q_cols, q_cols), q_cols), :], wo_v, w_sem)
-        load.start()
-        gather.begin()
-        stage_in.start()
-
-        @pl.loop(0, n_blocks)
-        def _(c):
-            kt[c] = k_ref[pl.ds(pl.multiple_of(c * BLK, BLK), BLK), :].T
-
-        load.wait()
-
-    cols = [slice(a * HEAD_DIM, (a + 1) * HEAD_DIM) for a in range(heads)]
-    d_o = dot(dy_ref[...], wo_v[...], COLS_COLS).astype(BF16)
-    do_s[...] = d_o
-    dqt[...] = jnp.zeros_like(dqt)
-    delta = [jnp.sum(ot_ref[cols[a], :].astype(F32) * d_o[:, cols[a]].T.astype(F32), axis=0, keepdims=True) for a in range(heads)]
-
-    def chunk(c, diagonal):
-        rows = pl.ds(pl.multiple_of(c * BLK, BLK), BLK)
-        k_c, v_c, kt_c = k_ref[rows, :], v_ref[rows, :], kt[c]
+    def ht_store(i):
+        at = pl.ds(pl.multiple_of(i * rows, rows), rows)
+        return pltpu.make_async_copy(ht_v.at[lax.rem(i, 2)], ht_ref.at[:, at], ht_sems.at[lax.rem(i, 2)])
+
+    block_load(h_all, 0, 0).start()
+
+    @pl.loop(0, n_blocks)
+    def _(i):
+        slot = lax.rem(i, 2)
+        block_load(h_all, i, slot).wait()
+
+        @pl.when(i + 1 < n_blocks)
+        def _():
+            block_load(h_all, i + 1, 1 - slot).start()
+
+        @pl.when(i >= 2)
+        def _():
+            ht_store(i - 2).wait()
+
+        ht_v[slot] = blk[slot].T
+        ht_store(i).start()
+        prod = dot(blk[slot], w_v[...])
+        cos_t, sin_t = cos_s[i], sin_s[i]
+        for a in range(heads + 1):
+            val = prod[:, a * HEAD_DIM:(a + 1) * HEAD_DIM]
+            rot = (val * cos_t + pltpu.roll(val, HALF, 1) * sin_t).astype(BF16)
+            if a < heads:
+                q_s[i, :, cols[a]] = rot
+            else:
+                k_s[i] = rot
+                kt[i] = rot.T
+        v_i = prod[:, q_cols + HEAD_DIM:].astype(BF16)
+        v_s[i] = v_i
+        vt[i] = v_i.T
+        acc[...] = jnp.zeros_like(acc)
+        start = tuple((jnp.full((1, rows), NEG_LARGE, F32), jnp.zeros((1, rows), F32)) for _ in range(heads))
+        carry = lax.fori_loop(0, i, lambda c, carry: fwd_chunk(i, c, carry, False), start)
+        carry = fwd_chunk(i, i, carry, True)
+        at = pl.ds(pl.multiple_of(i * rows, rows), rows)
+        for a in range(heads):
+            m_a, l_a = carry[a]
+            ot_s[cols[a], at] = (acc[a] / l_a).astype(BF16)
+            lse_s[i, a:a + 1, :] = m_a + jnp.log2(l_a)
+
+        @pl.when(i == FWD_MIDDLE)
+        def _():
+            gather_dy.middle()
+
+        @pl.when(i == FWD_LATE)
+        def _():
+            gather_dy.late()
+
+    for chunk in range(CHUNKS):
+        gather_o.start(chunk)
+    own_o = pltpu.make_async_copy(ot_s, gather_o.block(near.me, 0, CHUNKS), own_sems.at[0])
+    own_o.start()
+
+    def d_o_blocks(low, high):
+        block_load(dy_all, near.across(low), 0).start()
+
+        @pl.loop(low, high)
+        def _(r):
+            slot = lax.rem(r - low, 2)
+            block_load(dy_all, 0, slot).wait()
+
+            @pl.when(r + 1 < high)
+            def _():
+                block_load(dy_all, near.across(r + 1), 1 - slot).start()
+
+            do_s[near.across(r)] = dot(blk[slot], wo_v[...], COLS_COLS).astype(BF16)
+
+    stage_out.wait()
+    gather_dy.end_near()
+    d_o_blocks(0, n_blocks * 3 // 4)
+    gather_dy.end_far()
+    d_o_blocks(n_blocks * 3 // 4, n_blocks)
+
+    def bwd_chunk(i, c, delta, diagonal):
+        k_c, v_c, kt_c = k_s[c], v_s[c], kt[c]
         dk_c = dv_c = None
         for a in range(heads):
-            q_a, do_a = q_ref[:, cols[a]], do_s[:, cols[a]]
+            q_a, do_a = q_s[i, :, cols[a]], do_s[i, :, cols[a]]
             s = dot(k_c, q_a, COLS_COLS) * to_log2
             if diagonal:
                 s = masked(s)
-            p = jnp.exp2(s - lse_ref[a:a + 1, :])
+            p = jnp.exp2(s - lse_s[i, a:a + 1, :])
             d_p = dot(v_c, do_a, COLS_COLS)
             d_s = (p * (d_p - delta[a])).astype(BF16)
             dv_a = dot(p.astype(BF16), do_a)
             dk_a = dot(d_s, q_a)
             dv_c = dv_a if dv_c is None else dv_c + dv_a
             dk_c = dk_a if dk_c is None else dk_c + dk_a
-            dqt[a] += dot(kt_c, d_s)
+            acc[a] += dot(kt_c, d_s)
         if diagonal:
             dk_acc[c] = dk_c
             dv_acc[c] = dv_c
@@ -384,67 +345,92 @@
             dk_acc[c] += dk_c
             dv_acc[c] += dv_c
 
-    @pl.loop(0, i)
+    def dq_stores(i):
+        slot = lax.rem(i, 2)
+        at = pl.ds(pl.multiple_of(i * rows, rows), rows)
+        last = q_cols - HEAD_DIM
+        return [pltpu.make_async_copy(dq_v.at[slot, :, pl.ds(0, last)], dq_a_ref.at[at, :], dq_sems.at[slot, 0]),
+                pltpu.make_async_copy(dq_v.at[slot, :, pl.ds(last, HEAD_DIM)], dq_b_ref.at[at, :], dq_sems.at[slot, 1])]
+
+    for i in (n_blocks - 2, n_blocks - 1):
+        ht_store(i).wait()
+
+    @pl.loop(0, n_blocks)
+    def _(i):
+        at = pl.ds(pl.multiple_of(i * rows, rows), rows)
+        acc[...] = jnp.zeros_like(acc)
+        delta = [jnp.sum(ot_s[cols[a], at].astype(F32) * do_s[i, :, cols[a]].T.astype(F32), axis=0, keepdims=True) for a in range(heads)]
+
+        @pl.loop(0, i)
+        def _(c):
+            bwd_chunk(i, c, delta, False)
+
+        bwd_chunk(i, i, delta, True)
+
+        @pl.when(i >= 2)
+        def _():
+            for store in dq_stores(i - 2):
+                store.wait()
+
+        for a in range(heads):
+            dq_v[lax.rem(i, 2), :, cols[a]] = unrotate(acc[a].T * qk_scale, cos_s[i], sin_s[i])
+        for store in dq_stores(i):
+            store.start()
+
+        @pl.when(i == BWD_MIDDLE)
+        def _():
+            gather_o.middle()
+
+        @pl.when(i == BWD_LATE)
+        def _():
+            gather_o.late()
+
+    @pl.loop(0, n_blocks)
     def _(c):
-        chunk(c, False)
-
-    chunk(i, True)
-    rows = pl.ds(pl.multiple_of(i * BLK, BLK), BLK)
-    for a in range(heads):
-        d_q = unrotate(dqt[a].T * qk_scale, cos_ref[rows, :], sin_ref[rows, :])
-        if a < heads - 1:
-            dq_a_ref[:, cols[a]] = d_q
-        else:
-            dq_b_ref[...] = d_q
-
-    @pl.when(i == BWD_MIDDLE)
-    def _():
-        gather.middle()
-        stage_in.wait()
-        stage_out.start()
-
-    @pl.when(i == BWD_LATE)
-    def _():
-        gather.late()
-
-    @pl.when(i == n_blocks - 1)
-    def _():
-        @pl.loop(0, n_blocks)
-        def _(c):
-            rows_c = pl.ds(pl.multiple_of(c * BLK, BLK), BLK)
-            dkv_ref[rows_c, :HEAD_DIM] = unrotate(dk_acc[c] * qk_scale, cos_ref[rows_c, :], sin_ref[rows_c, :])
-            dkv_ref[rows_c, HEAD_DIM:] = dv_acc[c].astype(BF16)
-
-        stage_out.wait()
-        gather.end()
-
-
-def backward(q, k, v, d_out, w_o, ot, lse, cos_t, sin_t, heads, sp_size):
-    seq_len, width = d_out.shape
-    n_blocks = seq_len // BLK
-    whole = lambda i: (0, 0)
-    pairs = heads * seq_len * (seq_len + BLK) // 2
+        at = pl.ds(pl.multiple_of(c * rows, rows), rows)
+        dkv_v[at, :HEAD_DIM] = unrotate(dk_acc[c] * qk_scale, cos_s[c], sin_s[c])
+        dkv_v[at, HEAD_DIM:] = dv_acc[c].astype(BF16)
+
+    dkv_store = pltpu.make_async_copy(dkv_v, dkv_ref, own_sems.at[1])
+    dkv_store.start()
+    own_o.wait()
+    gather_o.end()
+    for i in (n_blocks - 2, n_blocks - 1):
+        for store in dq_stores(i):
+            store.wait()
+    dkv_store.wait()
+
+
+def attention(x, gain, positions, grad_out, w_q, w_k, w_v, w_o, sp_size, heads):
+    rows, width = x.shape
+    seq_len = rows * sp_size
     q_cols = heads * HEAD_DIM
     any_spec = pl.BlockSpec(memory_space=pl.ANY)
-    rows = lambda cols: pl.BlockSpec((BLK, cols), lambda i: (i, 0))
-    cols = lambda rows: pl.BlockSpec((rows, BLK), lambda i: (0, i))
-    kv_spec = pl.BlockSpec(k.shape, whole)
-    last = (heads - 1) * HEAD_DIM
+    vmem = pl.BlockSpec(memory_space=pltpu.VMEM)
+    dma = pltpu.SemaphoreType.DMA
+    inv_freq = ROPE_THETA ** (-np.arange(0, HEAD_DIM, 2) / HEAD_DIM)
+    freq = jnp.asarray(np.concatenate([inv_freq, inv_freq])[None, :], F32)
+    pairs = heads * seq_len * (seq_len + rows) // 2
     out = lambda *shape: jax.ShapeDtypeStruct(shape, BF16)
+    blocks = lambda *shape, dtype=BF16: pltpu.VMEM((sp_size,) + shape, dtype)
     return pl.pallas_call(
-        functools.partial(backward_kernel, heads),
-        grid=(n_blocks,),
-        in_specs=[rows(q_cols), kv_spec, kv_spec, rows(width), any_spec, cols(q_cols), cols(8), kv_spec, kv_spec, any_spec],
-        out_specs=[pl.BlockSpec((seq_len, 2 * HEAD_DIM), whole), rows(last), rows(HEAD_DIM), any_spec],
-        out_shape=[out(seq_len, 2 * HEAD_DIM), out(seq_len, last), out(seq_len, HEAD_DIM), out(q_cols * sp_size, seq_len)],
-        scratch_shapes=[pltpu.VMEM((q_cols, width), BF16), pltpu.SemaphoreType.DMA, pltpu.VMEM((BLK, q_cols), BF16),
-                        pltpu.VMEM((n_blocks, HEAD_DIM, BLK), BF16), pltpu.VMEM((n_blocks, BLK, HEAD_DIM), F32),
-                        pltpu.VMEM((n_blocks, BLK, HEAD_DIM), F32), pltpu.VMEM((heads, HEAD_DIM, BLK), F32), pltpu.VMEM(ot.shape, BF16),
-                        pltpu.SemaphoreType.DMA((2,)), SEMS],
-        compiler_params=comm_params(2),
-        cost_estimate=pl.CostEstimate(flops=20 * pairs * HEAD_DIM + 2 * seq_len * width * q_cols, bytes_accessed=8 * seq_len * q_cols, transcendentals=pairs),
-        name="backward",
-    )(q, k, v, d_out, w_o, ot, lse, cos_t, sin_t, ot)
+        functools.partial(attention_kernel, heads),
+        in_specs=[any_spec, vmem, vmem, vmem] + [any_spec] * 5,
+        out_specs=[any_spec] * 7,
+        out_shape=[out(seq_len, width), out(seq_len, width), out(q_cols * sp_size, seq_len), out(width, seq_len), out(seq_len, 2 * HEAD_DIM),
+                   out(seq_len, q_cols - HEAD_DIM), out(seq_len, HEAD_DIM)],
+        scratch_shapes=[pltpu.VMEM((rows, width), BF16), pltpu.VMEM((rows, width), BF16), dma((CHUNKS,)), dma((3,)),
+                        blocks(8, rows, dtype=jnp.int32), dma((2, 7)), blocks(rows, HEAD_DIM, dtype=F32), blocks(rows, HEAD_DIM, dtype=F32),
+                        pltpu.VMEM((width, q_cols + 2 * HEAD_DIM), BF16), pltpu.VMEM((q_cols, width), BF16), dma((4,)),
+                        pltpu.VMEM((2, rows, width), BF16), dma((2,)), pltpu.VMEM((2, width, rows), BF16), dma((2,)),
+                        blocks(rows, q_cols), blocks(rows, HEAD_DIM), blocks(rows, HEAD_DIM), blocks(HEAD_DIM, rows), blocks(HEAD_DIM, rows),
+                        pltpu.VMEM((q_cols, seq_len), BF16), blocks(8, rows, dtype=F32), pltpu.VMEM((heads, HEAD_DIM, rows), F32),
+                        blocks(rows, q_cols), blocks(rows, HEAD_DIM, dtype=F32), blocks(rows, HEAD_DIM, dtype=F32),
+                        pltpu.VMEM((2, rows, q_cols), BF16), dma((2, 2)), pltpu.VMEM((seq_len, 2 * HEAD_DIM), BF16), SEMS, SEMS, SEMS],
+        compiler_params=pltpu.CompilerParams(vmem_limit_bytes=VMEM_LIMIT, collective_id=0, has_side_effects=True),
+        cost_estimate=pl.CostEstimate(flops=28 * pairs * HEAD_DIM, bytes_accessed=20 * seq_len * width, transcendentals=2 * pairs),
+        name="attention",
+    )(x, gain.reshape(1, -1), positions.reshape(1, -1), freq, grad_out, w_q, w_k, w_v, w_o)
 
 
 def lanes(*parts):
@@ -716,21 +702,21 @@
                         pltpu.VMEM((ot_all.shape[0], x.shape[0]), BF16), pltpu.VMEM((x.shape[0], ot_all.shape[0]), BF16), pltpu.VMEM(x.shape, BF16),
                         dma((4,)), pltpu.VMEM((sp_size, x.shape[0], 2 * HEAD_DIM), BF16), dma((sp_size, 2)),
                         pltpu.VMEM((2, width, 2 * HEAD_DIM), BF16), dma((2, 2)), pltpu.VMEM(x.shape, F32), SEMS, SEMS, SEMS],
-        compiler_params=pltpu.CompilerParams(vmem_limit_bytes=VMEM_LIMIT, collective_id=3, has_side_effects=True),
+        compiler_params=pltpu.CompilerParams(vmem_limit_bytes=VMEM_LIMIT, collective_id=1, has_side_effects=True),
         cost_estimate=pl.CostEstimate(flops=2 * half * cols * seq_len * n_all, bytes_accessed=8 * half * cols * n_all, transcendentals=0),
         name="products",
     )(ot_all, ht, d_out, d_kv, d_qa, d_qb, x, w_o, w_k, w_v, w_q)
 
 
 def finish_kernel(heads, n_o, n_qa, ht_ref, d_ref, hid_ref, x_ref, dy_ref, gain_ref, part_ref, tiles,
-                  wk_ref, wv_ref, wq_ref, wo_ref, gx_ref, gg_ref, res_ref, ring, ring_sems):
+                  wk_ref, wv_ref, wq_ref, wo_ref, gx_ref, gg_ref, res_ref, d_v, d_sems, ring, ring_sems):
     step = pl.program_id(0) * pl.num_programs(1) + pl.program_id(1)
-    half = ring.shape[2]
-    every = [(c, t) for t in range(tiles.shape[1]) for c in range(2)]
+    half, high = tiles.shape[2], ring.shape[2]
+    every = [(c, t, n) for t in range(tiles.shape[1]) for c in range(2) for n in range(half // high)]
     groups = [every[g:g + RING] for g in range(0, len(every), RING)]
 
-    def pieces(c, t):
-        rows = pl.ds(c * half, half)
+    def pieces(c, t, part):
+        rows = pl.ds(c * half + part * high, high)
         cols = ring.shape[3]
         if t < n_o:
             return [(0, cols, wo_ref.at[rows, pl.ds(t * cols, cols)])]
@@ -739,31 +725,46 @@
         return [(n * wide, wide, wq_ref.at[rows, pl.ds(((t * per + n) * heads + first) * HEAD_DIM, wide)]) for n in range(per)]
 
     def ins(g):
-        return [pltpu.make_async_copy(tiles.at[c, t], ring.at[g % 2, n], ring_sems.at[0, g % 2, n, 0]) for n, (c, t) in enumerate(groups[g])]
+        return [pltpu.make_async_copy(tiles.at[c, t, pl.ds(part * high, high), :], ring.at[g % DEPTH, n], ring_sems.at[0, g % DEPTH, n, 0])
+                for n, (c, t, part) in enumerate(groups[g])]
 
     def outs(g):
-        return [pltpu.make_async_copy(ring.at[g % 2, n, :, pl.ds(col, count)], dst, ring_sems.at[1, g % 2, n, m])
-                for n, (c, t) in enumerate(groups[g]) for m, (col, count, dst) in enumerate(pieces(c, t))]
-
-    for g in range(len(groups) + 2):
+        return [pltpu.make_async_copy(ring.at[g % DEPTH, n, :, pl.ds(col, count)], dst, ring_sems.at[1, g % DEPTH, n, m])
+                for n, item in enumerate(groups[g]) for m, (col, count, dst) in enumerate(pieces(*item))]
+
+    def pair_load(p):
+        at = pl.ds(2 * p, 2)
+        return pltpu.make_async_copy(d_ref.at[at], d_v.at[at], d_sems.at[p])
+
+    @pl.when(step == 0)
+    def _():
+        for p in range(d_v.shape[0] // 2):
+            pair_load(p).start()
+
+    for g in range(len(groups) + DEPTH):
         @pl.when(step == g)
         def _():
-            if 0 <= g - 1 < len(groups):
-                for copy in ins(g - 1):
-                    copy.wait()
-                for copy in outs(g - 1):
-                    copy.start()
-            if 0 <= g - 2 < len(groups):
-                for copy in outs(g - 2):
+            if g >= DEPTH:
+                for copy in outs(g - DEPTH):
                     copy.wait()
             if g < len(groups):
                 for copy in ins(g):
                     copy.start()
+            if 2 <= g < len(groups) + 2:
+                for copy in ins(g - 2):
+                    copy.wait()
+                for copy in outs(g - 2):
+                    copy.start()
+
+    for p in range(d_v.shape[0] // 2):
+        @pl.when(step == p)
+        def _():
+            pair_load(p).wait()
 
     ht = ht_ref[...]
     pair = 2 * pl.program_id(1)
-    wk_ref[...] = dot(ht, lanes(d_ref[pair, :, :HEAD_DIM], d_ref[pair + 1, :, :HEAD_DIM]))
-    wv_ref[...] = dot(ht, lanes(d_ref[pair, :, HEAD_DIM:], d_ref[pair + 1, :, HEAD_DIM:]))
+    wk_ref[...] = dot(ht, lanes(d_v[pair, :, :HEAD_DIM], d_v[pair + 1, :, :HEAD_DIM]))
+    wv_ref[...] = dot(ht, lanes(d_v[pair, :, HEAD_DIM:], d_v[pair + 1, :, HEAD_DIM:]))
 
     @pl.when(step == 0)
     def _():
@@ -776,7 +777,7 @@
         normed = x_f * inv_rms
         d_hid = hid_ref[...]
         both = d_hid * normed
-        gain = gain_ref[...]
+        gain = gain_ref[...].astype(F32)
         gg_ref[...] += jnp.sum(both.reshape(both.shape[0] // 8, 8, both.shape[1]), axis=0)
         mean = jnp.mean(both * gain, axis=-1, keepdims=True)
         d_x = inv_rms * (d_hid * gain - normed * mean)
@@ -789,7 +790,7 @@
     groups = d_kv.shape[0]
     n_j = groups // 2
     steps = (width // MROWS) * n_j
-    assert -(-2 * tiles.shape[1] // RING) + 2 <= steps
+    assert -(-4 * tiles.shape[1] // RING) + DEPTH <= steps
     any_spec = pl.BlockSpec(memory_space=pl.ANY)
     rows = pl.BlockSpec((x.shape[0] // ROW_STEPS, width), lambda m, j: (jnp.minimum(m * n_j + j, ROW_STEPS - 1), 0))
     whole = lambda *shape: pl.BlockSpec(shape, lambda m, j: (0,) * len(shape))
@@ -799,13 +800,13 @@
         functools.partial(finish_kernel, heads, n_o, n_qa),
         grid=(width // MROWS, n_j),
         in_specs=[pl.BlockSpec((MROWS, seq_len), lambda m, j: (m, 0)),
-                  pl.BlockSpec(d_kv.shape, lambda m, j: (0, 0, 0), pipeline_mode=pl.Buffered(1)),
-                  rows, rows, rows, whole(1, width), rows, any_spec],
+                  any_spec, rows, rows, rows, whole(1, width), rows, any_spec],
         out_specs=[kv_out, kv_out, any_spec, any_spec, rows, whole(8, width), rows],
         out_shape=[out(groups * HEAD_DIM), out(groups * HEAD_DIM), out(groups * heads * HEAD_DIM),
                    jax.ShapeDtypeStruct((groups * heads * HEAD_DIM, width), F32), jax.ShapeDtypeStruct(x.shape, BF16),
                    jax.ShapeDtypeStruct((8, width), F32), jax.ShapeDtypeStruct(x.shape, BF16)],
-        scratch_shapes=[pltpu.VMEM((2, RING) + tiles.shape[2:], F32), pltpu.SemaphoreType.DMA((2, 2, RING, 4))],
+        scratch_shapes=[pltpu.VMEM(d_kv.shape, BF16), pltpu.SemaphoreType.DMA((groups // 2,)),
+                        pltpu.VMEM((DEPTH, RING, tiles.shape[2] // 2, tiles.shape[3]), F32), pltpu.SemaphoreType.DMA((2, DEPTH, RING, 4))],
         compiler_params=params(2),
         cost_estimate=pl.CostEstimate(flops=4 * width * seq_len * groups * HEAD_DIM, bytes_accessed=2 * width * seq_len, transcendentals=0),
         name="finish",
@@ -822,14 +823,11 @@
     def local_step(x, grad_out, positions, gain, w_q, w_k, w_v, w_o):
         n_heads = w_q.shape[1] // HEAD_DIM
         heads = n_heads // sp_size
-        gain_f = gain.astype(F32).reshape(1, -1)
-        hidden, cos_t, sin_t = gather_h(x, gain_f, positions, sp_size)
-        q, k, v, ht, ot, lse, d_out = forward(hidden, w_q, w_k, w_v, cos_t, sin_t, grad_out, heads)
-        *grads, ot_all = backward(q, k, v, d_out, w_o, ot, lse, cos_t, sin_t, heads, sp_size)
+        _, d_out, ot_all, ht, *grads = attention(x, gain, positions, grad_out, w_q, w_k, w_v, w_o, sp_size, heads)
         tiles, kv_all, _, _, part, d_hid = products(ot_all, ht, d_out, *grads, x, w_o, w_k, w_v, w_q, sp_size, heads)
         n_o = x.shape[1] // tiles.shape[3]
         grad_wk, grad_wv, grad_wq, grad_wo, grad_x, gg, result = finish(
-            ht, kv_all.reshape(sp_size, -1, 2 * HEAD_DIM), tiles, d_hid, x, grad_out, gain_f, part, heads, n_o, (tiles.shape[1] - n_o) * 2 // 3)
+            ht, kv_all.reshape(sp_size, -1, 2 * HEAD_DIM), tiles, d_hid, x, grad_out, gain.reshape(1, -1), part, heads, n_o, (tiles.shape[1] - n_o) * 2 // 3)
         grad_gain = jnp.sum(lax.all_gather(gg, 'sp', axis=0, tiled=True), axis=0)
         return result, grad_x, grad_wq, grad_wk, grad_wv, grad_wo, grad_gain
 

time: 641 us -> 614 us (0.958)
  Pallas kernels: 626 us -> 601 us
    pallas_call x3 -> x1, Pallas kernels: 348 us -> 326 us  [attention(): pl.pallas_call(functools.partial(attention_kernel, heads), in_specs=[any_...]
where the time goes in v3:
time: 614 us; the launch traced here: 613 us
  Pallas kernels  601 us (98%)
  blocking collectives  10.1 us (2%)
    pallas_call x1, Pallas kernels, attention(): pl.pallas_call(functools.partial(attention_kernel, heads), in_specs=[any_...  326 us
    pallas_call x1, Pallas kernels, products(): pl.pallas_call(functools.partial(products_kernel, heads), in_specs=[any_s...  183 us
    pallas_call x1, Pallas kernels, finish(): pl.pallas_call(functools.partial(finish_kernel, heads, n_o, n_qa), grid=(...  92.7 us

profile of v3, /device:TPU:0, one launch (start us, length us, event | category | flops | bytes accessed | tf_op | source)
XLA Modules:
  0.0 613.4 jit_solution(3228730303649416077)
XLA Ops:
  0.6 1.3 reshape.24.gain_ref
  1.9 325.5 %attention.1 = (bf16[4096,3072]{1,0:T(8,128)(2,1)}, bf16[4096,3072]{1,0:T(8,128)(2,1)}, bf16[3072,4096]{1,0:T(8,128)(2,1)}, bf16[3072,4096]{1,0:T(8,128)(2,1)}, ...) custom-call(bf16[512,3072]{1,0:T(8,128)(2,1)} %x_ref.5, ...), custom_call_target="tpu_custom_call" | custom-call | flops 101468602368 | bytes 251658240 | tf_op jit(solution)/shard_map/attention/pallas_call | solution.py:416
  327.5 182.5 %products.1 = (f32[2,12,1536,512]{3,2,1,0:T(8,128)}, bf16[32768,256]{1,0:T(8,128)(2,1)}, bf16[32768,256]{1,0:T(8,128)(2,1)}, bf16[32768,128]{1,0:T(8,128)(2,1)},...) custom-call(bf16[3072,4096]{1,0:T(8,128)(2,1)} %get-tuple-element.25.ot_ref, ...), custom_call_target="tpu_custom_call" | custom-call | flops 77309411328 | bytes 75497472 | tf_op jit(solution)/shard_map/products/pallas_call | solution.py:694
  510.0 92.7 %finish.1 = (f32[3072,1024]{1,0:T(8,128)}, f32[3072,1024]{1,0:T(8,128)}, f32[3072,3072]{1,0:T(8,128)}, f32[3072,3072]{1,0:T(8,128)}, bf16[512,3072]{1,0:T(8,128)...) custom-call(bf16[3072,4096]{1,0:T(8,128)(2,1)} %get-tuple-element.24.ht_ref, bf16[8,4096,256]{2,1,0:T(8,128)(2,1)} %bitcast.3, ...), custom_call_target="tpu_custom_call" | custom-call | flops 51539607552 | bytes 25165824 | tf_op jit(solution)/shard_map/finish/pallas_call | solution.py:799
  602.7 10.1 %all_gather.3 = f32[64,3072]{1,0:T(8,128)S(1)} all-gather(f32[8,3072]{1,0:T(8,128)} %get-tuple-element.40), channel_id=1, replica_groups=mesh['dp'=2,'sp'=8] {'sp'}, dimensions={0}, use_global_device_ids=true | all-gather | bytes 884736 | tf_op jit(solution)/shard_map/all_gather | solution.py:831
  612.7 0.7 reduce_sum.9

commit v4 on v3

--- a/solution.py
+++ b/solution.py
@@ -20,6 +20,7 @@
 MROWS = 384
 RING = 2
 DEPTH = 5
+COPY_ROWS = 24
 ROW_STEPS = 8
 F32 = jnp.float32
 BF16 = jnp.bfloat16
@@ -437,10 +438,10 @@
     return jnp.concatenate(parts, axis=1)
 
 
-def products_kernel(heads, ot_ref, ht_ref, dy_ref, d_kv_ref, d_qa_ref, d_qb_ref, x_ref, wo_ref, wk_ref, wv_ref, wq_ref,
-                    tiles, kv_all, qa_all, qb_all, res_ref, hid_ref,
+def products_kernel(heads, ot_ref, ht_ref, dy_ref, d_kv_ref, d_qa_ref, d_qb_ref, x_ref, own_dy_ref, gain_ref, wo_ref, wk_ref, wv_ref, wq_ref,
+                    wo_out, wq_out, kv_all, qa_all, qb_all, res_ref, gx_ref, gg_ref,
                     a_buf, b_buf, tile, a_sem, b_sems, t_sems, x_sems, stage, stage_sems, ot_v, o_v, x_v, io_sems, own, own_sems, w_v, w_sems, acc,
-                    kv_sems, qa_sems, qb_sems):
+                    gg_v, gg_all, gg_sems, kv_sems, qa_sems, qb_sems):
     near = Neighbours()
     core = lax.rem(near.me, 2)
     half = a_buf.shape[0]
@@ -448,9 +449,8 @@
     rows, width = x_ref.shape
     chunk = seq_len // CHUNKS
     n_cols = d_kv_ref.shape[1]
-    n_o, n_all = width // (2 * n_cols), tiles.shape[1]
-    n_qa = (n_all - n_o) * 2 // 3
-    n_oa = n_o + n_qa
+    n_o, n_all = width // (2 * n_cols), x_sems.shape[1]
+    n_oa = n_o + (n_all - n_o) * 2 // 3
 
     def gather_of(src, dst, sems):
         return Gather(near, lambda c: src.at[pl.ds(c * chunk, chunk), :], dst, seq_len, sems)
@@ -473,7 +473,8 @@
     ot_load = pltpu.make_async_copy(ot_ref.at[:, tokens], ot_v, io_sems.at[0])
     x_load = pltpu.make_async_copy(x_ref, x_v, io_sems.at[1])
     res_store = pltpu.make_async_copy(x_v, res_ref, io_sems.at[2])
-    hid_store = pltpu.make_async_copy(acc, hid_ref, io_sems.at[3])
+    dy_load = pltpu.make_async_copy(own_dy_ref, o_v, io_sems.at[3])
+    gx_store = pltpu.make_async_copy(o_v, gx_ref, io_sems.at[0])
 
     def a_load(ref):
         return pltpu.make_async_copy(ref.at[own_rows, :], a_buf, a_sem)
@@ -496,11 +497,35 @@
                     for load in b_loads(source, step - low, slot, g):
                         load.start()
 
-    def keep(step):
-        return pltpu.make_async_copy(tile.at[lax.rem(step, 2)], tiles.at[core, step], t_sems.at[lax.rem(step, 2)])
-
-    def give(step):
-        return send(tile.at[lax.rem(step, 2)], tiles.at[core, step], x_sems, step, near.sib)
+    def pieces(kind, step):
+        wide = (2 * n_cols, n_cols, HEAD_DIM)[kind]
+        slot = lax.rem(step, 2)
+        out = []
+        for n in range(2 * n_cols // wide):
+            group = (step - (0, n_o, n_oa)[kind]) * (2 * n_cols // wide) + n
+            col = (group * wide, group * heads * HEAD_DIM, (group + 1) * heads * HEAD_DIM - HEAD_DIM)[kind]
+            dst = (wo_out, wq_out, wq_out)[kind].at[own_rows, pl.ds(pl.multiple_of(col, HEAD_DIM), wide)]
+            src = tile.at[slot, :, pl.ds(n * wide, wide)]
+            out.append((pltpu.make_async_copy(src, dst, t_sems.at[slot]), send(src, dst, x_sems, step, near.sib)))
+        return out
+
+    def start_tile(step):
+        for kind, (low, high) in enumerate(((0, n_o), (n_o, n_oa), (n_oa, n_all))):
+            @pl.when(jnp.logical_and(step >= low, step < high))
+            def _():
+                for keep, give in pieces(kind, step):
+                    keep.start()
+                    give.start()
+
+    def whole_tile(step):
+        slot = lax.rem(step, 2)
+        dst = wo_out.at[own_rows, pl.ds(0, 2 * n_cols)]
+        return pltpu.make_async_copy(tile.at[slot], dst, t_sems.at[slot]), send(tile.at[slot], dst, x_sems, step, near.sib)
+
+    def wait_tile(step):
+        keep, give = whole_tile(step)
+        keep.wait()
+        give.wait_send()
 
     def result_part():
         cols = b_buf.shape[2]
@@ -587,7 +612,8 @@
             else:
                 acc[...] += prod
 
-    near.meet([near.sib, near.xn, near.yn])
+    others = near.others()
+    near.meet(others)
     for c in range(CHUNKS):
         gathers[0].start(c)
     a_load(ot_ref).start()
@@ -609,16 +635,14 @@
 
         @pl.when(step >= 2)
         def _():
-            keep(step - 2).wait()
-            give(step - 2).wait_send()
+            wait_tile(step - 2)
 
         @pl.when(step == n_o)
         def _():
             a_load(ht_ref).wait()
 
         tile[slot] = dot(a_buf[...], b_buf[slot])
-        keep(step).start()
-        give(step).start()
+        start_tile(step)
 
         @pl.when(step == n_o - 2)
         def _():
@@ -653,6 +677,9 @@
 
         @pl.when(step == n_oa - 1)
         def _():
+            res_store.wait()
+            x_load.start()
+            dy_load.start()
             gathers[1].end()
             start_b(step + 1)
             hidden_add(0)
@@ -667,70 +694,85 @@
     near_count = own.shape[0] * 3 // 4
     hidden_start(2, 0, near_count)
     for step in (n_all - 2, n_all - 1):
-        keep(step).wait()
-        give(step).wait_send()
+        wait_tile(jnp.int32(step))
     hidden_add(2, 0, near_count)
     gathers[2].end_far()
     hidden_start(2, near_count)
     hidden_add(2, near_count)
-    hid_store.start()
+
+    gain = gain_ref[...].astype(F32)
+    gg_v[...] = jnp.zeros_like(gg_v)
+    x_load.wait()
+    dy_load.wait()
+
+    @pl.loop(0, rows // 32)
+    def _(r):
+        at = pl.ds(pl.multiple_of(r * 32, 32), 32)
+        x_f = x_v[at, :].astype(F32)
+        inv_rms = lax.rsqrt(jnp.mean(x_f * x_f, axis=-1, keepdims=True) + NORM_EPS)
+        normed = x_f * inv_rms
+        d_hid = acc[at, :]
+        both = d_hid * normed
+        gg_v[...] += jnp.sum(both.reshape(4, 8, width), axis=0)
+        mean = jnp.mean(both * gain, axis=-1, keepdims=True)
+        o_v[at, :] = (o_v[at, :].astype(F32) + inv_rms * (d_hid * gain - normed * mean)).astype(BF16)
+
+    gg_all[near.me] = gg_v[...]
+    parts = [send(gg_v, gg_all.at[near.me], gg_sems, r, peer) for r, peer in enumerate(others)]
+    for copy in parts:
+        copy.start()
+    gx_store.start()
 
     @pl.loop(0, n_all)
     def _(step):
-        give(step).wait_recv()
-
-    res_store.wait()
-    hid_store.wait()
-
-
-def products(ot_all, ht, d_out, d_kv, d_qa, d_qb, x, w_o, w_k, w_v, w_q, sp_size, heads):
+        whole_tile(step)[1].wait_recv()
+
+    for copy in parts:
+        copy.wait()
+    gg_ref[...] = jnp.sum(jnp.sum(gg_all[...], axis=0), axis=0, keepdims=True)
+    gx_store.wait()
+
+
+def products(ot_all, ht, d_out, d_kv, d_qa, d_qb, x, grad_out, gain, w_o, w_k, w_v, w_q, sp_size, heads):
     width, seq_len = ht.shape
     half = width // 2
     cols = 2 * d_kv.shape[1]
     n_all = width // cols + sp_size * (d_qa.shape[1] + d_qb.shape[1]) // cols
     any_spec = pl.BlockSpec(memory_space=pl.ANY)
+    vmem = pl.BlockSpec(memory_space=pltpu.VMEM)
     dma = pltpu.SemaphoreType.DMA
     gathered = [jax.ShapeDtypeStruct((sp_size * seq_len, d.shape[1]), BF16) for d in (d_kv, d_qa, d_qb)]
     return pl.pallas_call(
         functools.partial(products_kernel, heads),
-        in_specs=[any_spec] * 11,
-        out_specs=[any_spec] * 6,
-        out_shape=[jax.ShapeDtypeStruct((2, n_all, half, cols), F32)] + gathered
-        + [jax.ShapeDtypeStruct(x.shape, BF16), jax.ShapeDtypeStruct(x.shape, F32)],
+        in_specs=[any_spec] * 8 + [vmem] + [any_spec] * 4,
+        out_specs=[any_spec] * 7 + [vmem],
+        out_shape=[jax.ShapeDtypeStruct((ot_all.shape[0], width), F32), jax.ShapeDtypeStruct(w_q.shape, F32)] + gathered
+        + [jax.ShapeDtypeStruct(x.shape, BF16), jax.ShapeDtypeStruct(x.shape, BF16), jax.ShapeDtypeStruct((1, width), F32)],
         scratch_shapes=[pltpu.VMEM((half, seq_len), BF16), pltpu.VMEM((2, seq_len, cols), BF16), pltpu.VMEM((2, half, cols), F32),
                         dma, dma((2, 2)), dma((2,)), dma((2, n_all)), pltpu.VMEM(d_kv.shape, BF16), dma((2,)),
                         pltpu.VMEM((ot_all.shape[0], x.shape[0]), BF16), pltpu.VMEM((x.shape[0], ot_all.shape[0]), BF16), pltpu.VMEM(x.shape, BF16),
                         dma((4,)), pltpu.VMEM((sp_size, x.shape[0], 2 * HEAD_DIM), BF16), dma((sp_size, 2)),
-                        pltpu.VMEM((2, width, 2 * HEAD_DIM), BF16), dma((2, 2)), pltpu.VMEM(x.shape, F32), SEMS, SEMS, SEMS],
+                        pltpu.VMEM((2, width, 2 * HEAD_DIM), BF16), dma((2, 2)), pltpu.VMEM(x.shape, F32),
+                        pltpu.VMEM((8, width), F32), pltpu.VMEM((sp_size, 8, width), F32), dma((2, 7)), SEMS, SEMS, SEMS],
         compiler_params=pltpu.CompilerParams(vmem_limit_bytes=VMEM_LIMIT, collective_id=1, has_side_effects=True),
         cost_estimate=pl.CostEstimate(flops=2 * half * cols * seq_len * n_all, bytes_accessed=8 * half * cols * n_all, transcendentals=0),
         name="products",
-    )(ot_all, ht, d_out, d_kv, d_qa, d_qb, x, w_o, w_k, w_v, w_q)
-
-
-def finish_kernel(heads, n_o, n_qa, ht_ref, d_ref, hid_ref, x_ref, dy_ref, gain_ref, part_ref, tiles,
-                  wk_ref, wv_ref, wq_ref, wo_ref, gx_ref, gg_ref, res_ref, d_v, d_sems, ring, ring_sems):
+    )(ot_all, ht, d_out, d_kv, d_qa, d_qb, x, grad_out, gain, w_o, w_k, w_v, w_q)
+
+
+def finish_kernel(ht_ref, d_ref, gx_in, res_in, gg_in, wo_in, wq_in, wk_ref, wv_ref, wq_ref, wo_ref, gx_ref, res_ref, gg_ref, d_v, d_sems, ring, ring_sems):
     step = pl.program_id(0) * pl.num_programs(1) + pl.program_id(1)
-    half, high = tiles.shape[2], ring.shape[2]
-    every = [(c, t, n) for t in range(tiles.shape[1]) for c in range(2) for n in range(half // high)]
+    high = ring.shape[2]
+    every = [(src, dst, r) for src, dst in ((wo_in, wo_ref), (wq_in, wq_ref)) for r in range(src.shape[0] // high)]
     groups = [every[g:g + RING] for g in range(0, len(every), RING)]
 
-    def pieces(c, t, part):
-        rows = pl.ds(c * half + part * high, high)
-        cols = ring.shape[3]
-        if t < n_o:
-            return [(0, cols, wo_ref.at[rows, pl.ds(t * cols, cols)])]
-        wide, first, t = ((heads - 1) * HEAD_DIM, 0, t - n_o) if t < n_o + n_qa else (HEAD_DIM, heads - 1, t - n_o - n_qa)
-        per = cols // wide
-        return [(n * wide, wide, wq_ref.at[rows, pl.ds(((t * per + n) * heads + first) * HEAD_DIM, wide)]) for n in range(per)]
-
     def ins(g):
-        return [pltpu.make_async_copy(tiles.at[c, t, pl.ds(part * high, high), :], ring.at[g % DEPTH, n], ring_sems.at[0, g % DEPTH, n, 0])
-                for n, (c, t, part) in enumerate(groups[g])]
+        return [pltpu.make_async_copy(src.at[pl.ds(r * high, high), :], ring.at[g % DEPTH, n], ring_sems.at[0, g % DEPTH, n])
+                for n, (src, dst, r) in enumerate(groups[g])]
 
     def outs(g):
-        return [pltpu.make_async_copy(ring.at[g % DEPTH, n, :, pl.ds(col, count)], dst, ring_sems.at[1, g % DEPTH, n, m])
-                for n, item in enumerate(groups[g]) for m, (col, count, dst) in enumerate(pieces(*item))]
+        return [pltpu.make_async_copy(ring.at[g % DEPTH, n], dst.at[pl.ds(r * high, high), :], ring_sems.at[1, g % DEPTH, n])
+                for n, (src, dst, r) in enumerate(groups[g])]
 
     def pair_load(p):
         at = pl.ds(2 * p, 2)
@@ -768,49 +810,39 @@
 
     @pl.when(step == 0)
     def _():
-        gg_ref[...] = jnp.zeros_like(gg_ref)
+        gg_ref[...] = gg_in[...]
 
     @pl.when(step < ROW_STEPS)
     def _():
-        x_f = x_ref[...].astype(F32)
-        inv_rms = lax.rsqrt(jnp.mean(x_f * x_f, axis=-1, keepdims=True) + NORM_EPS)
-        normed = x_f * inv_rms
-        d_hid = hid_ref[...]
-        both = d_hid * normed
-        gain = gain_ref[...].astype(F32)
-        gg_ref[...] += jnp.sum(both.reshape(both.shape[0] // 8, 8, both.shape[1]), axis=0)
-        mean = jnp.mean(both * gain, axis=-1, keepdims=True)
-        d_x = inv_rms * (d_hid * gain - normed * mean)
-        gx_ref[...] = (dy_ref[...].astype(F32) + d_x).astype(BF16)
-        res_ref[...] = part_ref[...]
-
-
-def finish(ht, d_kv, tiles, d_hid, x, grad_out, gain_f, result, heads, n_o, n_qa):
+        gx_ref[...] = gx_in[...]
+        res_ref[...] = res_in[...]
+
+
+def finish(ht, d_kv, w_o_grad, w_q_grad, grad_x, result, grad_gain):
     width, seq_len = ht.shape
     groups = d_kv.shape[0]
     n_j = groups // 2
     steps = (width // MROWS) * n_j
-    assert -(-4 * tiles.shape[1] // RING) + DEPTH <= steps
+    high = width // COPY_ROWS
+    assert -(-(w_o_grad.shape[0] + w_q_grad.shape[0]) // (high * RING)) + DEPTH <= steps
     any_spec = pl.BlockSpec(memory_space=pl.ANY)
-    rows = pl.BlockSpec((x.shape[0] // ROW_STEPS, width), lambda m, j: (jnp.minimum(m * n_j + j, ROW_STEPS - 1), 0))
-    whole = lambda *shape: pl.BlockSpec(shape, lambda m, j: (0,) * len(shape))
+    rows = pl.BlockSpec((grad_x.shape[0] // ROW_STEPS, width), lambda m, j: (jnp.minimum(m * n_j + j, ROW_STEPS - 1), 0))
+    whole = pl.BlockSpec((1, width), lambda m, j: (0, 0))
     kv_out = pl.BlockSpec((MROWS, 2 * HEAD_DIM), lambda m, j: (m, j))
     out = lambda cols: jax.ShapeDtypeStruct((width, cols), F32)
+    like = lambda val: jax.ShapeDtypeStruct(val.shape, val.dtype)
     return pl.pallas_call(
-        functools.partial(finish_kernel, heads, n_o, n_qa),
+        finish_kernel,
         grid=(width // MROWS, n_j),
-        in_specs=[pl.BlockSpec((MROWS, seq_len), lambda m, j: (m, 0)),
-                  any_spec, rows, rows, rows, whole(1, width), rows, any_spec],
-        out_specs=[kv_out, kv_out, any_spec, any_spec, rows, whole(8, width), rows],
-        out_shape=[out(groups * HEAD_DIM), out(groups * HEAD_DIM), out(groups * heads * HEAD_DIM),
-                   jax.ShapeDtypeStruct((groups * heads * HEAD_DIM, width), F32), jax.ShapeDtypeStruct(x.shape, BF16),
-                   jax.ShapeDtypeStruct((8, width), F32), jax.ShapeDtypeStruct(x.shape, BF16)],
+        in_specs=[pl.BlockSpec((MROWS, seq_len), lambda m, j: (m, 0)), any_spec, rows, rows, whole, any_spec, any_spec],
+        out_specs=[kv_out, kv_out, any_spec, any_spec, rows, rows, whole],
+        out_shape=[out(groups * HEAD_DIM), out(groups * HEAD_DIM), like(w_q_grad), like(w_o_grad), like(grad_x), like(result), like(grad_gain)],
         scratch_shapes=[pltpu.VMEM(d_kv.shape, BF16), pltpu.SemaphoreType.DMA((groups // 2,)),
-                        pltpu.VMEM((DEPTH, RING, tiles.shape[2] // 2, tiles.shape[3]), F32), pltpu.SemaphoreType.DMA((2, DEPTH, RING, 4))],
+                        pltpu.VMEM((DEPTH, RING, high, width), F32), pltpu.SemaphoreType.DMA((2, DEPTH, RING))],
         compiler_params=params(2),
         cost_estimate=pl.CostEstimate(flops=4 * width * seq_len * groups * HEAD_DIM, bytes_accessed=2 * width * seq_len, transcendentals=0),
         name="finish",
-    )(ht, d_kv, d_hid, x, grad_out, gain_f, result, tiles)
+    )(ht, d_kv, grad_x, result, grad_gain, w_o_grad, w_q_grad)
 
 
 def solution(mesh):
@@ -824,12 +856,12 @@
         n_heads = w_q.shape[1] // HEAD_DIM
         heads = n_heads // sp_size
         _, d_out, ot_all, ht, *grads = attention(x, gain, positions, grad_out, w_q, w_k, w_v, w_o, sp_size, heads)
-        tiles, kv_all, _, _, part, d_hid = products(ot_all, ht, d_out, *grads, x, w_o, w_k, w_v, w_q, sp_size, heads)
-        n_o = x.shape[1] // tiles.shape[3]
-        grad_wk, grad_wv, grad_wq, grad_wo, grad_x, gg, result = finish(
-            ht, kv_all.reshape(sp_size, -1, 2 * HEAD_DIM), tiles, d_hid, x, grad_out, gain.reshape(1, -1), part, heads, n_o, (tiles.shape[1] - n_o) * 2 // 3)
-        grad_gain = jnp.sum(lax.all_gather(gg, 'sp', axis=0, tiled=True), axis=0)
-        return result, grad_x, grad_wq, grad_wk, grad_wv, grad_wo, grad_gain
+        gain = gain.reshape(1, -1)
+        w_o_grad, w_q_grad, kv_all, _, _, result, grad_x, grad_gain = products(ot_all, ht, d_out, *grads, x, grad_out, gain, w_o, w_k, w_v, w_q,
+                                                                               sp_size, heads)
+        grad_wk, grad_wv, grad_wq, grad_wo, grad_x, result, grad_gain = finish(
+            ht, kv_all.reshape(sp_size, -1, 2 * HEAD_DIM), w_o_grad, w_q_grad, grad_x, result, grad_gain)
+        return result, grad_x, grad_wq, grad_wk, grad_wv, grad_wo, grad_gain.reshape(-1)
 
     return jax.shard_map(local_step, mesh=mesh,
                          in_specs=(seq_spec, seq_spec, pos_spec, P(None), replicated, replicated, replicated, replicated),

time: 614 us -> 614 us (level)
  blocking collectives: 10.1 us -> 0 us
  Pallas kernels: 601 us -> 610 us
    pallas_call x1, Pallas kernels: 183 us -> 197 us  [products(): pl.pallas_call(functools.partial(products_kernel, heads), in_specs=[any_s...]
    all_gather x1 -> x0, blocking collectives: 10.1 us -> none  [local_step(): grad_gain = jnp.sum(lax.all_gather(gg, 'sp', axis=0, tiled=True), axis=0)]
where the time goes in v4:
time: 614 us; the launch traced here: 613 us
  Pallas kernels  610 us (99%)
    pallas_call x1, Pallas kernels, attention(): pl.pallas_call(functools.partial(attention_kernel, heads), in_specs=[any_...  326 us
    pallas_call x1, Pallas kernels, products(): pl.pallas_call(functools.partial(products_kernel, heads), in_specs=[any_s...  197 us
    pallas_call x1, Pallas kernels, finish(): pl.pallas_call(finish_kernel, grid=(width // MROWS, n_j), in_specs=[pl.Bl...  87.6 us

profile of v4, /device:TPU:0, one launch (start us, length us, event | category | flops | bytes accessed | tf_op | source)
XLA Modules:
  0.0 612.6 jit_solution(6895766646052280681)
XLA Ops:
  0.6 1.3 reshape.27.gain_ref
  1.9 325.5 %attention.1 = (bf16[4096,3072]{1,0:T(8,128)(2,1)}, bf16[4096,3072]{1,0:T(8,128)(2,1)}, bf16[3072,4096]{1,0:T(8,128)(2,1)}, bf16[3072,4096]{1,0:T(8,128)(2,1)}, ...) custom-call(bf16[512,3072]{1,0:T(8,128)(2,1)} %x_ref.3, ...), custom_call_target="tpu_custom_call" | custom-call | flops 101468602368 | bytes 251658240 | tf_op jit(solution)/shard_map/attention/pallas_call | solution.py:417
  327.5 197.3 %products.1 = (f32[3072,3072]{1,0:T(8,128)}, f32[3072,3072]{1,0:T(8,128)}, bf16[32768,256]{1,0:T(8,128)(2,1)}, bf16[32768,256]{1,0:T(8,128)(2,1)}, bf16[32768,12...) custom-call(bf16[3072,4096]{1,0:T(8,128)(2,1)} %get-tuple-element.27.ot_ref, ...), custom_call_target="tpu_custom_call" | custom-call | flops 77309411328 | bytes 75497472 | tf_op jit(solution)/shard_map/products/pallas_call | solution.py:745
  524.8 87.6 %finish.1 = (f32[3072,1024]{1,0:T(8,128)}, f32[3072,1024]{1,0:T(8,128)}, f32[3072,3072]{1,0:T(8,128)}, f32[3072,3072]{1,0:T(8,128)}, bf16[512,3072]{1,0:T(8,128)...) custom-call(bf16[3072,4096]{1,0:T(8,128)(2,1)} %get-tuple-element.26.ht_ref, bf16[8,4096,256]{2,1,0:T(8,128)(2,1)} %bitcast.4, ...), custom_call_target="tpu_custom_call" | custom-call | flops 51539607552 | bytes 25165824 | tf_op jit(solution)/shard_map/finish/pallas_call | solution.py:834

commit v5 on v4

--- a/solution.py
+++ b/solution.py
@@ -16,10 +16,10 @@
 LOG2E = 1.4426950408889634
 BLK = 512
 CHUNKS = 4
-FWD_MIDDLE, FWD_LATE, BWD_MIDDLE, BWD_LATE = 5, 6, 5, 6
-MROWS = 384
-RING = 2
-DEPTH = 5
+FWD_MIDDLE, FWD_LATE, BWD_MIDDLE, BWD_LATE = 6, 7, 5, 6
+MROWS = 768
+RING = 4
+DEPTH = 3
 COPY_ROWS = 24
 ROW_STEPS = 8
 F32 = jnp.float32
@@ -441,7 +441,7 @@
 def products_kernel(heads, ot_ref, ht_ref, dy_ref, d_kv_ref, d_qa_ref, d_qb_ref, x_ref, own_dy_ref, gain_ref, wo_ref, wk_ref, wv_ref, wq_ref,
                     wo_out, wq_out, kv_all, qa_all, qb_all, res_ref, gx_ref, gg_ref,
                     a_buf, b_buf, tile, a_sem, b_sems, t_sems, x_sems, stage, stage_sems, ot_v, o_v, x_v, io_sems, own, own_sems, w_v, w_sems, acc,
-                    gg_v, gg_all, gg_sems, kv_sems, qa_sems, qb_sems):
+                    gg_v, gg_row, gg_all, gg_sems, kv_sems, qa_sems, qb_sems):
     near = Neighbours()
     core = lax.rem(near.me, 2)
     half = a_buf.shape[0]
@@ -717,8 +717,9 @@
         mean = jnp.mean(both * gain, axis=-1, keepdims=True)
         o_v[at, :] = (o_v[at, :].astype(F32) + inv_rms * (d_hid * gain - normed * mean)).astype(BF16)
 
-    gg_all[near.me] = gg_v[...]
-    parts = [send(gg_v, gg_all.at[near.me], gg_sems, r, peer) for r, peer in enumerate(others)]
+    gg_row[...] = jnp.sum(gg_v[...], axis=0, keepdims=True)
+    gg_all[near.me] = gg_row[...]
+    parts = [send(gg_row, gg_all.at[near.me], gg_sems, r, peer) for r, peer in enumerate(others)]
     for copy in parts:
         copy.start()
     gx_store.start()
@@ -729,7 +730,7 @@
 
     for copy in parts:
         copy.wait()
-    gg_ref[...] = jnp.sum(jnp.sum(gg_all[...], axis=0), axis=0, keepdims=True)
+    gg_ref[...] = jnp.sum(gg_all[...], axis=0)
     gx_store.wait()
 
 
@@ -753,7 +754,7 @@
                         pltpu.VMEM((ot_all.shape[0], x.shape[0]), BF16), pltpu.VMEM((x.shape[0], ot_all.shape[0]), BF16), pltpu.VMEM(x.shape, BF16),
                         dma((4,)), pltpu.VMEM((sp_size, x.shape[0], 2 * HEAD_DIM), BF16), dma((sp_size, 2)),
                         pltpu.VMEM((2, width, 2 * HEAD_DIM), BF16), dma((2, 2)), pltpu.VMEM(x.shape, F32),
-                        pltpu.VMEM((8, width), F32), pltpu.VMEM((sp_size, 8, width), F32), dma((2, 7)), SEMS, SEMS, SEMS],
+                        pltpu.VMEM((8, width), F32), pltpu.VMEM((1, width), F32), pltpu.VMEM((sp_size, 1, width), F32), dma((2, 7)), SEMS, SEMS, SEMS],
         compiler_params=pltpu.CompilerParams(vmem_limit_bytes=VMEM_LIMIT, collective_id=1, has_side_effects=True),
         cost_estimate=pl.CostEstimate(flops=2 * half * cols * seq_len * n_all, bytes_accessed=8 * half * cols * n_all, transcendentals=0),
         name="products",
@@ -763,16 +764,23 @@
 def finish_kernel(ht_ref, d_ref, gx_in, res_in, gg_in, wo_in, wq_in, wk_ref, wv_ref, wq_ref, wo_ref, gx_ref, res_ref, gg_ref, d_v, d_sems, ring, ring_sems):
     step = pl.program_id(0) * pl.num_programs(1) + pl.program_id(1)
     high = ring.shape[2]
-    every = [(src, dst, r) for src, dst in ((wo_in, wo_ref), (wq_in, wq_ref)) for r in range(src.shape[0] // high)]
-    groups = [every[g:g + RING] for g in range(0, len(every), RING)]
-
-    def ins(g):
-        return [pltpu.make_async_copy(src.at[pl.ds(r * high, high), :], ring.at[g % DEPTH, n], ring_sems.at[0, g % DEPTH, n])
-                for n, (src, dst, r) in enumerate(groups[g])]
-
-    def outs(g):
-        return [pltpu.make_async_copy(ring.at[g % DEPTH, n], dst.at[pl.ds(r * high, high), :], ring_sems.at[1, g % DEPTH, n])
-                for n, (src, dst, r) in enumerate(groups[g])]
+    per_array = wo_in.shape[0] // (high * RING)
+    count = 2 * per_array
+
+    def copy_in(src, g, n):
+        at = pl.ds(pl.multiple_of((lax.rem(g, per_array) * RING + n) * high, high), high)
+        return pltpu.make_async_copy(src.at[at, :], ring.at[lax.rem(g, DEPTH), n], ring_sems.at[0, lax.rem(g, DEPTH), n])
+
+    def copy_out(dst, g, n):
+        at = pl.ds(pl.multiple_of((lax.rem(g, per_array) * RING + n) * high, high), high)
+        return pltpu.make_async_copy(ring.at[lax.rem(g, DEPTH), n], dst.at[at, :], ring_sems.at[1, lax.rem(g, DEPTH), n])
+
+    def start(copy, first, second, g):
+        for ref, mine in ((first, g < per_array), (second, g >= per_array)):
+            @pl.when(mine)
+            def _():
+                for n in range(RING):
+                    copy(ref, g, n).start()
 
     def pair_load(p):
         at = pl.ds(2 * p, 2)
@@ -783,20 +791,20 @@
         for p in range(d_v.shape[0] // 2):
             pair_load(p).start()
 
-    for g in range(len(groups) + DEPTH):
-        @pl.when(step == g)
-        def _():
-            if g >= DEPTH:
-                for copy in outs(g - DEPTH):
-                    copy.wait()
-            if g < len(groups):
-                for copy in ins(g):
-                    copy.start()
-            if 2 <= g < len(groups) + 2:
-                for copy in ins(g - 2):
-                    copy.wait()
-                for copy in outs(g - 2):
-                    copy.start()
+    @pl.when(jnp.logical_and(step >= DEPTH, step < count + DEPTH))
+    def _():
+        for n in range(RING):
+            copy_out(wo_ref, step - DEPTH, n).wait()
+
+    @pl.when(step < count)
+    def _():
+        start(copy_in, wo_in, wq_in, step)
+
+    @pl.when(jnp.logical_and(step >= 1, step < count + 1))
+    def _():
+        for n in range(RING):
+            copy_in(wo_in, step - 1, n).wait()
+        start(copy_out, wo_ref, wq_ref, step - 1)
 
     for p in range(d_v.shape[0] // 2):
         @pl.when(step == p)

time: 614 us -> 606 us (0.987)
  Pallas kernels: 610 us -> 603 us
    pallas_call x1, Pallas kernels: 197 us -> 190 us  [products(): pl.pallas_call(functools.partial(products_kernel, heads), in_specs=[any_s...]
where the time goes in v5:
time: 606 us; the launch traced here: 605 us
  Pallas kernels  603 us (100%)
    pallas_call x1, Pallas kernels, attention(): pl.pallas_call(functools.partial(attention_kernel, heads), in_specs=[any_...  326 us
    pallas_call x1, Pallas kernels, products(): pl.pallas_call(functools.partial(products_kernel, heads), in_specs=[any_s...  190 us
    pallas_call x1, Pallas kernels, finish(): pl.pallas_call(finish_kernel, grid=(width // MROWS, n_j), in_specs=[pl.Bl...  87.5 us

profile of v5, /device:TPU:0, one launch (start us, length us, event | category | flops | bytes accessed | tf_op | source)
XLA Modules:
  0.0 605.4 jit_solution(659794398827035950)
XLA Ops:
  0.6 1.3 reshape.27.gain_ref
  1.9 325.5 %attention.1 = (bf16[4096,3072]{1,0:T(8,128)(2,1)}, bf16[4096,3072]{1,0:T(8,128)(2,1)}, bf16[3072,4096]{1,0:T(8,128)(2,1)}, bf16[3072,4096]{1,0:T(8,128)(2,1)}, ...) custom-call(bf16[512,3072]{1,0:T(8,128)(2,1)} %x_ref.3, ...), custom_call_target="tpu_custom_call" | custom-call | flops 101468602368 | bytes 251658240 | tf_op jit(solution)/shard_map/attention/pallas_call | solution.py:417
  327.5 190.2 %products.1 = (f32[3072,3072]{1,0:T(8,128)}, f32[3072,3072]{1,0:T(8,128)}, bf16[32768,256]{1,0:T(8,128)(2,1)}, bf16[32768,256]{1,0:T(8,128)(2,1)}, bf16[32768,12...) custom-call(bf16[3072,4096]{1,0:T(8,128)(2,1)} %get-tuple-element.27.ot_ref, ...), custom_call_target="tpu_custom_call" | custom-call | flops 77309411328 | bytes 75497472 | tf_op jit(solution)/shard_map/products/pallas_call | solution.py:746
  517.7 87.5 %finish.1 = (f32[3072,1024]{1,0:T(8,128)}, f32[3072,1024]{1,0:T(8,128)}, f32[3072,3072]{1,0:T(8,128)}, f32[3072,3072]{1,0:T(8,128)}, bf16[512,3072]{1,0:T(8,128)...) custom-call(bf16[3072,4096]{1,0:T(8,128)(2,1)} %get-tuple-element.26.ht_ref, bf16[8,4096,256]{2,1,0:T(8,128)(2,1)} %bitcast.4, ...), custom_call_target="tpu_custom_call" | custom-call | flops 51539607552 | bytes 25165824 | tf_op jit(solution)/shard_map/finish/pallas_call | solution.py:842

commit v6 on v5

--- a/solution.py
+++ b/solution.py
@@ -18,9 +18,10 @@
 CHUNKS = 4
 FWD_MIDDLE, FWD_LATE, BWD_MIDDLE, BWD_LATE = 6, 7, 5, 6
 MROWS = 768
-RING = 4
+RING = 3
 DEPTH = 3
 COPY_ROWS = 24
+PARTS = 3
 ROW_STEPS = 8
 F32 = jnp.float32
 BF16 = jnp.bfloat16
@@ -157,11 +158,10 @@
     return (val * cos_t - pltpu.roll(val, HALF, 1) * sin_t).astype(BF16)
 
 
-def attention_kernel(heads, x_ref, gain_ref, pos_ref, freq_ref, dy_ref, wq_ref, wk_ref, wv_ref, wo_ref,
-                     h_all, dy_all, o_all, ht_ref, dkv_ref, dq_a_ref, dq_b_ref,
-                     x_v, h_v, x_sems, own_sems, pos_all, pos_sems, cos_s, sin_s, w_v, wo_v, w_sems, blk, blk_sems, ht_v, ht_sems,
-                     q_s, k_s, v_s, vt, kt, ot_s, lse_s, acc, do_s, dk_acc, dv_acc, dq_v, dq_sems, dkv_v, h_sems, dy_sems, o_sems):
-    near = Neighbours()
+def attention_part(heads, near, gather_next, x_ref, gain_ref, pos_ref, freq_ref, dy_ref, wq_ref, wk_ref, wv_ref, wo_ref,
+                   h_all, dy_all, o_all, ht_ref, dkv_ref, dq_a_ref, dq_b_ref, pos_all, pos_sems, h_sems, dy_sems, o_sems,
+                   x_v, h_v, x_sems, own_sems, cos_s, sin_s, w_v, wo_v, w_sems, blk, blk_sems, ht_v, ht_sems,
+                   q_s, k_s, v_s, vt, kt, ot_s, lse_s, acc, do_s, dk_acc, dv_acc, dq_v, dq_sems, dkv_v):
     rows, width = x_ref.shape
     n_blocks = k_s.shape[0]
     q_cols = heads * HEAD_DIM
@@ -386,6 +386,12 @@
         def _():
             gather_o.late()
 
+    for i in (n_blocks - 2, n_blocks - 1):
+        for store in dq_stores(i):
+            store.wait()
+    for chunk in range(CHUNKS):
+        gather_next.start(chunk)
+
     @pl.loop(0, n_blocks)
     def _(c):
         at = pl.ds(pl.multiple_of(c * rows, rows), rows)
@@ -396,67 +402,26 @@
     dkv_store.start()
     own_o.wait()
     gather_o.end()
-    for i in (n_blocks - 2, n_blocks - 1):
-        for store in dq_stores(i):
-            store.wait()
     dkv_store.wait()
-
-
-def attention(x, gain, positions, grad_out, w_q, w_k, w_v, w_o, sp_size, heads):
-    rows, width = x.shape
-    seq_len = rows * sp_size
-    q_cols = heads * HEAD_DIM
-    any_spec = pl.BlockSpec(memory_space=pl.ANY)
-    vmem = pl.BlockSpec(memory_space=pltpu.VMEM)
-    dma = pltpu.SemaphoreType.DMA
-    inv_freq = ROPE_THETA ** (-np.arange(0, HEAD_DIM, 2) / HEAD_DIM)
-    freq = jnp.asarray(np.concatenate([inv_freq, inv_freq])[None, :], F32)
-    pairs = heads * seq_len * (seq_len + rows) // 2
-    out = lambda *shape: jax.ShapeDtypeStruct(shape, BF16)
-    blocks = lambda *shape, dtype=BF16: pltpu.VMEM((sp_size,) + shape, dtype)
-    return pl.pallas_call(
-        functools.partial(attention_kernel, heads),
-        in_specs=[any_spec, vmem, vmem, vmem] + [any_spec] * 5,
-        out_specs=[any_spec] * 7,
-        out_shape=[out(seq_len, width), out(seq_len, width), out(q_cols * sp_size, seq_len), out(width, seq_len), out(seq_len, 2 * HEAD_DIM),
-                   out(seq_len, q_cols - HEAD_DIM), out(seq_len, HEAD_DIM)],
-        scratch_shapes=[pltpu.VMEM((rows, width), BF16), pltpu.VMEM((rows, width), BF16), dma((CHUNKS,)), dma((3,)),
-                        blocks(8, rows, dtype=jnp.int32), dma((2, 7)), blocks(rows, HEAD_DIM, dtype=F32), blocks(rows, HEAD_DIM, dtype=F32),
-                        pltpu.VMEM((width, q_cols + 2 * HEAD_DIM), BF16), pltpu.VMEM((q_cols, width), BF16), dma((4,)),
-                        pltpu.VMEM((2, rows, width), BF16), dma((2,)), pltpu.VMEM((2, width, rows), BF16), dma((2,)),
-                        blocks(rows, q_cols), blocks(rows, HEAD_DIM), blocks(rows, HEAD_DIM), blocks(HEAD_DIM, rows), blocks(HEAD_DIM, rows),
-                        pltpu.VMEM((q_cols, seq_len), BF16), blocks(8, rows, dtype=F32), pltpu.VMEM((heads, HEAD_DIM, rows), F32),
-                        blocks(rows, q_cols), blocks(rows, HEAD_DIM, dtype=F32), blocks(rows, HEAD_DIM, dtype=F32),
-                        pltpu.VMEM((2, rows, q_cols), BF16), dma((2, 2)), pltpu.VMEM((seq_len, 2 * HEAD_DIM), BF16), SEMS, SEMS, SEMS],
-        compiler_params=pltpu.CompilerParams(vmem_limit_bytes=VMEM_LIMIT, collective_id=0, has_side_effects=True),
-        cost_estimate=pl.CostEstimate(flops=28 * pairs * HEAD_DIM, bytes_accessed=20 * seq_len * width, transcendentals=2 * pairs),
-        name="attention",
-    )(x, gain.reshape(1, -1), positions.reshape(1, -1), freq, grad_out, w_q, w_k, w_v, w_o)
 
 
 def lanes(*parts):
     return jnp.concatenate(parts, axis=1)
 
 
-def products_kernel(heads, ot_ref, ht_ref, dy_ref, d_kv_ref, d_qa_ref, d_qb_ref, x_ref, own_dy_ref, gain_ref, wo_ref, wk_ref, wv_ref, wq_ref,
-                    wo_out, wq_out, kv_all, qa_all, qb_all, res_ref, gx_ref, gg_ref,
-                    a_buf, b_buf, tile, a_sem, b_sems, t_sems, x_sems, stage, stage_sems, ot_v, o_v, x_v, io_sems, own, own_sems, w_v, w_sems, acc,
-                    gg_v, gg_row, gg_all, gg_sems, kv_sems, qa_sems, qb_sems):
-    near = Neighbours()
+def products_part(heads, near, gathers, ot_ref, ht_ref, dy_ref, d_kv_ref, d_qa_ref, d_qb_ref, x_ref, own_dy_ref, gain_ref, wo_ref, wk_ref, wv_ref, wq_ref,
+                  wo_out, wq_out, kv_all, qa_all, qb_all, res_ref, gx_ref, gg_ref, gg_row, gg_all, gg_sems, x_sems,
+                  a_buf, b_buf, tile, a_sem, b_sems, t_sems, stage, stage_sems, ot_v, o_v, x_v, io_sems, own, own_sems, w_v, w_sems, acc,
+                  gg_v):
     core = lax.rem(near.me, 2)
     half = a_buf.shape[0]
     seq_len = d_kv_ref.shape[0]
     rows, width = x_ref.shape
-    chunk = seq_len // CHUNKS
     n_cols = d_kv_ref.shape[1]
     n_o, n_all = width // (2 * n_cols), x_sems.shape[1]
     n_oa = n_o + (n_all - n_o) * 2 // 3
 
-    def gather_of(src, dst, sems):
-        return Gather(near, lambda c: src.at[pl.ds(c * chunk, chunk), :], dst, seq_len, sems)
-
     local = (d_qa_ref, d_qb_ref, d_kv_ref)
-    gathers = [gather_of(d_qa_ref, qa_all, qa_sems), gather_of(d_qb_ref, qb_all, qb_sems), gather_of(d_kv_ref, kv_all, kv_sems)]
 
     def stage_in(n):
         return pltpu.make_async_copy(local[n], stage.at[:, pl.ds(0, local[n].shape[1])], stage_sems.at[0])
@@ -600,22 +565,10 @@
                 for g in range(2):
                     w_load(r + 1, g).start()
 
-            prod = dot(own[r], w_v[lax.rem(r, 2)], COLS_COLS)
-            if kind == 0:
-                @pl.when(r == 0)
-                def _():
-                    acc[...] = prod
-
-                @pl.when(r > 0)
-                def _():
-                    acc[...] += prod
-            else:
-                acc[...] += prod
-
-    others = near.others()
-    near.meet(others)
-    for c in range(CHUNKS):
-        gathers[0].start(c)
+            for col in range(0, width, width // PARTS):
+                at = slice(col, col + width // PARTS)
+                acc[:, at] += dot(own[r], w_v[lax.rem(r, 2), at, :], COLS_COLS)
+
     a_load(ot_ref).start()
     start_b(jnp.int32(0))
     stage_in(0).start()
@@ -641,11 +594,13 @@
         def _():
             a_load(ht_ref).wait()
 
-        tile[slot] = dot(a_buf[...], b_buf[slot])
+        for r in range(0, half, half // PARTS):
+            tile[slot, r:r + half // PARTS, :] = dot(a_buf[r:r + half // PARTS, :], b_buf[slot])
         start_tile(step)
 
-        @pl.when(step == n_o - 2)
-        def _():
+        @pl.when(step == n_o - 3)
+        def _():
+            acc[...] = jnp.zeros_like(acc)
             copy_own(0)
             gathers[0].middle()
 
@@ -719,7 +674,7 @@
 
     gg_row[...] = jnp.sum(gg_v[...], axis=0, keepdims=True)
     gg_all[near.me] = gg_row[...]
-    parts = [send(gg_row, gg_all.at[near.me], gg_sems, r, peer) for r, peer in enumerate(others)]
+    parts = [send(gg_row, gg_all.at[near.me], gg_sems, r, peer) for r, peer in enumerate(near.others())]
     for copy in parts:
         copy.start()
     gx_store.start()
@@ -734,38 +689,78 @@
     gx_store.wait()
 
 
-def products(ot_all, ht, d_out, d_kv, d_qa, d_qb, x, grad_out, gain, w_o, w_k, w_v, w_q, sp_size, heads):
-    width, seq_len = ht.shape
+def step_kernel(heads, first_scratch, second_scratch, x_ref, gain_ref, pos_ref, freq_ref, dy_ref, wq_ref, wk_ref, wv_ref, wo_ref,
+                h_all, dy_all, o_all, ht, d_kv, d_qa, d_qb, wo_out, wq_out, kv_all, qa_all, qb_all, res, gx, gg,
+                pos_all, pos_sems, gg_row, gg_all, gg_sems, x_sems, h_sems, dy_sems, o_sems, kv_sems, qa_sems, qb_sems):
+    near = Neighbours()
+    seq_len = d_kv.shape[0]
+
+    def gather_of(src, dst, sems):
+        return Gather(near, lambda c: src.at[pl.ds(c * (seq_len // CHUNKS), seq_len // CHUNKS), :], dst, seq_len, sems)
+
+    gathers = [gather_of(d_qa, qa_all, qa_sems), gather_of(d_qb, qb_all, qb_sems), gather_of(d_kv, kv_all, kv_sems)]
+
+    def first(*scratch):
+        attention_part(heads, near, gathers[0], x_ref, gain_ref, pos_ref, freq_ref, dy_ref, wq_ref, wk_ref, wv_ref, wo_ref,
+                       h_all, dy_all, o_all, ht, d_kv, d_qa, d_qb, pos_all, pos_sems, h_sems, dy_sems, o_sems, *scratch)
+
+    def second(*scratch):
+        products_part(heads, near, gathers, o_all, ht, dy_all, d_kv, d_qa, d_qb, x_ref, dy_ref, gain_ref, wo_ref, wk_ref, wv_ref, wq_ref,
+                      wo_out, wq_out, kv_all, qa_all, qb_all, res, gx, gg, gg_row, gg_all, gg_sems, x_sems, *scratch)
+
+    pl.run_scoped(first, *first_scratch)
+    pl.run_scoped(second, *second_scratch)
+
+
+def step(x, gain, positions, grad_out, w_q, w_k, w_v, w_o, sp_size, heads):
+    rows, width = x.shape
+    seq_len = rows * sp_size
+    q_cols = heads * HEAD_DIM
+    all_cols = q_cols * sp_size
     half = width // 2
-    cols = 2 * d_kv.shape[1]
-    n_all = width // cols + sp_size * (d_qa.shape[1] + d_qb.shape[1]) // cols
+    cols = 4 * HEAD_DIM
+    n_all = (width + all_cols) // cols
     any_spec = pl.BlockSpec(memory_space=pl.ANY)
     vmem = pl.BlockSpec(memory_space=pltpu.VMEM)
     dma = pltpu.SemaphoreType.DMA
-    gathered = [jax.ShapeDtypeStruct((sp_size * seq_len, d.shape[1]), BF16) for d in (d_kv, d_qa, d_qb)]
+    inv_freq = ROPE_THETA ** (-np.arange(0, HEAD_DIM, 2) / HEAD_DIM)
+    freq = jnp.asarray(np.concatenate([inv_freq, inv_freq])[None, :], F32)
+    pairs = heads * seq_len * (seq_len + rows) // 2
+    out = lambda *shape, dtype=BF16: jax.ShapeDtypeStruct(shape, dtype)
+    array = lambda *shape, dtype=BF16: pltpu.VMEM(shape, dtype)
+    blocks = lambda *shape, dtype=BF16: pltpu.VMEM((sp_size,) + shape, dtype)
+    first_scratch = [array(rows, width), array(rows, width), dma((CHUNKS,)), dma((3,)), blocks(rows, HEAD_DIM, dtype=F32),
+                     blocks(rows, HEAD_DIM, dtype=F32), array(width, q_cols + 2 * HEAD_DIM), array(q_cols, width), dma((4,)),
+                     array(2, rows, width), dma((2,)), array(2, width, rows), dma((2,)),
+                     blocks(rows, q_cols), blocks(rows, HEAD_DIM), blocks(rows, HEAD_DIM), blocks(HEAD_DIM, rows), blocks(HEAD_DIM, rows),
+                     array(q_cols, seq_len), blocks(8, rows, dtype=F32), array(heads, HEAD_DIM, rows, dtype=F32),
+                     blocks(rows, q_cols), blocks(rows, HEAD_DIM, dtype=F32), blocks(rows, HEAD_DIM, dtype=F32),
+                     array(2, rows, q_cols), dma((2, 2)), array(seq_len, 2 * HEAD_DIM)]
+    second_scratch = [array(half, seq_len), array(2, seq_len, cols), array(2, half, cols, dtype=F32), dma, dma((2, 2)), dma((2,)),
+                      array(seq_len, 2 * HEAD_DIM), dma((2,)), array(all_cols, rows), array(rows, all_cols), array(rows, width),
+                      dma((4,)), blocks(rows, 2 * HEAD_DIM), dma((sp_size, 2)), array(2, width, 2 * HEAD_DIM), dma((2, 2)),
+                      array(rows, width, dtype=F32), array(8, width, dtype=F32)]
     return pl.pallas_call(
-        functools.partial(products_kernel, heads),
-        in_specs=[any_spec] * 8 + [vmem] + [any_spec] * 4,
-        out_specs=[any_spec] * 7 + [vmem],
-        out_shape=[jax.ShapeDtypeStruct((ot_all.shape[0], width), F32), jax.ShapeDtypeStruct(w_q.shape, F32)] + gathered
-        + [jax.ShapeDtypeStruct(x.shape, BF16), jax.ShapeDtypeStruct(x.shape, BF16), jax.ShapeDtypeStruct((1, width), F32)],
-        scratch_shapes=[pltpu.VMEM((half, seq_len), BF16), pltpu.VMEM((2, seq_len, cols), BF16), pltpu.VMEM((2, half, cols), F32),
-                        dma, dma((2, 2)), dma((2,)), dma((2, n_all)), pltpu.VMEM(d_kv.shape, BF16), dma((2,)),
-                        pltpu.VMEM((ot_all.shape[0], x.shape[0]), BF16), pltpu.VMEM((x.shape[0], ot_all.shape[0]), BF16), pltpu.VMEM(x.shape, BF16),
-                        dma((4,)), pltpu.VMEM((sp_size, x.shape[0], 2 * HEAD_DIM), BF16), dma((sp_size, 2)),
-                        pltpu.VMEM((2, width, 2 * HEAD_DIM), BF16), dma((2, 2)), pltpu.VMEM(x.shape, F32),
-                        pltpu.VMEM((8, width), F32), pltpu.VMEM((1, width), F32), pltpu.VMEM((sp_size, 1, width), F32), dma((2, 7)), SEMS, SEMS, SEMS],
-        compiler_params=pltpu.CompilerParams(vmem_limit_bytes=VMEM_LIMIT, collective_id=1, has_side_effects=True),
-        cost_estimate=pl.CostEstimate(flops=2 * half * cols * seq_len * n_all, bytes_accessed=8 * half * cols * n_all, transcendentals=0),
-        name="products",
-    )(ot_all, ht, d_out, d_kv, d_qa, d_qb, x, grad_out, gain, w_o, w_k, w_v, w_q)
+        functools.partial(step_kernel, heads, first_scratch, second_scratch),
+        in_specs=[any_spec, vmem, vmem, vmem] + [any_spec] * 5,
+        out_specs=[any_spec] * 14 + [vmem],
+        out_shape=[out(seq_len, width), out(seq_len, width), out(all_cols, seq_len), out(width, seq_len), out(seq_len, 2 * HEAD_DIM),
+                   out(seq_len, q_cols - HEAD_DIM), out(seq_len, HEAD_DIM), out(all_cols, width, dtype=F32), out(width, all_cols, dtype=F32),
+                   out(sp_size * seq_len, 2 * HEAD_DIM), out(sp_size * seq_len, q_cols - HEAD_DIM), out(sp_size * seq_len, HEAD_DIM),
+                   out(rows, width), out(rows, width), out(1, width, dtype=F32)],
+        scratch_shapes=[blocks(8, rows, dtype=jnp.int32), dma((2, 7)), array(1, width, dtype=F32), blocks(1, width, dtype=F32), dma((2, 7)),
+                        dma((2, n_all))] + [SEMS] * 6,
+        compiler_params=pltpu.CompilerParams(vmem_limit_bytes=VMEM_LIMIT, collective_id=0, has_side_effects=True),
+        cost_estimate=pl.CostEstimate(flops=28 * pairs * HEAD_DIM + 2 * half * cols * seq_len * n_all, bytes_accessed=20 * seq_len * width,
+                                      transcendentals=2 * pairs),
+        name="step",
+    )(x, gain, positions.reshape(1, -1), freq, grad_out, w_q, w_k, w_v, w_o)
 
 
 def finish_kernel(ht_ref, d_ref, gx_in, res_in, gg_in, wo_in, wq_in, wk_ref, wv_ref, wq_ref, wo_ref, gx_ref, res_ref, gg_ref, d_v, d_sems, ring, ring_sems):
     step = pl.program_id(0) * pl.num_programs(1) + pl.program_id(1)
     high = ring.shape[2]
     per_array = wo_in.shape[0] // (high * RING)
-    count = 2 * per_array
 
     def copy_in(src, g, n):
         at = pl.ds(pl.multiple_of((lax.rem(g, per_array) * RING + n) * high, high), high)
@@ -791,20 +786,26 @@
         for p in range(d_v.shape[0] // 2):
             pair_load(p).start()
 
-    @pl.when(jnp.logical_and(step >= DEPTH, step < count + DEPTH))
+    last = pl.num_programs(0) * pl.num_programs(1) - 1
+
+    def free(g):
+        for n in range(RING):
+            copy_out(wo_ref, g, n).wait()
+
+    def pass_on(g):
+        for n in range(RING):
+            copy_in(wo_in, g, n).wait()
+        start(copy_out, wo_ref, wq_ref, g)
+
+    @pl.when(step >= DEPTH)
     def _():
-        for n in range(RING):
-            copy_out(wo_ref, step - DEPTH, n).wait()
-
-    @pl.when(step < count)
+        free(step - DEPTH)
+
+    start(copy_in, wo_in, wq_in, step)
+
+    @pl.when(step >= 1)
     def _():
-        start(copy_in, wo_in, wq_in, step)
-
-    @pl.when(jnp.logical_and(step >= 1, step < count + 1))
-    def _():
-        for n in range(RING):
-            copy_in(wo_in, step - 1, n).wait()
-        start(copy_out, wo_ref, wq_ref, step - 1)
+        pass_on(step - 1)
 
     for p in range(d_v.shape[0] // 2):
         @pl.when(step == p)
@@ -819,6 +820,12 @@
     @pl.when(step == 0)
     def _():
         gg_ref[...] = gg_in[...]
+
+    @pl.when(step == last)
+    def _():
+        pass_on(last)
+        for back in range(DEPTH):
+            free(last - back)
 
     @pl.when(step < ROW_STEPS)
     def _():
@@ -832,7 +839,7 @@
     n_j = groups // 2
     steps = (width // MROWS) * n_j
     high = width // COPY_ROWS
-    assert -(-(w_o_grad.shape[0] + w_q_grad.shape[0]) // (high * RING)) + DEPTH <= steps
+    assert w_o_grad.shape[0] + w_q_grad.shape[0] == high * RING * steps
     any_spec = pl.BlockSpec(memory_space=pl.ANY)
     rows = pl.BlockSpec((grad_x.shape[0] // ROW_STEPS, width), lambda m, j: (jnp.minimum(m * n_j + j, ROW_STEPS - 1), 0))
     whole = pl.BlockSpec((1, width), lambda m, j: (0, 0))
@@ -863,10 +870,8 @@
     def local_step(x, grad_out, positions, gain, w_q, w_k, w_v, w_o):
         n_heads = w_q.shape[1] // HEAD_DIM
         heads = n_heads // sp_size
-        _, d_out, ot_all, ht, *grads = attention(x, gain, positions, grad_out, w_q, w_k, w_v, w_o, sp_size, heads)
-        gain = gain.reshape(1, -1)
-        w_o_grad, w_q_grad, kv_all, _, _, result, grad_x, grad_gain = products(ot_all, ht, d_out, *grads, x, grad_out, gain, w_o, w_k, w_v, w_q,
-                                                                               sp_size, heads)
+        _, _, _, ht, _, _, _, w_o_grad, w_q_grad, kv_all, _, _, result, grad_x, grad_gain = step(
+            x, gain.reshape(1, -1), positions, grad_out, w_q, w_k, w_v, w_o, sp_size, heads)
         grad_wk, grad_wv, grad_wq, grad_wo, grad_x, result, grad_gain = finish(
             ht, kv_all.reshape(sp_size, -1, 2 * HEAD_DIM), w_o_grad, w_q_grad, grad_x, result, grad_gain)
         return result, grad_x, grad_wq, grad_wk, grad_wv, grad_wo, grad_gain.reshape(-1)

time: 606 us -> 600 us (0.990)
    pallas_call x2 -> x1, Pallas kernels: 516 us -> 512 us  [step(): pl.pallas_call(functools.partial(step_kernel, heads, first_scratch, secon...]
where the time goes in v6:
time: 600 us; the launch traced here: 599 us
  Pallas kernels  597 us (100%)
    pallas_call x1, Pallas kernels, step(): pl.pallas_call(functools.partial(step_kernel, heads, first_scratch, secon...  512 us
    pallas_call x1, Pallas kernels, finish(): pl.pallas_call(finish_kernel, grid=(width // MROWS, n_j), in_specs=[pl.Bl...  85.2 us

profile of v6, /device:TPU:0, one launch (start us, length us, event | category | flops | bytes accessed | tf_op | source)
XLA Modules:
  0.0 599.0 jit_solution(11139858954218100517)
XLA Ops:
  0.6 1.3 reshape.26.gain_ref
  1.9 511.6 %step.1 = (bf16[4096,3072]{1,0:T(8,128)(2,1)}, bf16[4096,3072]{1,0:T(8,128)(2,1)}, bf16[3072,4096]{1,0:T(8,128)(2,1)}, bf16[3072,4096]{1,0:T(8,128)(2,1)}, bf16[...) custom-call(bf16[512,3072]{1,0:T(8,128)(2,1)} %x_ref.1, ...), custom_call_target="tpu_custom_call" | custom-call | flops 178778013696 | bytes 251658240 | tf_op jit(solution)/shard_map/step/pallas_call | solution.py:743
  513.6 85.2 %finish.1 = (f32[3072,1024]{1,0:T(8,128)}, f32[3072,1024]{1,0:T(8,128)}, f32[3072,3072]{1,0:T(8,128)}, f32[3072,3072]{1,0:T(8,128)}, bf16[512,3072]{1,0:T(8,128)...) custom-call(bf16[3072,4096]{1,0:T(8,128)(2,1)} %get-tuple-element.21.ht_ref, bf16[8,4096,256]{2,1,0:T(8,128)(2,1)} %bitcast.4, ...), custom_call_target="tpu_custom_call" | custom-call | flops 51539607552 | bytes 25165824 | tf_op jit(solution)/shard_map/finish/pallas_call | solution.py:849

commit v7 on v6

--- a/solution.py
+++ b/solution.py
@@ -16,7 +16,7 @@
 LOG2E = 1.4426950408889634
 BLK = 512
 CHUNKS = 4
-FWD_MIDDLE, FWD_LATE, BWD_MIDDLE, BWD_LATE = 6, 7, 5, 6
+FWD_MIDDLE, FWD_LATE, BWD_MIDDLE = 6, 7, 31
 MROWS = 768
 RING = 3
 DEPTH = 3
@@ -121,9 +121,11 @@
             self.first(chunk, 1).wait_recv()
         self.share(1).start()
 
-    def end_near(self):
+    def end_sib(self):
         for chunk in range(CHUNKS):
             self.first(chunk, 2).wait_recv()
+
+    def end_near(self):
         for kind in range(2):
             self.share(kind).wait_recv()
 
@@ -141,6 +143,7 @@
             self.share_diag(chunk).wait()
 
     def end(self):
+        self.end_sib()
         self.end_near()
         self.end_far()
 
@@ -303,26 +306,6 @@
     own_o = pltpu.make_async_copy(ot_s, gather_o.block(near.me, 0, CHUNKS), own_sems.at[0])
     own_o.start()
 
-    def d_o_blocks(low, high):
-        block_load(dy_all, near.across(low), 0).start()
-
-        @pl.loop(low, high)
-        def _(r):
-            slot = lax.rem(r - low, 2)
-            block_load(dy_all, 0, slot).wait()
-
-            @pl.when(r + 1 < high)
-            def _():
-                block_load(dy_all, near.across(r + 1), 1 - slot).start()
-
-            do_s[near.across(r)] = dot(blk[slot], wo_v[...], COLS_COLS).astype(BF16)
-
-    stage_out.wait()
-    gather_dy.end_near()
-    d_o_blocks(0, n_blocks * 3 // 4)
-    gather_dy.end_far()
-    d_o_blocks(n_blocks * 3 // 4, n_blocks)
-
     def bwd_chunk(i, c, delta, diagonal):
         k_c, v_c, kt_c = k_s[c], v_s[c], kt[c]
         dk_c = dv_c = None
@@ -339,55 +322,83 @@
             dv_c = dv_a if dv_c is None else dv_c + dv_a
             dk_c = dk_a if dk_c is None else dk_c + dk_a
             acc[a] += dot(kt_c, d_s)
-        if diagonal:
-            dk_acc[c] = dk_c
-            dv_acc[c] = dv_c
-        else:
-            dk_acc[c] += dk_c
-            dv_acc[c] += dv_c
-
-    def dq_stores(i):
-        slot = lax.rem(i, 2)
-        at = pl.ds(pl.multiple_of(i * rows, rows), rows)
+        dk_acc[c] += dk_c
+        dv_acc[c] += dv_c
+
+    def dq_stores(r):
+        slot = lax.rem(r, 2)
+        at = pl.ds(pl.multiple_of(near.across(r) * rows, rows), rows)
         last = q_cols - HEAD_DIM
         return [pltpu.make_async_copy(dq_v.at[slot, :, pl.ds(0, last)], dq_a_ref.at[at, :], dq_sems.at[slot, 0]),
                 pltpu.make_async_copy(dq_v.at[slot, :, pl.ds(last, HEAD_DIM)], dq_b_ref.at[at, :], dq_sems.at[slot, 1])]
 
+    def pass_on(done):
+        @pl.when(done == BWD_MIDDLE)
+        def _():
+            gather_o.middle()
+
     for i in (n_blocks - 2, n_blocks - 1):
         ht_store(i).wait()
-
-    @pl.loop(0, n_blocks)
-    def _(i):
+    dk_acc[...] = jnp.zeros_like(dk_acc)
+    dv_acc[...] = jnp.zeros_like(dv_acc)
+    stage_out.wait()
+    block_load(dy_all, near.me, 0).start()
+
+    def bwd_block(r, done):
+        i = near.across(r)
+        slot = lax.rem(r, 2)
         at = pl.ds(pl.multiple_of(i * rows, rows), rows)
+
+        @pl.when(r == 1)
+        def _():
+            gather_dy.end_sib()
+
+        @pl.when(r == 2)
+        def _():
+            gather_dy.end_near()
+
+        @pl.when(r == n_blocks * 3 // 4)
+        def _():
+            gather_dy.end_far()
+
+        waits = [r == first for first in (1, 2, n_blocks * 3 // 4)]
+        @pl.when(functools.reduce(jnp.logical_or, waits))
+        def _():
+            block_load(dy_all, i, slot).start()
+
+        block_load(dy_all, 0, slot).wait()
+
+        @pl.when(functools.reduce(jnp.logical_and, [r + 1 != first for first in (1, 2, n_blocks * 3 // 4, n_blocks)]))
+        def _():
+            block_load(dy_all, near.across(r + 1), 1 - slot).start()
+
+        do_s[i] = dot(blk[slot], wo_v[...], COLS_COLS).astype(BF16)
         acc[...] = jnp.zeros_like(acc)
         delta = [jnp.sum(ot_s[cols[a], at].astype(F32) * do_s[i, :, cols[a]].T.astype(F32), axis=0, keepdims=True) for a in range(heads)]
 
         @pl.loop(0, i)
         def _(c):
             bwd_chunk(i, c, delta, False)
+            pass_on(done + c)
 
         bwd_chunk(i, i, delta, True)
-
-        @pl.when(i >= 2)
-        def _():
-            for store in dq_stores(i - 2):
+        pass_on(done + i)
+
+        @pl.when(r >= 2)
+        def _():
+            for store in dq_stores(r - 2):
                 store.wait()
 
         for a in range(heads):
-            dq_v[lax.rem(i, 2), :, cols[a]] = unrotate(acc[a].T * qk_scale, cos_s[i], sin_s[i])
-        for store in dq_stores(i):
+            dq_v[slot, :, cols[a]] = unrotate(acc[a].T * qk_scale, cos_s[i], sin_s[i])
+        for store in dq_stores(r):
             store.start()
-
-        @pl.when(i == BWD_MIDDLE)
-        def _():
-            gather_o.middle()
-
-        @pl.when(i == BWD_LATE)
-        def _():
-            gather_o.late()
-
-    for i in (n_blocks - 2, n_blocks - 1):
-        for store in dq_stores(i):
+        return done + i + 1
+
+    lax.fori_loop(0, n_blocks, bwd_block, jnp.int32(0))
+    gather_o.late()
+    for r in (n_blocks - 2, n_blocks - 1):
+        for store in dq_stores(r):
             store.wait()
     for chunk in range(CHUNKS):
         gather_next.start(chunk)
@@ -645,6 +656,7 @@
     gathers[2].middle()
     gathers[2].late()
     stage_out(2).wait()
+    gathers[2].end_sib()
     gathers[2].end_near()
     near_count = own.shape[0] * 3 // 4
     hidden_start(2, 0, near_count)

time: 600 us -> 616 us (1.027)
  Pallas kernels: 597 us -> 613 us
    pallas_call x1, Pallas kernels: 512 us -> 527 us  [step(): pl.pallas_call(functools.partial(step_kernel, heads, first_scratch, secon...]
where the time goes in v7:
time: 616 us; the launch traced here: 615 us
  Pallas kernels  613 us (100%)
    pallas_call x1, Pallas kernels, step(): pl.pallas_call(functools.partial(step_kernel, heads, first_scratch, secon...  527 us
    pallas_call x1, Pallas kernels, finish(): pl.pallas_call(finish_kernel, grid=(width // MROWS, n_j), in_specs=[pl.Bl...  85.2 us

profile of v7, /device:TPU:0, one launch (start us, length us, event | category | flops | bytes accessed | tf_op | source)
XLA Modules:
  0.0 614.8 jit_solution(18314550124322412297)
XLA Ops:
  0.6 1.3 reshape.26.gain_ref
  1.9 527.4 %step.1 = (bf16[4096,3072]{1,0:T(8,128)(2,1)}, bf16[4096,3072]{1,0:T(8,128)(2,1)}, bf16[3072,4096]{1,0:T(8,128)(2,1)}, bf16[3072,4096]{1,0:T(8,128)(2,1)}, bf16[...) custom-call(bf16[512,3072]{1,0:T(8,128)(2,1)} %x_ref.1, ...), custom_call_target="tpu_custom_call" | custom-call | flops 178778013696 | bytes 251658240 | tf_op jit(solution)/shard_map/step/pallas_call | solution.py:755
  529.4 85.2 %finish.1 = (f32[3072,1024]{1,0:T(8,128)}, f32[3072,1024]{1,0:T(8,128)}, f32[3072,3072]{1,0:T(8,128)}, f32[3072,3072]{1,0:T(8,128)}, bf16[512,3072]{1,0:T(8,128)...) custom-call(bf16[3072,4096]{1,0:T(8,128)(2,1)} %get-tuple-element.21.ht_ref, bf16[8,4096,256]{2,1,0:T(8,128)(2,1)} %bitcast.4, ...), custom_call_target="tpu_custom_call" | custom-call | flops 51539607552 | bytes 25165824 | tf_op jit(solution)/shard_map/finish/pallas_call | solution.py:861

commit v8 on v7

--- a/solution.py
+++ b/solution.py
@@ -16,7 +16,7 @@
 LOG2E = 1.4426950408889634
 BLK = 512
 CHUNKS = 4
-FWD_MIDDLE, FWD_LATE, BWD_MIDDLE = 6, 7, 31
+FWD_MIDDLE, BWD_MIDDLE = 5, 27
 MROWS = 768
 RING = 3
 DEPTH = 3
@@ -95,25 +95,21 @@
         rows = self.block(self.near.diag, chunk)
         return send(rows, rows, self.sems, 18 + chunk, self.near.sib)
 
-    def begin(self):
-        self.near.meet([self.near.sib, self.near.xn, self.near.yn])
+    def start(self):
         for chunk in range(CHUNKS):
-            self.start(chunk)
-
-    def start(self, chunk):
-        for kind in range(3):
-            self.first(chunk, kind).start()
+            for kind in (0, 1):
+                self.send_first(chunk, kind)
+            self.first(chunk, 2).start()
+
+    def send_first(self, turn, kind):
+        self.first(turn if kind == 0 else (turn + CHUNKS // 2) % CHUNKS, kind).start()
 
     def middle(self):
-        for chunk in (0, 1):
-            self.first(chunk, 0).wait_recv()
+        for chunk in (0, 2, 1, 3):
+            self.first(chunk, 0 if chunk < CHUNKS // 2 else 1).wait_recv()
             self.onward(chunk).start()
-        self.first(2, 1).wait_recv()
-        self.onward(2).start()
 
     def late(self):
-        self.first(3, 1).wait_recv()
-        self.onward(3).start()
         for chunk in (2, 3):
             self.first(chunk, 0).wait_recv()
         self.share(0).start()
@@ -129,10 +125,12 @@
         for kind in range(2):
             self.share(kind).wait_recv()
 
-    def end_far(self):
+    def end_far(self, between=None):
         for chunk in (0, 2, 1, 3):
             self.onward(chunk).wait_recv()
             self.share_diag(chunk).start()
+            if chunk == 2 and between:
+                between()
         for chunk in range(CHUNKS):
             for kind in range(3):
                 self.first(chunk, kind).wait_send()
@@ -142,10 +140,10 @@
         for chunk in range(CHUNKS):
             self.share_diag(chunk).wait()
 
-    def end(self):
+    def end(self, between=None):
         self.end_sib()
         self.end_near()
-        self.end_far()
+        self.end_far(between)
 
 
 SEMS = pltpu.SemaphoreType.DMA((2, Gather.COPIES))
@@ -185,7 +183,7 @@
     pos_all[near.me] = jnp.broadcast_to(pos_ref[...], pos_all.shape[1:])
     positions = [send(pos_ref, pos_all.at[near.me, pl.ds(0, 1), :], pos_sems, r, peer) for r, peer in enumerate(others)]
     gain = gain_ref[...].astype(F32)
-    for chunk in range(CHUNKS):
+    for turn, chunk in enumerate((0, 2, 1, 3)):
         loads[chunk].wait()
 
         @pl.loop(0, size // 32)
@@ -195,7 +193,11 @@
             normed = x_f * lax.rsqrt(jnp.mean(x_f * x_f, axis=-1, keepdims=True) + NORM_EPS)
             h_v[at, :] = (normed * gain).astype(BF16)
 
-        gather_h.start(chunk)
+        gather_h.send_first(turn // 2, turn % 2)
+        gather_h.first(chunk, 2).start()
+    for turn in (2, 3):
+        for kind in (0, 1):
+            gather_h.send_first(turn, kind)
     for copy in positions:
         copy.start()
     own_h = pltpu.make_async_copy(h_v, gather_h.block(near.me, 0, CHUNKS), own_sems.at[0])
@@ -223,13 +225,11 @@
 
     gather_h.middle()
     gather_h.late()
-    for chunk in range(CHUNKS):
-        gather_dy.start(chunk)
     for load in w_loads + [stage_in]:
         load.wait()
     stage_out.start()
     own_h.wait()
-    gather_h.end()
+    gather_h.end(gather_dy.start)
 
     def block_load(ref, block, slot):
         return pltpu.make_async_copy(ref.at[pl.ds(pl.multiple_of(block * rows, rows), rows), :], blk.at[slot], blk_sems.at[slot])
@@ -297,12 +297,8 @@
         def _():
             gather_dy.middle()
 
-        @pl.when(i == FWD_LATE)
-        def _():
-            gather_dy.late()
-
-    for chunk in range(CHUNKS):
-        gather_o.start(chunk)
+    gather_dy.late()
+    gather_o.start()
     own_o = pltpu.make_async_copy(ot_s, gather_o.block(near.me, 0, CHUNKS), own_sems.at[0])
     own_o.start()
 
@@ -400,8 +396,7 @@
     for r in (n_blocks - 2, n_blocks - 1):
         for store in dq_stores(r):
             store.wait()
-    for chunk in range(CHUNKS):
-        gather_next.start(chunk)
+    gather_next.start()
 
     @pl.loop(0, n_blocks)
     def _(c):
@@ -609,7 +604,7 @@
             tile[slot, r:r + half // PARTS, :] = dot(a_buf[r:r + half // PARTS, :], b_buf[slot])
         start_tile(step)
 
-        @pl.when(step == n_o - 3)
+        @pl.when(step == n_o - 4)
         def _():
             acc[...] = jnp.zeros_like(acc)
             copy_own(0)
@@ -619,8 +614,7 @@
         def _():
             a_load(ht_ref).start()
             gathers[0].late()
-            for c in range(CHUNKS):
-                gathers[1].start(c)
+            gathers[1].start()
             stage_out(0).wait()
             stage_in(1).start()
             result_part()
@@ -628,7 +622,7 @@
             start_b(step + 1)
             hidden_start(0)
 
-        @pl.when(step == n_oa - 3)
+        @pl.when(step == n_oa - 4)
         def _():
             copy_own(1)
             gathers[1].middle()
@@ -636,8 +630,7 @@
         @pl.when(step == n_oa - 2)
         def _():
             gathers[1].late()
-            for c in range(CHUNKS):
-                gathers[2].start(c)
+            gathers[2].start()
             stage_out(1).wait()
             stage_in(2).start()
 
@@ -651,9 +644,9 @@
             hidden_add(0)
             hidden_start(1)
 
-    hidden_add(1)
     copy_own(2)
     gathers[2].middle()
+    hidden_add(1)
     gathers[2].late()
     stage_out(2).wait()
     gathers[2].end_sib()

time: 616 us -> 604 us (0.981)
  Pallas kernels: 613 us -> 601 us
    pallas_call x1, Pallas kernels: 527 us -> 516 us  [step(): pl.pallas_call(functools.partial(step_kernel, heads, first_scratch, secon...]
where the time goes in v8:
time: 604 us; the launch traced here: 603 us
  Pallas kernels  601 us (100%)
    pallas_call x1, Pallas kernels, step(): pl.pallas_call(functools.partial(step_kernel, heads, first_scratch, secon...  516 us
    pallas_call x1, Pallas kernels, finish(): pl.pallas_call(finish_kernel, grid=(width // MROWS, n_j), in_specs=[pl.Bl...  85.2 us

profile of v8, /device:TPU:0, one launch (start us, length us, event | category | flops | bytes accessed | tf_op | source)
XLA Modules:
  0.0 603.1 jit_solution(7313988582645230512)
XLA Ops:
  0.6 1.3 reshape.26.gain_ref
  1.9 515.8 %step.1 = (bf16[4096,3072]{1,0:T(8,128)(2,1)}, bf16[4096,3072]{1,0:T(8,128)(2,1)}, bf16[3072,4096]{1,0:T(8,128)(2,1)}, bf16[3072,4096]{1,0:T(8,128)(2,1)}, bf16[...) custom-call(bf16[512,3072]{1,0:T(8,128)(2,1)} %x_ref.1, ...), custom_call_target="tpu_custom_call" | custom-call | flops 178778013696 | bytes 251658240 | tf_op jit(solution)/shard_map/step/pallas_call | solution.py:748
  517.7 85.2 %finish.1 = (f32[3072,1024]{1,0:T(8,128)}, f32[3072,1024]{1,0:T(8,128)}, f32[3072,3072]{1,0:T(8,128)}, f32[3072,3072]{1,0:T(8,128)}, bf16[512,3072]{1,0:T(8,128)...) custom-call(bf16[3072,4096]{1,0:T(8,128)(2,1)} %get-tuple-element.21.ht_ref, bf16[8,4096,256]{2,1,0:T(8,128)(2,1)} %bitcast.4, ...), custom_call_target="tpu_custom_call" | custom-call | flops 51539607552 | bytes 25165824 | tf_op jit(solution)/shard_map/finish/pallas_call | solution.py:854

commit v9 on v8

--- a/solution.py
+++ b/solution.py
@@ -224,15 +224,72 @@
         sin_s[b] = jnp.sin(angles) * sign
 
     gather_h.middle()
-    gather_h.late()
     for load in w_loads + [stage_in]:
         load.wait()
     stage_out.start()
     own_h.wait()
-    gather_h.end(gather_dy.start)
 
     def block_load(ref, block, slot):
         return pltpu.make_async_copy(ref.at[pl.ds(pl.multiple_of(block * rows, rows), rows), :], blk.at[slot], blk_sems.at[slot])
+
+    far = n_blocks * 3 // 4
+
+    def arrive(r, ref, gather, before_near=None, between=None):
+        slot = lax.rem(r, 2)
+
+        @pl.when(r == 1)
+        def _():
+            gather.end_sib()
+
+        @pl.when(r == 2)
+        def _():
+            if before_near:
+                before_near()
+            gather.end_near()
+
+        @pl.when(r == far)
+        def _():
+            gather.end_far(between)
+
+        @pl.when(functools.reduce(jnp.logical_or, [r == first for first in (0, 1, 2, far)]))
+        def _():
+            block_load(ref, near.across(r), slot).start()
+
+        block_load(ref, 0, slot).wait()
+
+        @pl.when(functools.reduce(jnp.logical_and, [r + 1 != first for first in (1, 2, far, n_blocks)]))
+        def _():
+            block_load(ref, near.across(r + 1), 1 - slot).start()
+
+    def ht_store(r):
+        at = pl.ds(pl.multiple_of(near.across(r) * rows, rows), rows)
+        return pltpu.make_async_copy(ht_v.at[lax.rem(r, 2)], ht_ref.at[:, at], ht_sems.at[lax.rem(r, 2)])
+
+    @pl.loop(0, n_blocks)
+    def _(r):
+        i = near.across(r)
+        slot = lax.rem(r, 2)
+        arrive(r, h_all, gather_h, gather_h.late, gather_dy.start)
+
+        @pl.when(r >= 2)
+        def _():
+            ht_store(r - 2).wait()
+
+        ht_v[slot] = blk[slot].T
+        ht_store(r).start()
+        prod = dot(blk[slot], w_v[...])
+        cos_t, sin_t = cos_s[i], sin_s[i]
+        for a in range(heads + 1):
+            val = prod[:, a * HEAD_DIM:(a + 1) * HEAD_DIM]
+            rot = (val * cos_t + pltpu.roll(val, HALF, 1) * sin_t).astype(BF16)
+            if a < heads:
+                q_s[i, :, cols[a]] = rot
+            else:
+                k_s[i] = rot
+                kt[i] = rot.T
+        v_i = prod[:, q_cols + HEAD_DIM:].astype(BF16)
+        v_s[i] = v_i
+        vt[i] = v_i.T
 
     def fwd_chunk(i, c, carry, diagonal):
         k_c, vt_c = k_s[c], vt[c]
@@ -249,40 +306,8 @@
             out.append((m_new, l_new))
         return tuple(out)
 
-    def ht_store(i):
-        at = pl.ds(pl.multiple_of(i * rows, rows), rows)
-        return pltpu.make_async_copy(ht_v.at[lax.rem(i, 2)], ht_ref.at[:, at], ht_sems.at[lax.rem(i, 2)])
-
-    block_load(h_all, 0, 0).start()
-
     @pl.loop(0, n_blocks)
     def _(i):
-        slot = lax.rem(i, 2)
-        block_load(h_all, i, slot).wait()
-
-        @pl.when(i + 1 < n_blocks)
-        def _():
-            block_load(h_all, i + 1, 1 - slot).start()
-
-        @pl.when(i >= 2)
-        def _():
-            ht_store(i - 2).wait()
-
-        ht_v[slot] = blk[slot].T
-        ht_store(i).start()
-        prod = dot(blk[slot], w_v[...])
-        cos_t, sin_t = cos_s[i], sin_s[i]
-        for a in range(heads + 1):
-            val = prod[:, a * HEAD_DIM:(a + 1) * HEAD_DIM]
-            rot = (val * cos_t + pltpu.roll(val, HALF, 1) * sin_t).astype(BF16)
-            if a < heads:
-                q_s[i, :, cols[a]] = rot
-            else:
-                k_s[i] = rot
-                kt[i] = rot.T
-        v_i = prod[:, q_cols + HEAD_DIM:].astype(BF16)
-        v_s[i] = v_i
-        vt[i] = v_i.T
         acc[...] = jnp.zeros_like(acc)
         start = tuple((jnp.full((1, rows), NEG_LARGE, F32), jnp.zeros((1, rows), F32)) for _ in range(heads))
         carry = lax.fori_loop(0, i, lambda c, carry: fwd_chunk(i, c, carry, False), start)
@@ -333,41 +358,18 @@
         def _():
             gather_o.middle()
 
-    for i in (n_blocks - 2, n_blocks - 1):
-        ht_store(i).wait()
+    for r in (n_blocks - 2, n_blocks - 1):
+        ht_store(jnp.int32(r)).wait()
     dk_acc[...] = jnp.zeros_like(dk_acc)
     dv_acc[...] = jnp.zeros_like(dv_acc)
     stage_out.wait()
-    block_load(dy_all, near.me, 0).start()
 
     def bwd_block(r, done):
         i = near.across(r)
         slot = lax.rem(r, 2)
         at = pl.ds(pl.multiple_of(i * rows, rows), rows)
 
-        @pl.when(r == 1)
-        def _():
-            gather_dy.end_sib()
-
-        @pl.when(r == 2)
-        def _():
-            gather_dy.end_near()
-
-        @pl.when(r == n_blocks * 3 // 4)
-        def _():
-            gather_dy.end_far()
-
-        waits = [r == first for first in (1, 2, n_blocks * 3 // 4)]
-        @pl.when(functools.reduce(jnp.logical_or, waits))
-        def _():
-            block_load(dy_all, i, slot).start()
-
-        block_load(dy_all, 0, slot).wait()
-
-        @pl.when(functools.reduce(jnp.logical_and, [r + 1 != first for first in (1, 2, n_blocks * 3 // 4, n_blocks)]))
-        def _():
-            block_load(dy_all, near.across(r + 1), 1 - slot).start()
-
+        arrive(r, dy_all, gather_dy)
         do_s[i] = dot(blk[slot], wo_v[...], COLS_COLS).astype(BF16)
         acc[...] = jnp.zeros_like(acc)
         delta = [jnp.sum(ot_s[cols[a], at].astype(F32) * do_s[i, :, cols[a]].T.astype(F32), axis=0, keepdims=True) for a in range(heads)]

time: 604 us -> 602 us (level)
  no operation moved by 1% of the time
where the time goes in v9:
time: 602 us; the launch traced here: 600 us
  Pallas kernels  598 us (99%)
    pallas_call x1, Pallas kernels, step(): pl.pallas_call(functools.partial(step_kernel, heads, first_scratch, secon...  513 us
    pallas_call x1, Pallas kernels, finish(): pl.pallas_call(finish_kernel, grid=(width // MROWS, n_j), in_specs=[pl.Bl...  85.2 us

profile of v9, /device:TPU:0, one launch (start us, length us, event | category | flops | bytes accessed | tf_op | source)
XLA Modules:
  0.0 600.5 jit_solution(1687276363091414104)
XLA Ops:
  0.6 1.3 reshape.26.gain_ref
  1.9 513.1 %step.1 = (bf16[4096,3072]{1,0:T(8,128)(2,1)}, bf16[4096,3072]{1,0:T(8,128)(2,1)}, bf16[3072,4096]{1,0:T(8,128)(2,1)}, bf16[3072,4096]{1,0:T(8,128)(2,1)}, bf16[...) custom-call(bf16[512,3072]{1,0:T(8,128)(2,1)} %x_ref.1, ...), custom_call_target="tpu_custom_call" | custom-call | flops 178778013696 | bytes 251658240 | tf_op jit(solution)/shard_map/step/pallas_call | solution.py:750
  515.1 85.2 %finish.1 = (f32[3072,1024]{1,0:T(8,128)}, f32[3072,1024]{1,0:T(8,128)}, f32[3072,3072]{1,0:T(8,128)}, f32[3072,3072]{1,0:T(8,128)}, bf16[512,3072]{1,0:T(8,128)...) custom-call(bf16[3072,4096]{1,0:T(8,128)(2,1)} %get-tuple-element.21.ht_ref, bf16[8,4096,256]{2,1,0:T(8,128)(2,1)} %bitcast.4, ...), custom_call_target="tpu_custom_call" | custom-call | flops 51539607552 | bytes 25165824 | tf_op jit(solution)/shard_map/finish/pallas_call | solution.py:856

commit v10 on v9

--- a/solution.py
+++ b/solution.py
@@ -19,7 +19,7 @@
 FWD_MIDDLE, BWD_MIDDLE = 5, 27
 MROWS = 768
 RING = 3
-DEPTH = 3
+DEPTH = 4
 COPY_ROWS = 24
 PARTS = 3
 ROW_STEPS = 8
@@ -643,11 +643,11 @@
             dy_load.start()
             gathers[1].end()
             start_b(step + 1)
-            hidden_add(0)
-            hidden_start(1)
-
+
+    hidden_add(0)
     copy_own(2)
     gathers[2].middle()
+    hidden_start(1)
     hidden_add(1)
     gathers[2].late()
     stage_out(2).wait()
@@ -804,11 +804,17 @@
             copy_in(wo_in, g, n).wait()
         start(copy_out, wo_ref, wq_ref, g)
 
-    @pl.when(step >= DEPTH)
+    @pl.when(step == 0)
     def _():
-        free(step - DEPTH)
-
-    start(copy_in, wo_in, wq_in, step)
+        start(copy_in, wo_in, wq_in, step)
+
+    @pl.when(step >= DEPTH - 1)
+    def _():
+        free(step + 1 - DEPTH)
+
+    @pl.when(step < last)
+    def _():
+        start(copy_in, wo_in, wq_in, step + 1)
 
     @pl.when(step >= 1)
     def _():
@@ -831,7 +837,7 @@
     @pl.when(step == last)
     def _():
         pass_on(last)
-        for back in range(DEPTH):
+        for back in range(DEPTH - 1):
             free(last - back)
 
     @pl.when(step < ROW_STEPS)

time: 602 us -> 594 us (0.987)
  Pallas kernels: 598 us -> 590 us
    pallas_call x1, Pallas kernels: 85.2 us -> 77.1 us  [finish(): pl.pallas_call(finish_kernel, grid=(width // MROWS, n_j), in_specs=[pl.Bl...]
where the time goes in v10:
time: 594 us; the launch traced here: 592 us
  Pallas kernels  590 us (99%)
    pallas_call x1, Pallas kernels, step(): pl.pallas_call(functools.partial(step_kernel, heads, first_scratch, secon...  513 us
    pallas_call x1, Pallas kernels, finish(): pl.pallas_call(finish_kernel, grid=(width // MROWS, n_j), in_specs=[pl.Bl...  77.1 us

profile of v10, /device:TPU:0, one launch (start us, length us, event | category | flops | bytes accessed | tf_op | source)
XLA Modules:
  0.0 592.3 jit_solution(8740018311237913054)
XLA Ops:
  0.6 1.3 reshape.26.gain_ref
  1.9 513.1 %step.1 = (bf16[4096,3072]{1,0:T(8,128)(2,1)}, bf16[4096,3072]{1,0:T(8,128)(2,1)}, bf16[3072,4096]{1,0:T(8,128)(2,1)}, bf16[3072,4096]{1,0:T(8,128)(2,1)}, bf16[...) custom-call(bf16[512,3072]{1,0:T(8,128)(2,1)} %x_ref.1, ...), custom_call_target="tpu_custom_call" | custom-call | flops 178778013696 | bytes 251658240 | tf_op jit(solution)/shard_map/step/pallas_call | solution.py:750
  515.1 77.1 %finish.1 = (f32[3072,1024]{1,0:T(8,128)}, f32[3072,1024]{1,0:T(8,128)}, f32[3072,3072]{1,0:T(8,128)}, f32[3072,3072]{1,0:T(8,128)}, bf16[512,3072]{1,0:T(8,128)...) custom-call(bf16[3072,4096]{1,0:T(8,128)(2,1)} %get-tuple-element.21.ht_ref, bf16[8,4096,256]{2,1,0:T(8,128)(2,1)} %bitcast.4, ...), custom_call_target="tpu_custom_call" | custom-call | flops 51539607552 | bytes 25165824 | tf_op jit(solution)/shard_map/finish/pallas_call | solution.py:862

commit v11 on v10

--- a/solution.py
+++ b/solution.py
@@ -15,7 +15,7 @@
 NEG_LARGE = -1e30
 LOG2E = 1.4426950408889634
 BLK = 512
-CHUNKS = 4
+CHUNKS = 2
 FWD_MIDDLE, BWD_MIDDLE = 5, 27
 MROWS = 768
 RING = 3
@@ -69,7 +69,9 @@
 
 
 class Gather:
-    COPIES = 22
+    COPIES = 5 * CHUNKS + 2
+    HALF_CHUNKS = CHUNKS // 2
+    ORDER = [chunk + half * (CHUNKS // 2) for chunk in range(CHUNKS // 2) for half in range(2)]
 
     def __init__(self, near, own, dst, rows, sems):
         self.near, self.own, self.dst, self.rows, self.sems = near, own, dst, rows, sems
@@ -83,17 +85,17 @@
         return send(self.own(chunk), self.block(self.near.me, chunk), self.sems, kind * CHUNKS + chunk, peer)
 
     def onward(self, chunk):
-        over_y = chunk < CHUNKS // 2
+        over_y = chunk < self.HALF_CHUNKS
         rows = self.block(self.near.xn if over_y else self.near.yn, chunk)
-        return send(rows, rows, self.sems, 12 + chunk, self.near.yn if over_y else self.near.xn)
+        return send(rows, rows, self.sems, 3 * CHUNKS + chunk, self.near.yn if over_y else self.near.xn)
 
     def share(self, kind):
         rows = self.block((self.near.xn, self.near.yn)[kind], 0, CHUNKS)
-        return send(rows, rows, self.sems, 16 + kind, self.near.sib)
+        return send(rows, rows, self.sems, 4 * CHUNKS + kind, self.near.sib)
 
     def share_diag(self, chunk):
         rows = self.block(self.near.diag, chunk)
-        return send(rows, rows, self.sems, 18 + chunk, self.near.sib)
+        return send(rows, rows, self.sems, 4 * CHUNKS + 2 + chunk, self.near.sib)
 
     def start(self):
         for chunk in range(CHUNKS):
@@ -102,18 +104,18 @@
             self.first(chunk, 2).start()
 
     def send_first(self, turn, kind):
-        self.first(turn if kind == 0 else (turn + CHUNKS // 2) % CHUNKS, kind).start()
+        self.first(turn if kind == 0 else (turn + self.HALF_CHUNKS) % CHUNKS, kind).start()
 
     def middle(self):
-        for chunk in (0, 2, 1, 3):
-            self.first(chunk, 0 if chunk < CHUNKS // 2 else 1).wait_recv()
+        for chunk in self.ORDER:
+            self.first(chunk, 0 if chunk < self.HALF_CHUNKS else 1).wait_recv()
             self.onward(chunk).start()
 
     def late(self):
-        for chunk in (2, 3):
+        for chunk in range(self.HALF_CHUNKS, CHUNKS):
             self.first(chunk, 0).wait_recv()
         self.share(0).start()
-        for chunk in (0, 1):
+        for chunk in range(self.HALF_CHUNKS):
             self.first(chunk, 1).wait_recv()
         self.share(1).start()
 
@@ -125,12 +127,10 @@
         for kind in range(2):
             self.share(kind).wait_recv()
 
-    def end_far(self, between=None):
-        for chunk in (0, 2, 1, 3):
+    def end_far(self):
+        for chunk in self.ORDER:
             self.onward(chunk).wait_recv()
             self.share_diag(chunk).start()
-            if chunk == 2 and between:
-                between()
         for chunk in range(CHUNKS):
             for kind in range(3):
                 self.first(chunk, kind).wait_send()
@@ -140,10 +140,10 @@
         for chunk in range(CHUNKS):
             self.share_diag(chunk).wait()
 
-    def end(self, between=None):
+    def end(self):
         self.end_sib()
         self.end_near()
-        self.end_far(between)
+        self.end_far()
 
 
 SEMS = pltpu.SemaphoreType.DMA((2, Gather.COPIES))
@@ -183,7 +183,7 @@
     pos_all[near.me] = jnp.broadcast_to(pos_ref[...], pos_all.shape[1:])
     positions = [send(pos_ref, pos_all.at[near.me, pl.ds(0, 1), :], pos_sems, r, peer) for r, peer in enumerate(others)]
     gain = gain_ref[...].astype(F32)
-    for turn, chunk in enumerate((0, 2, 1, 3)):
+    for turn, chunk in enumerate(Gather.ORDER):
         loads[chunk].wait()
 
         @pl.loop(0, size // 32)
@@ -195,7 +195,7 @@
 
         gather_h.send_first(turn // 2, turn % 2)
         gather_h.first(chunk, 2).start()
-    for turn in (2, 3):
+    for turn in range(Gather.HALF_CHUNKS, CHUNKS):
         for kind in (0, 1):
             gather_h.send_first(turn, kind)
     for copy in positions:
@@ -234,7 +234,7 @@
 
     far = n_blocks * 3 // 4
 
-    def arrive(r, ref, gather, before_near=None, between=None):
+    def arrive(r, ref, gather, before_near=None, before_far=None):
         slot = lax.rem(r, 2)
 
         @pl.when(r == 1)
@@ -249,7 +249,9 @@
 
         @pl.when(r == far)
         def _():
-            gather.end_far(between)
+            if before_far:
+                before_far()
+            gather.end_far()
 
         @pl.when(functools.reduce(jnp.logical_or, [r == first for first in (0, 1, 2, far)]))
         def _():

time: 594 us -> 595 us (level)
  no operation moved by 1% of the time
where the time goes in v11:
time: 595 us; the launch traced here: 594 us
  Pallas kernels  592 us (99%)
    pallas_call x1, Pallas kernels, step(): pl.pallas_call(functools.partial(step_kernel, heads, first_scratch, secon...  515 us
    pallas_call x1, Pallas kernels, finish(): pl.pallas_call(finish_kernel, grid=(width // MROWS, n_j), in_specs=[pl.Bl...  77.1 us

profile of v11, /device:TPU:0, one launch (start us, length us, event | category | flops | bytes accessed | tf_op | source)
XLA Modules:
  0.0 594.1 jit_solution(15102090608275700024)
XLA Ops:
  0.6 1.3 reshape.26.gain_ref
  1.9 514.9 %step.1 = (bf16[4096,3072]{1,0:T(8,128)(2,1)}, bf16[4096,3072]{1,0:T(8,128)(2,1)}, bf16[3072,4096]{1,0:T(8,128)(2,1)}, bf16[3072,4096]{1,0:T(8,128)(2,1)}, bf16[...) custom-call(bf16[512,3072]{1,0:T(8,128)(2,1)} %x_ref.1, ...), custom_call_target="tpu_custom_call" | custom-call | flops 178778013696 | bytes 251658240 | tf_op jit(solution)/shard_map/step/pallas_call | solution.py:752
  516.9 77.1 %finish.1 = (f32[3072,1024]{1,0:T(8,128)}, f32[3072,1024]{1,0:T(8,128)}, f32[3072,3072]{1,0:T(8,128)}, f32[3072,3072]{1,0:T(8,128)}, bf16[512,3072]{1,0:T(8,128)...) custom-call(bf16[3072,4096]{1,0:T(8,128)(2,1)} %get-tuple-element.21.ht_ref, bf16[8,4096,256]{2,1,0:T(8,128)(2,1)} %bitcast.4, ...), custom_call_target="tpu_custom_call" | custom-call | flops 51539607552 | bytes 25165824 | tf_op jit(solution)/shard_map/finish/pallas_call | solution.py:864

commit v12 on v11

--- a/solution.py
+++ b/solution.py
@@ -15,7 +15,7 @@
 NEG_LARGE = -1e30
 LOG2E = 1.4426950408889634
 BLK = 512
-CHUNKS = 2
+CHUNKS = 8
 FWD_MIDDLE, BWD_MIDDLE = 5, 27
 MROWS = 768
 RING = 3
@@ -179,10 +179,9 @@
     for load in loads:
         load.start()
     others = near.others()
-    near.meet(others)
     pos_all[near.me] = jnp.broadcast_to(pos_ref[...], pos_all.shape[1:])
     positions = [send(pos_ref, pos_all.at[near.me, pl.ds(0, 1), :], pos_sems, r, peer) for r, peer in enumerate(others)]
-    gain = gain_ref[...].astype(F32)
+    gain = gain_ref[...].astype(F32).reshape(1, width)
     for turn, chunk in enumerate(Gather.ORDER):
         loads[chunk].wait()
 
@@ -193,6 +192,8 @@
             normed = x_f * lax.rsqrt(jnp.mean(x_f * x_f, axis=-1, keepdims=True) + NORM_EPS)
             h_v[at, :] = (normed * gain).astype(BF16)
 
+        if turn == 0:
+            near.meet(others)
         gather_h.send_first(turn // 2, turn % 2)
         gather_h.first(chunk, 2).start()
     for turn in range(Gather.HALF_CHUNKS, CHUNKS):
@@ -664,7 +665,7 @@
     hidden_start(2, near_count)
     hidden_add(2, near_count)
 
-    gain = gain_ref[...].astype(F32)
+    gain = gain_ref[...].astype(F32).reshape(1, width)
     gg_v[...] = jnp.zeros_like(gg_v)
     x_load.wait()
     dy_load.wait()
@@ -886,7 +887,7 @@
         n_heads = w_q.shape[1] // HEAD_DIM
         heads = n_heads // sp_size
         _, _, _, ht, _, _, _, w_o_grad, w_q_grad, kv_all, _, _, result, grad_x, grad_gain = step(
-            x, gain.reshape(1, -1), positions, grad_out, w_q, w_k, w_v, w_o, sp_size, heads)
+            x, gain, positions, grad_out, w_q, w_k, w_v, w_o, sp_size, heads)
         grad_wk, grad_wv, grad_wq, grad_wo, grad_x, result, grad_gain = finish(
             ht, kv_all.reshape(sp_size, -1, 2 * HEAD_DIM), w_o_grad, w_q_grad, grad_x, result, grad_gain)
         return result, grad_x, grad_wq, grad_wk, grad_wv, grad_wo, grad_gain.reshape(-1)

time: 595 us -> 595 us (level)
  no operation moved by 1% of the time
where the time goes in v12:
time: 595 us; the launch traced here: 593 us
  Pallas kernels  593 us (100%)
    pallas_call x1, Pallas kernels, step(): pl.pallas_call(functools.partial(step_kernel, heads, first_scratch, secon...  516 us
    pallas_call x1, Pallas kernels, finish(): pl.pallas_call(finish_kernel, grid=(width // MROWS, n_j), in_specs=[pl.Bl...  77.1 us

profile of v12, /device:TPU:0, one launch (start us, length us, event | category | flops | bytes accessed | tf_op | source)
XLA Modules:
  0.0 593.5 jit_solution(18344757737420172817)
XLA Ops:
  0.6 515.6 %step.1 = (bf16[4096,3072]{1,0:T(8,128)(2,1)}, bf16[4096,3072]{1,0:T(8,128)(2,1)}, bf16[3072,4096]{1,0:T(8,128)(2,1)}, bf16[3072,4096]{1,0:T(8,128)(2,1)}, bf16[...) custom-call(bf16[512,3072]{1,0:T(8,128)(2,1)} %x_ref.1, ...), custom_call_target="tpu_custom_call" | custom-call | flops 178778013696 | bytes 251658240 | tf_op jit(solution)/shard_map/step/pallas_call | solution.py:753
  516.2 77.1 %finish.1 = (f32[3072,1024]{1,0:T(8,128)}, f32[3072,1024]{1,0:T(8,128)}, f32[3072,3072]{1,0:T(8,128)}, f32[3072,3072]{1,0:T(8,128)}, bf16[512,3072]{1,0:T(8,128)...) custom-call(bf16[3072,4096]{1,0:T(8,128)(2,1)} %get-tuple-element.21.ht_ref, bf16[8,4096,256]{2,1,0:T(8,128)(2,1)} %bitcast.4, ...), custom_call_target="tpu_custom_call" | custom-call | flops 51539607552 | bytes 25165824 | tf_op jit(solution)/shard_map/finish/pallas_call | solution.py:865

commit v13 on v12

--- a/solution.py
+++ b/solution.py
@@ -15,7 +15,7 @@
 NEG_LARGE = -1e30
 LOG2E = 1.4426950408889634
 BLK = 512
-CHUNKS = 8
+CHUNKS = 4
 FWD_MIDDLE, BWD_MIDDLE = 5, 27
 MROWS = 768
 RING = 3
@@ -179,6 +179,7 @@
     for load in loads:
         load.start()
     others = near.others()
+    near.meet(others)
     pos_all[near.me] = jnp.broadcast_to(pos_ref[...], pos_all.shape[1:])
     positions = [send(pos_ref, pos_all.at[near.me, pl.ds(0, 1), :], pos_sems, r, peer) for r, peer in enumerate(others)]
     gain = gain_ref[...].astype(F32).reshape(1, width)
@@ -192,8 +193,6 @@
             normed = x_f * lax.rsqrt(jnp.mean(x_f * x_f, axis=-1, keepdims=True) + NORM_EPS)
             h_v[at, :] = (normed * gain).astype(BF16)
 
-        if turn == 0:
-            near.meet(others)
         gather_h.send_first(turn // 2, turn % 2)
         gather_h.first(chunk, 2).start()
     for turn in range(Gather.HALF_CHUNKS, CHUNKS):
@@ -670,23 +669,30 @@
     x_load.wait()
     dy_load.wait()
 
-    @pl.loop(0, rows // 32)
-    def _(r):
+    def normed_rows(r):
         at = pl.ds(pl.multiple_of(r * 32, 32), 32)
         x_f = x_v[at, :].astype(F32)
         inv_rms = lax.rsqrt(jnp.mean(x_f * x_f, axis=-1, keepdims=True) + NORM_EPS)
-        normed = x_f * inv_rms
-        d_hid = acc[at, :]
-        both = d_hid * normed
-        gg_v[...] += jnp.sum(both.reshape(4, 8, width), axis=0)
-        mean = jnp.mean(both * gain, axis=-1, keepdims=True)
-        o_v[at, :] = (o_v[at, :].astype(F32) + inv_rms * (d_hid * gain - normed * mean)).astype(BF16)
+        return at, inv_rms, x_f * inv_rms
+
+    @pl.loop(0, rows // 32)
+    def _(r):
+        at, _, normed = normed_rows(r)
+        gg_v[...] += jnp.sum((acc[at, :] * normed).reshape(4, 8, width), axis=0)
 
     gg_row[...] = jnp.sum(gg_v[...], axis=0, keepdims=True)
     gg_all[near.me] = gg_row[...]
     parts = [send(gg_row, gg_all.at[near.me], gg_sems, r, peer) for r, peer in enumerate(near.others())]
     for copy in parts:
         copy.start()
+
+    @pl.loop(0, rows // 32)
+    def _(r):
+        at, inv_rms, normed = normed_rows(r)
+        d_normed = acc[at, :] * gain
+        mean = jnp.mean(d_normed * normed, axis=-1, keepdims=True)
+        o_v[at, :] = (o_v[at, :].astype(F32) + inv_rms * (d_normed - normed * mean)).astype(BF16)
+
     gx_store.start()
 
     @pl.loop(0, n_all)

time: 595 us -> 593 us (level)
  no operation moved by 1% of the time
where the time goes in v13:
time: 593 us; the launch traced here: 592 us
  Pallas kernels  591 us (100%)
    pallas_call x1, Pallas kernels, step(): pl.pallas_call(functools.partial(step_kernel, heads, first_scratch, secon...  514 us
    pallas_call x1, Pallas kernels, finish(): pl.pallas_call(finish_kernel, grid=(width // MROWS, n_j), in_specs=[pl.Bl...  77.1 us

profile of v13, /device:TPU:0, one launch (start us, length us, event | category | flops | bytes accessed | tf_op | source)
XLA Modules:
  0.0 592.1 jit_solution(8926554849713537911)
XLA Ops:
  0.6 514.2 %step.1 = (bf16[4096,3072]{1,0:T(8,128)(2,1)}, bf16[4096,3072]{1,0:T(8,128)(2,1)}, bf16[3072,4096]{1,0:T(8,128)(2,1)}, bf16[3072,4096]{1,0:T(8,128)(2,1)}, bf16[...) custom-call(bf16[512,3072]{1,0:T(8,128)(2,1)} %x_ref.1, ...), custom_call_target="tpu_custom_call" | custom-call | flops 178778013696 | bytes 251658240 | tf_op jit(solution)/shard_map/step/pallas_call | solution.py:759
  514.9 77.1 %finish.1 = (f32[3072,1024]{1,0:T(8,128)}, f32[3072,1024]{1,0:T(8,128)}, f32[3072,3072]{1,0:T(8,128)}, f32[3072,3072]{1,0:T(8,128)}, bf16[512,3072]{1,0:T(8,128)...) custom-call(bf16[3072,4096]{1,0:T(8,128)(2,1)} %get-tuple-element.21.ht_ref, bf16[8,4096,256]{2,1,0:T(8,128)(2,1)} %bitcast.4, ...), custom_call_target="tpu_custom_call" | custom-call | flops 51539607552 | bytes 25165824 | tf_op jit(solution)/shard_map/finish/pallas_call | solution.py:871

commit v14 on v13

--- a/solution.py
+++ b/solution.py
@@ -19,10 +19,10 @@
 FWD_MIDDLE, BWD_MIDDLE = 5, 27
 MROWS = 768
 RING = 3
-DEPTH = 4
+DEPTH = 5
 COPY_ROWS = 24
 PARTS = 3
-ROW_STEPS = 8
+ROW_STEPS = 16
 F32 = jnp.float32
 BF16 = jnp.bfloat16
 ROWS_ROWS = (((0,), (0,)), ((), ()))
@@ -816,14 +816,15 @@
     @pl.when(step == 0)
     def _():
         start(copy_in, wo_in, wq_in, step)
-
-    @pl.when(step >= DEPTH - 1)
+        start(copy_in, wo_in, wq_in, step + 1)
+
+    @pl.when(step >= DEPTH - 2)
     def _():
-        free(step + 1 - DEPTH)
-
-    @pl.when(step < last)
+        free(step + 2 - DEPTH)
+
+    @pl.when(step < last - 1)
     def _():
-        start(copy_in, wo_in, wq_in, step + 1)
+        start(copy_in, wo_in, wq_in, step + 2)
 
     @pl.when(step >= 1)
     def _():
@@ -846,7 +847,7 @@
     @pl.when(step == last)
     def _():
         pass_on(last)
-        for back in range(DEPTH - 1):
+        for back in range(DEPTH - 2):
             free(last - back)
 
     @pl.when(step < ROW_STEPS)

time: 593 us -> 594 us (level)
  no operation moved by 1% of the time
where the time goes in v14:
time: 594 us; the launch traced here: 593 us
  Pallas kernels  592 us (100%)
    pallas_call x1, Pallas kernels, step(): pl.pallas_call(functools.partial(step_kernel, heads, first_scratch, secon...  514 us
    pallas_call x1, Pallas kernels, finish(): pl.pallas_call(finish_kernel, grid=(width // MROWS, n_j), in_specs=[pl.Bl...  78 us

profile of v14, /device:TPU:0, one launch (start us, length us, event | category | flops | bytes accessed | tf_op | source)
XLA Modules:
  0.0 593.0 jit_solution(15198656973112536546)
XLA Ops:
  0.6 514.2 %step.1 = (bf16[4096,3072]{1,0:T(8,128)(2,1)}, bf16[4096,3072]{1,0:T(8,128)(2,1)}, bf16[3072,4096]{1,0:T(8,128)(2,1)}, bf16[3072,4096]{1,0:T(8,128)(2,1)}, bf16[...) custom-call(bf16[512,3072]{1,0:T(8,128)(2,1)} %x_ref.1, ...), custom_call_target="tpu_custom_call" | custom-call | flops 178778013696 | bytes 251658240 | tf_op jit(solution)/shard_map/step/pallas_call | solution.py:759
  514.9 78.0 %finish.1 = (f32[3072,1024]{1,0:T(8,128)}, f32[3072,1024]{1,0:T(8,128)}, f32[3072,3072]{1,0:T(8,128)}, f32[3072,3072]{1,0:T(8,128)}, bf16[512,3072]{1,0:T(8,128)...) custom-call(bf16[3072,4096]{1,0:T(8,128)(2,1)} %get-tuple-element.21.ht_ref, bf16[8,4096,256]{2,1,0:T(8,128)(2,1)} %bitcast.4, ...), custom_call_target="tpu_custom_call" | custom-call | flops 51539607552 | bytes 25165824 | tf_op jit(solution)/shard_map/finish/pallas_call | solution.py:872
